TPU v7x, 8 devices: a whole 2x2x1 slice. The times are simulated.
8 devices in a mesh: heads: 1 (over z), cp_outer: 2 (over y), cp: 4 (over x, core).
Axes of the slice: x: 2, y: 2, z: 1, core: 2. Of those that a mesh axis runs over, the one named last changes fastest.
Arguments:
- q_segs: bfloat16 [32, 256, 24, 128], P(None, ('cp_outer', 'cp'), 'heads')
- k_prefix: bfloat16 [8448, 8, 128], P(('cp_outer', 'cp'), 'heads')
- v_prefix: bfloat16 [8448, 8, 128], P(('cp_outer', 'cp'), 'heads')
- o_segs: bfloat16 [32, 256, 24, 128], P(None, ('cp_outer', 'cp'), 'heads')
- do_segs: bfloat16 [32, 256, 24, 128], P(None, ('cp_outer', 'cp'), 'heads')
- lse_segs: float32 [32, 256, 24], P(None, ('cp_outer', 'cp'), 'heads')
Outputs:
- output 1: bfloat16 [32, 256, 24, 128], P(None, ('cp_outer', 'cp'), 'heads')
- output 2: float32 [8448, 8, 128], P(('cp_outer', 'cp'), 'heads')
- output 3: float32 [8448, 8, 128], P(('cp_outer', 'cp'), 'heads')
All inputs are finite; a program needn't handle non-finite values.
Results may differ from a plain program's by a relative error of at most 0.001.
Values are sent between devices in bfloat16 or wider.
A program may use at most 1 GiB of HBM per device.

v0:
```python
import jax
import jax.numpy as jnp
from jax import lax
from jax.sharding import PartitionSpec as P

SEQ_AXES = ("cp_outer", "cp")


def heads_first(stat_rows, kv_heads):
    n_rows, q_heads = stat_rows.shape
    return jnp.transpose(stat_rows.reshape(n_rows, kv_heads, q_heads // kv_heads), (1, 2, 0))[..., None]


def block_grads(q_four, do_four, lse_four, delta_four, k_block, v_block, visible, qk_scale):
    scores = jnp.einsum("qhgd,khd->hgqk", q_four, k_block, preferred_element_type=jnp.float32) * qk_scale
    p_block = jnp.exp(jnp.where(visible, scores - lse_four, -jnp.inf))
    dp_block = jnp.einsum("qhgd,khd->hgqk", do_four, v_block, preferred_element_type=jnp.float32)
    ds_low = (p_block * (dp_block - delta_four)).astype(jnp.bfloat16)
    p_low = p_block.astype(jnp.bfloat16)
    dq_part = jnp.einsum("hgqk,khd->qhgd", ds_low, k_block, preferred_element_type=jnp.float32) * qk_scale
    dk_part = jnp.einsum("hgqk,qhgd->khd", ds_low, q_four, preferred_element_type=jnp.float32) * qk_scale
    dv_part = jnp.einsum("hgqk,qhgd->khd", p_low, do_four, preferred_element_type=jnp.float32)
    return dq_part, dk_part, dv_part


def solution(mesh):
    outer_size = mesh.shape["cp_outer"]
    inner_size = mesh.shape["cp"]
    n_blocks = outer_size * inner_size
    seq_spec = P(None, SEQ_AXES, "heads", None)
    stat_spec = P(None, SEQ_AXES, "heads")
    kv_spec = P(SEQ_AXES, "heads", None)

    def gather_all(local_part):
        inner_part = lax.all_gather(local_part, "cp", axis=0)
        outer_part = lax.all_gather(inner_part, "cp_outer", axis=0)
        return outer_part.reshape((n_blocks,) + local_part.shape)

    def scatter_sum(block_stack):
        grouped = block_stack.reshape((outer_size, inner_size) + block_stack.shape[1:])
        outer_part = lax.psum_scatter(grouped, "cp_outer", scatter_dimension=0)
        return lax.psum_scatter(outer_part, "cp", scatter_dimension=0)

    def local_grads(q_loc, k_loc, v_loc, o_loc, do_loc, lse_loc):
        n_segs, q_rows, q_heads, head_dim = q_loc.shape
        k_rows = k_loc.shape[0]
        kv_heads = k_loc.shape[1]
        group_size = q_heads // kv_heads
        qk_scale = head_dim ** -0.5
        seg_len = q_rows * n_blocks
        prefix0 = k_rows * n_blocks - n_segs * seg_len
        my_block = lax.axis_index("cp_outer") * inner_size + lax.axis_index("cp")
        k_pos = my_block * k_rows + jnp.arange(k_rows)
        delta_loc = jnp.einsum("sqhd,sqhd->sqh", do_loc, o_loc, preferred_element_type=jnp.float32)
        dk_acc = jnp.zeros(k_loc.shape, jnp.float32)
        dv_acc = jnp.zeros(v_loc.shape, jnp.float32)
        dq_segs = [None] * n_segs
        for seg_idx in reversed(range(n_segs)):
            q_all = gather_all(q_loc[seg_idx])
            do_all = gather_all(do_loc[seg_idx])
            lse_all = gather_all(lse_loc[seg_idx])
            delta_all = gather_all(delta_loc[seg_idx])
            seg_start = prefix0 + seg_idx * seg_len

            def source_step(grad_pair, source_in):
                dk_run, dv_run = grad_pair
                q_blk, do_blk, lse_blk, delta_blk, src_block = source_in
                q_pos = seg_start + src_block * q_rows + jnp.arange(q_rows)
                visible = q_pos[:, None] >= k_pos[None, :]
                dq_part, dk_part, dv_part = block_grads(
                    q_blk.reshape(q_rows, kv_heads, group_size, head_dim),
                    do_blk.reshape(q_rows, kv_heads, group_size, head_dim),
                    heads_first(lse_blk, kv_heads), heads_first(delta_blk, kv_heads),
                    k_loc, v_loc, visible, qk_scale)
                return (dk_run + dk_part, dv_run + dv_part), dq_part.reshape(q_rows, q_heads, head_dim)

            (dk_acc, dv_acc), dq_parts = lax.scan(
                source_step, (dk_acc, dv_acc),
                (q_all, do_all, lse_all, delta_all, jnp.arange(n_blocks)))
            dq_segs[seg_idx] = scatter_sum(dq_parts).astype(jnp.bfloat16)
        return jnp.stack(dq_segs), dk_acc, dv_acc

    return jax.shard_map(local_grads, mesh=mesh,
                         in_specs=(seq_spec, kv_spec, kv_spec, seq_spec, seq_spec, stat_spec),
                         out_specs=(seq_spec, kv_spec, kv_spec), check_vma=False)
```

profile of v0, /device:TPU:1, one launch (start us, length us, event | category | flops | bytes accessed | tf_op | source)
XLA Modules:
  0.0 9490.8 jit_solution(10835157741263319336)
XLA Ops:
  1653.3 182.4 %while.511 = (s32[]{:T(128)}, f32[1056,8,128]{2,0,1:T(8,128)}, f32[1056,8,128]{2,0,1:T(8,128)}, f32[8,32,24,128]{3,2,1,0:T(8,128)}, bf16[8,32,24,128]{3,2,1,0:T(...) while((s32[]{:T(128)}, f32[1056,8,128]{2,0,1:T(8,128)}, ...), condition=%wide.region_1.2_spmd.clone, body=%wide.region_0.1_spmd.clone.sunk | while | flops 1049307200 | bytes 61498636 | solution.py:77
  1837.6 169.6 %while.480 = (s32[]{:T(128)}, f32[1056,8,128]{2,0,1:T(8,128)}, f32[1056,8,128]{2,0,1:T(8,128)}, f32[8,32,24,128]{3,2,1,0:T(8,128)}, bf16[8,32,24,128]{3,2,1,0:T(...) while((s32[]{:T(128)}, f32[1056,8,128]{2,0,1:T(8,128)}, ...), condition=%wide.region_3.4_spmd.clone, body=%wide.region_2.3_spmd.clone.sunk | while | flops 1047144512 | bytes 55010524 | solution.py:77
  2009.1 169.8 %while.481 = (s32[]{:T(128)}, f32[1056,8,128]{2,0,1:T(8,128)}, f32[1056,8,128]{2,0,1:T(8,128)}, f32[8,32,24,128]{3,2,1,0:T(8,128)}, bf16[8,32,24,128]{3,2,1,0:T(...) while((s32[]{:T(128)}, f32[1056,8,128]{2,0,1:T(8,128)}, ...), condition=%wide.region_5.6_spmd.clone, body=%wide.region_4.5_spmd.clone.sunk | while | flops 1047144512 | bytes 55010524 | solution.py:77
  2180.9 175.3 %while.482 = (s32[]{:T(128)}, f32[1056,8,128]{2,0,1:T(8,128)}, f32[1056,8,128]{2,0,1:T(8,128)}, f32[8,32,24,128]{3,2,1,0:T(8,128)}, bf16[8,32,24,128]{3,2,1,0:T(...) while((s32[]{:T(128)}, f32[1056,8,128]{2,0,1:T(8,128)}, ...), condition=%wide.region_7.8_spmd.clone, body=%wide.region_6.7_spmd.clone.sunk | while | flops 1047144512 | bytes 55010524 | solution.py:77
  2358.0 175.7 %while.483 = (s32[]{:T(128)}, f32[1056,8,128]{2,0,1:T(8,128)}, f32[1056,8,128]{2,0,1:T(8,128)}, f32[8,32,24,128]{3,2,1,0:T(8,128)}, bf16[8,32,24,128]{3,2,1,0:T(...) while((s32[]{:T(128)}, f32[1056,8,128]{2,0,1:T(8,128)}, ...), condition=%wide.region_9.10_spmd.clone, body=%wide.region_8.9_spmd.clone.sunk | while | flops 1047144512 | bytes 55010524 | solution.py:77
  2535.6 175.3 %while.484 = (s32[]{:T(128)}, f32[1056,8,128]{2,0,1:T(8,128)}, f32[1056,8,128]{2,0,1:T(8,128)}, f32[8,32,24,128]{3,2,1,0:T(8,128)}, bf16[8,32,24,128]{3,2,1,0:T(...) while((s32[]{:T(128)}, f32[1056,8,128]{2,0,1:T(8,128)}, ...), condition=%wide.region_11.12_spmd.clone, body=%wide.region_10.11_spmd.clone.sunk | while | flops 1047144512 | bytes 55010524 | solution.py:77
  2712.8 175.4 %while.485 = (s32[]{:T(128)}, f32[1056,8,128]{2,0,1:T(8,128)}, f32[1056,8,128]{2,0,1:T(8,128)}, f32[8,32,24,128]{3,2,1,0:T(8,128)}, bf16[8,32,24,128]{3,2,1,0:T(...) while((s32[]{:T(128)}, f32[1056,8,128]{2,0,1:T(8,128)}, ...), condition=%wide.region_13.14_spmd.clone, body=%wide.region_12.13_spmd.clone.sunk | while | flops 1047144512 | bytes 55010524 | solution.py:77
  2890.1 175.3 %while.486 = (s32[]{:T(128)}, f32[1056,8,128]{2,0,1:T(8,128)}, f32[1056,8,128]{2,0,1:T(8,128)}, f32[8,32,24,128]{3,2,1,0:T(8,128)}, bf16[8,32,24,128]{3,2,1,0:T(...) while((s32[]{:T(128)}, f32[1056,8,128]{2,0,1:T(8,128)}, ...), condition=%wide.region_15.16_spmd.clone, body=%wide.region_14.15_spmd.clone.sunk | while | flops 1047144512 | bytes 55010524 | solution.py:77
  3067.3 175.5 %while.487 = (s32[]{:T(128)}, f32[1056,8,128]{2,0,1:T(8,128)}, f32[1056,8,128]{2,0,1:T(8,128)}, f32[8,32,24,128]{3,2,1,0:T(8,128)}, bf16[8,32,24,128]{3,2,1,0:T(...) while((s32[]{:T(128)}, f32[1056,8,128]{2,0,1:T(8,128)}, ...), condition=%wide.region_17.18_spmd.clone, body=%wide.region_16.17_spmd.clone.sunk | while | flops 1047144512 | bytes 55010524 | solution.py:77
  3244.8 175.3 %while.488 = (s32[]{:T(128)}, f32[1056,8,128]{2,0,1:T(8,128)}, f32[1056,8,128]{2,0,1:T(8,128)}, f32[8,32,24,128]{3,2,1,0:T(8,128)}, bf16[8,32,24,128]{3,2,1,0:T(...) while((s32[]{:T(128)}, f32[1056,8,128]{2,0,1:T(8,128)}, ...), condition=%wide.region_19.20_spmd.clone, body=%wide.region_18.19_spmd.clone.sunk | while | flops 1047144512 | bytes 55010524 | solution.py:77
  3422.0 175.7 %while.489 = (s32[]{:T(128)}, f32[1056,8,128]{2,0,1:T(8,128)}, f32[1056,8,128]{2,0,1:T(8,128)}, f32[8,32,24,128]{3,2,1,0:T(8,128)}, bf16[8,32,24,128]{3,2,1,0:T(...) while((s32[]{:T(128)}, f32[1056,8,128]{2,0,1:T(8,128)}, ...), condition=%wide.region_21.22_spmd.clone, body=%wide.region_20.21_spmd.clone.sunk | while | flops 1047144512 | bytes 55010524 | solution.py:77
  3599.6 175.3 %while.490 = (s32[]{:T(128)}, f32[1056,8,128]{2,0,1:T(8,128)}, f32[1056,8,128]{2,0,1:T(8,128)}, f32[8,32,24,128]{3,2,1,0:T(8,128)}, bf16[8,32,24,128]{3,2,1,0:T(...) while((s32[]{:T(128)}, f32[1056,8,128]{2,0,1:T(8,128)}, ...), condition=%wide.region_23.24_spmd.clone, body=%wide.region_22.23_spmd.clone.sunk | while | flops 1047144512 | bytes 55010524 | solution.py:77
  3776.7 175.4 %while.491 = (s32[]{:T(128)}, f32[1056,8,128]{2,0,1:T(8,128)}, f32[1056,8,128]{2,0,1:T(8,128)}, f32[8,32,24,128]{3,2,1,0:T(8,128)}, bf16[8,32,24,128]{3,2,1,0:T(...) while((s32[]{:T(128)}, f32[1056,8,128]{2,0,1:T(8,128)}, ...), condition=%wide.region_25.26_spmd.clone, body=%wide.region_24.25_spmd.clone.sunk | while | flops 1047144512 | bytes 55010524 | solution.py:77
  3954.1 175.3 %while.492 = (s32[]{:T(128)}, f32[1056,8,128]{2,0,1:T(8,128)}, f32[1056,8,128]{2,0,1:T(8,128)}, f32[8,32,24,128]{3,2,1,0:T(8,128)}, bf16[8,32,24,128]{3,2,1,0:T(...) while((s32[]{:T(128)}, f32[1056,8,128]{2,0,1:T(8,128)}, ...), condition=%wide.region_27.28_spmd.clone, body=%wide.region_26.27_spmd.clone.sunk | while | flops 1047144512 | bytes 55010524 | solution.py:77
  4131.3 175.5 %while.493 = (s32[]{:T(128)}, f32[1056,8,128]{2,0,1:T(8,128)}, f32[1056,8,128]{2,0,1:T(8,128)}, f32[8,32,24,128]{3,2,1,0:T(8,128)}, bf16[8,32,24,128]{3,2,1,0:T(...) while((s32[]{:T(128)}, f32[1056,8,128]{2,0,1:T(8,128)}, ...), condition=%wide.region_29.30_spmd.clone, body=%wide.region_28.29_spmd.clone.sunk | while | flops 1047144512 | bytes 55010524 | solution.py:77
  4308.7 175.3 %while.494 = (s32[]{:T(128)}, f32[1056,8,128]{2,0,1:T(8,128)}, f32[1056,8,128]{2,0,1:T(8,128)}, f32[8,32,24,128]{3,2,1,0:T(8,128)}, bf16[8,32,24,128]{3,2,1,0:T(...) while((s32[]{:T(128)}, f32[1056,8,128]{2,0,1:T(8,128)}, ...), condition=%wide.region_31.32_spmd.clone, body=%wide.region_30.31_spmd.clone.sunk | while | flops 1047144512 | bytes 55010524 | solution.py:77
  4485.8 175.7 %while.495 = (s32[]{:T(128)}, f32[1056,8,128]{2,0,1:T(8,128)}, f32[1056,8,128]{2,0,1:T(8,128)}, f32[8,32,24,128]{3,2,1,0:T(8,128)}, bf16[8,32,24,128]{3,2,1,0:T(...) while((s32[]{:T(128)}, f32[1056,8,128]{2,0,1:T(8,128)}, ...), condition=%wide.region_33.34_spmd.clone, body=%wide.region_32.33_spmd.clone.sunk | while | flops 1047144512 | bytes 55010524 | solution.py:77
  4663.4 175.3 %while.496 = (s32[]{:T(128)}, f32[1056,8,128]{2,0,1:T(8,128)}, f32[1056,8,128]{2,0,1:T(8,128)}, f32[8,32,24,128]{3,2,1,0:T(8,128)}, bf16[8,32,24,128]{3,2,1,0:T(...) while((s32[]{:T(128)}, f32[1056,8,128]{2,0,1:T(8,128)}, ...), condition=%wide.region_35.36_spmd.clone, body=%wide.region_34.35_spmd.clone.sunk | while | flops 1047144512 | bytes 55010524 | solution.py:77
  4840.7 175.4 %while.497 = (s32[]{:T(128)}, f32[1056,8,128]{2,0,1:T(8,128)}, f32[1056,8,128]{2,0,1:T(8,128)}, f32[8,32,24,128]{3,2,1,0:T(8,128)}, bf16[8,32,24,128]{3,2,1,0:T(...) while((s32[]{:T(128)}, f32[1056,8,128]{2,0,1:T(8,128)}, ...), condition=%wide.region_37.38_spmd.clone, body=%wide.region_36.37_spmd.clone.sunk | while | flops 1047144512 | bytes 55010524 | solution.py:77
  5018.0 175.3 %while.498 = (s32[]{:T(128)}, f32[1056,8,128]{2,0,1:T(8,128)}, f32[1056,8,128]{2,0,1:T(8,128)}, f32[8,32,24,128]{3,2,1,0:T(8,128)}, bf16[8,32,24,128]{3,2,1,0:T(...) while((s32[]{:T(128)}, f32[1056,8,128]{2,0,1:T(8,128)}, ...), condition=%wide.region_39.40_spmd.clone, body=%wide.region_38.39_spmd.clone.sunk | while | flops 1047144512 | bytes 55010524 | solution.py:77
  5195.2 175.5 %while.499 = (s32[]{:T(128)}, f32[1056,8,128]{2,0,1:T(8,128)}, f32[1056,8,128]{2,0,1:T(8,128)}, f32[8,32,24,128]{3,2,1,0:T(8,128)}, bf16[8,32,24,128]{3,2,1,0:T(...) while((s32[]{:T(128)}, f32[1056,8,128]{2,0,1:T(8,128)}, ...), condition=%wide.region_41.42_spmd.clone, body=%wide.region_40.41_spmd.clone.sunk | while | flops 1047144512 | bytes 55010524 | solution.py:77
  5372.6 175.3 %while.500 = (s32[]{:T(128)}, f32[1056,8,128]{2,0,1:T(8,128)}, f32[1056,8,128]{2,0,1:T(8,128)}, f32[8,32,24,128]{3,2,1,0:T(8,128)}, bf16[8,32,24,128]{3,2,1,0:T(...) while((s32[]{:T(128)}, f32[1056,8,128]{2,0,1:T(8,128)}, ...), condition=%wide.region_43.44_spmd.clone, body=%wide.region_42.43_spmd.clone.sunk | while | flops 1047144512 | bytes 55010524 | solution.py:77
  5549.8 175.7 %while.501 = (s32[]{:T(128)}, f32[1056,8,128]{2,0,1:T(8,128)}, f32[1056,8,128]{2,0,1:T(8,128)}, f32[8,32,24,128]{3,2,1,0:T(8,128)}, bf16[8,32,24,128]{3,2,1,0:T(...) while((s32[]{:T(128)}, f32[1056,8,128]{2,0,1:T(8,128)}, ...), condition=%wide.region_45.46_spmd.clone, body=%wide.region_44.45_spmd.clone.sunk | while | flops 1047144512 | bytes 55010524 | solution.py:77
  5727.4 175.3 %while.502 = (s32[]{:T(128)}, f32[1056,8,128]{2,0,1:T(8,128)}, f32[1056,8,128]{2,0,1:T(8,128)}, f32[8,32,24,128]{3,2,1,0:T(8,128)}, bf16[8,32,24,128]{3,2,1,0:T(...) while((s32[]{:T(128)}, f32[1056,8,128]{2,0,1:T(8,128)}, ...), condition=%wide.region_47.48_spmd.clone, body=%wide.region_46.47_spmd.clone.sunk | while | flops 1047144512 | bytes 55010524 | solution.py:77
  5904.5 175.4 %while.503 = (s32[]{:T(128)}, f32[1056,8,128]{2,0,1:T(8,128)}, f32[1056,8,128]{2,0,1:T(8,128)}, f32[8,32,24,128]{3,2,1,0:T(8,128)}, bf16[8,32,24,128]{3,2,1,0:T(...) while((s32[]{:T(128)}, f32[1056,8,128]{2,0,1:T(8,128)}, ...), condition=%wide.region_49.50_spmd.clone, body=%wide.region_48.49_spmd.clone.sunk | while | flops 1047144512 | bytes 55010524 | solution.py:77
  6081.9 175.3 %while.504 = (s32[]{:T(128)}, f32[1056,8,128]{2,0,1:T(8,128)}, f32[1056,8,128]{2,0,1:T(8,128)}, f32[8,32,24,128]{3,2,1,0:T(8,128)}, bf16[8,32,24,128]{3,2,1,0:T(...) while((s32[]{:T(128)}, f32[1056,8,128]{2,0,1:T(8,128)}, ...), condition=%wide.region_51.52_spmd.clone, body=%wide.region_50.51_spmd.clone.sunk | while | flops 1047144512 | bytes 55010524 | solution.py:77
  6259.0 175.5 %while.505 = (s32[]{:T(128)}, f32[1056,8,128]{2,0,1:T(8,128)}, f32[1056,8,128]{2,0,1:T(8,128)}, f32[8,32,24,128]{3,2,1,0:T(8,128)}, bf16[8,32,24,128]{3,2,1,0:T(...) while((s32[]{:T(128)}, f32[1056,8,128]{2,0,1:T(8,128)}, ...), condition=%wide.region_53.54_spmd.clone, body=%wide.region_52.53_spmd.clone.sunk | while | flops 1047144512 | bytes 55010524 | solution.py:77
  6436.4 175.3 %while.506 = (s32[]{:T(128)}, f32[1056,8,128]{2,0,1:T(8,128)}, f32[1056,8,128]{2,0,1:T(8,128)}, f32[8,32,24,128]{3,2,1,0:T(8,128)}, bf16[8,32,24,128]{3,2,1,0:T(...) while((s32[]{:T(128)}, f32[1056,8,128]{2,0,1:T(8,128)}, ...), condition=%wide.region_55.56_spmd.clone, body=%wide.region_54.55_spmd.clone.sunk | while | flops 1047144512 | bytes 55010524 | solution.py:77
  6613.6 175.7 %while.507 = (s32[]{:T(128)}, f32[1056,8,128]{2,0,1:T(8,128)}, f32[1056,8,128]{2,0,1:T(8,128)}, f32[8,32,24,128]{3,2,1,0:T(8,128)}, bf16[8,32,24,128]{3,2,1,0:T(...) while((s32[]{:T(128)}, f32[1056,8,128]{2,0,1:T(8,128)}, ...), condition=%wide.region_57.58_spmd.clone, body=%wide.region_56.57_spmd.clone.sunk | while | flops 1047144512 | bytes 55010524 | solution.py:77
  6791.2 175.3 %while.508 = (s32[]{:T(128)}, f32[1056,8,128]{2,0,1:T(8,128)}, f32[1056,8,128]{2,0,1:T(8,128)}, f32[8,32,24,128]{3,2,1,0:T(8,128)}, bf16[8,32,24,128]{3,2,1,0:T(...) while((s32[]{:T(128)}, f32[1056,8,128]{2,0,1:T(8,128)}, ...), condition=%wide.region_59.60_spmd.clone, body=%wide.region_58.59_spmd.clone.sunk | while | flops 1047144512 | bytes 55010524 | solution.py:77
  6968.4 175.4 %while.509 = (s32[]{:T(128)}, f32[1056,8,128]{2,0,1:T(8,128)}, f32[1056,8,128]{2,0,1:T(8,128)}, f32[8,32,24,128]{3,2,1,0:T(8,128)}, bf16[8,32,24,128]{3,2,1,0:T(...) while((s32[]{:T(128)}, f32[1056,8,128]{2,0,1:T(8,128)}, ...), condition=%wide.region_61.62_spmd.clone, body=%wide.region_60.61_spmd.clone.sunk | while | flops 1047144512 | bytes 55010524 | solution.py:77
  7145.8 175.3 %while.510 = (s32[]{:T(128)}, f32[1056,8,128]{2,0,1:T(8,128)}, f32[1056,8,128]{2,0,1:T(8,128)}, f32[8,32,24,128]{3,2,1,0:T(8,128)}, bf16[8,32,24,128]{3,2,1,0:T(...) while((s32[]{:T(128)}, f32[1056,8,128]{2,0,1:T(8,128)}, ...), condition=%wide.region_63.64_spmd.clone, body=%wide.region_62.63_spmd.clone.sunk | while | flops 1047144512 | bytes 55010524 | solution.py:77
  7449.5 42.7 reduce-scatter.135.cloned.1.call-done
  7492.3 42.7 reduce-scatter.137.cloned.1.call-done
  7577.8 42.7 reduce-scatter.141.cloned.1.call-done
  7748.5 42.7 reduce-scatter.149.cloned.1.call-done
  7833.9 42.7 reduce-scatter.153.cloned.1.call-done
  7876.7 42.7 reduce-scatter.155.cloned.1.call-done
  7919.5 42.7 reduce-scatter.157.cloned.1.call-done
  7962.3 42.7 reduce-scatter.159.cloned.1.call-done
  8005.1 42.7 reduce-scatter.161.cloned.1.call-done
  8090.5 42.7 reduce-scatter.165.cloned.1.call-done
  8176.0 42.7 reduce-scatter.169.cloned.1.call-done
  8346.7 42.7 reduce-scatter.177.cloned.1.call-done
  8389.5 42.7 reduce-scatter.179.cloned.1.call-done
  8432.3 42.7 reduce-scatter.181.cloned.1.call-done
  8560.3 42.7 reduce-scatter.187.cloned.1.call-done
  8603.1 42.7 reduce-scatter.189.cloned.1.call-done
  (5333 shorter events, 8605.4 us)
Async XLA Ops:
  199.7 2865.6 %all-gather.225.cloned.1.call-start = ((), (), s32[]{:S(2)}) async-start(), calls=%async_computation.112 | async-start | bytes 2359296 | tf_op jit(solution)/shard_map/all_gather | solution.py:36
  222.3 3020.5 %all-gather.229.cloned.1.call-start = ((), (), s32[]{:S(2)}) async-start(), calls=%async_computation.114 | async-start | bytes 2359296 | tf_op jit(solution)/shard_map/all_gather | solution.py:36
  233.3 3009.5 %all-gather.231.cloned.1.call-start = ((), (), s32[]{:S(2)}) async-start(), calls=%async_computation.115 | async-start | bytes 2359296 | tf_op jit(solution)/shard_map/all_gather | solution.py:36
  244.9 3175.2 %all-gather.233.cloned.1.call-start = ((), (), s32[]{:S(2)}) async-start(), calls=%async_computation.116 | async-start | bytes 2359296 | tf_op jit(solution)/shard_map/all_gather | solution.py:36
  255.9 3164.2 %all-gather.235.cloned.1.call-start = ((), (), s32[]{:S(2)}) async-start(), calls=%async_computation.117 | async-start | bytes 2359296 | tf_op jit(solution)/shard_map/all_gather | solution.py:36
  267.4 3330.2 %all-gather.237.cloned.1.call-start = ((), (), s32[]{:S(2)}) async-start(), calls=%async_computation.118 | async-start | bytes 2359296 | tf_op jit(solution)/shard_map/all_gather | solution.py:36
  278.7 3319.0 %all-gather.239.cloned.1.call-start = ((), (), s32[]{:S(2)}) async-start(), calls=%async_computation.119 | async-start | bytes 2359296 | tf_op jit(solution)/shard_map/all_gather | solution.py:36
  289.7 3485.1 %all-gather.241.cloned.1.call-start = ((), (), s32[]{:S(2)}) async-start(), calls=%async_computation.120 | async-start | bytes 2359296 | tf_op jit(solution)/shard_map/all_gather | solution.py:36
  305.1 3469.7 %all-gather.243.cloned.1.call-start = ((), (), s32[]{:S(2)}) async-start(), calls=%async_computation.121 | async-start | bytes 2359296 | tf_op jit(solution)/shard_map/all_gather | solution.py:36
  320.4 3631.8 %all-gather.245.cloned.1.call-start = ((), (), s32[]{:S(2)}) async-start(), calls=%async_computation.122 | async-start | bytes 2359296 | tf_op jit(solution)/shard_map/all_gather | solution.py:36
  332.9 3619.3 %all-gather.247.cloned.1.call-start = ((), (), s32[]{:S(2)}) async-start(), calls=%async_computation.123 | async-start | bytes 2359296 | tf_op jit(solution)/shard_map/all_gather | solution.py:36
  345.7 3783.7 %all-gather.249.cloned.1.call-start = ((), (), s32[]{:S(2)}) async-start(), calls=%async_computation.124 | async-start | bytes 2359296 | tf_op jit(solution)/shard_map/all_gather | solution.py:36
  358.2 3771.2 %all-gather.251.cloned.1.call-start = ((), (), s32[]{:S(2)}) async-start(), calls=%async_computation.125 | async-start | bytes 2359296 | tf_op jit(solution)/shard_map/all_gather | solution.py:36
  370.6 3936.1 %all-gather.253.cloned.1.call-start = ((), (), s32[]{:S(2)}) async-start(), calls=%async_computation.126 | async-start | bytes 2359296 | tf_op jit(solution)/shard_map/all_gather | solution.py:36
  383.1 3923.6 %all-gather.255.cloned.1.call-start = ((), (), s32[]{:S(2)}) async-start(), calls=%async_computation.127 | async-start | bytes 2359296 | tf_op jit(solution)/shard_map/all_gather | solution.py:36
  395.6 4088.3 %all-gather.257.cloned.1.call-start = ((), (), s32[]{:S(2)}) async-start(), calls=%async_computation.128 | async-start | bytes 2359296 | tf_op jit(solution)/shard_map/all_gather | solution.py:36
  408.1 4075.9 %all-gather.259.cloned.1.call-start = ((), (), s32[]{:S(2)}) async-start(), calls=%async_computation.129 | async-start | bytes 2359296 | tf_op jit(solution)/shard_map/all_gather | solution.py:36
  420.6 4240.9 %all-gather.261.cloned.1.call-start = ((), (), s32[]{:S(2)}) async-start(), calls=%async_computation.130 | async-start | bytes 2359296 | tf_op jit(solution)/shard_map/all_gather | solution.py:36
  433.0 4228.5 %all-gather.263.cloned.1.call-start = ((), (), s32[]{:S(2)}) async-start(), calls=%async_computation.131 | async-start | bytes 2359296 | tf_op jit(solution)/shard_map/all_gather | solution.py:36
  445.5 4393.2 %all-gather.265.cloned.1.call-start = ((), (), s32[]{:S(2)}) async-start(), calls=%async_computation.132 | async-start | bytes 2359296 | tf_op jit(solution)/shard_map/all_gather | solution.py:36
  458.0 4380.7 %all-gather.267.cloned.1.call-start = ((), (), s32[]{:S(2)}) async-start(), calls=%async_computation.133 | async-start | bytes 2359296 | tf_op jit(solution)/shard_map/all_gather | solution.py:36
  470.5 4545.6 %all-gather.269.cloned.1.call-start = ((), (), s32[]{:S(2)}) async-start(), calls=%async_computation.134 | async-start | bytes 2359296 | tf_op jit(solution)/shard_map/all_gather | solution.py:36
  483.2 4533.0 %all-gather.271.cloned.1.call-start = ((), (), s32[]{:S(2)}) async-start(), calls=%async_computation.135 | async-start | bytes 2359296 | tf_op jit(solution)/shard_map/all_gather | solution.py:36
  495.6 4697.7 %all-gather.273.cloned.1.call-start = ((), (), s32[]{:S(2)}) async-start(), calls=%async_computation.136 | async-start | bytes 2359296 | tf_op jit(solution)/shard_map/all_gather | solution.py:36
  508.1 4685.2 %all-gather.275.cloned.1.call-start = ((), (), s32[]{:S(2)}) async-start(), calls=%async_computation.137 | async-start | bytes 2359296 | tf_op jit(solution)/shard_map/all_gather | solution.py:36
  520.6 4850.1 %all-gather.277.cloned.1.call-start = ((), (), s32[]{:S(2)}) async-start(), calls=%async_computation.138 | async-start | bytes 2359296 | tf_op jit(solution)/shard_map/all_gather | solution.py:36
  533.0 4837.6 %all-gather.279.cloned.1.call-start = ((), (), s32[]{:S(2)}) async-start(), calls=%async_computation.139 | async-start | bytes 2359296 | tf_op jit(solution)/shard_map/all_gather | solution.py:36
  545.5 5002.3 %all-gather.281.cloned.1.call-start = ((), (), s32[]{:S(2)}) async-start(), calls=%async_computation.140 | async-start | bytes 2359296 | tf_op jit(solution)/shard_map/all_gather | solution.py:36
  558.0 4989.9 %all-gather.283.cloned.1.call-start = ((), (), s32[]{:S(2)}) async-start(), calls=%async_computation.141 | async-start | bytes 2359296 | tf_op jit(solution)/shard_map/all_gather | solution.py:36
  570.5 5155.0 %all-gather.285.cloned.1.call-start = ((), (), s32[]{:S(2)}) async-start(), calls=%async_computation.142 | async-start | bytes 2359296 | tf_op jit(solution)/shard_map/all_gather | solution.py:36
  581.4 5144.0 %all-gather.287.cloned.1.call-start = ((), (), s32[]{:S(2)}) async-start(), calls=%async_computation.143 | async-start | bytes 2359296 | tf_op jit(solution)/shard_map/all_gather | solution.py:36
  592.7 5309.9 %all-gather.289.cloned.1.call-start = ((), (), s32[]{:S(2)}) async-start(), calls=%async_computation.144 | async-start | bytes 2359296 | tf_op jit(solution)/shard_map/all_gather | solution.py:36
  604.0 5298.6 %all-gather.291.cloned.1.call-start = ((), (), s32[]{:S(2)}) async-start(), calls=%async_computation.145 | async-start | bytes 2359296 | tf_op jit(solution)/shard_map/all_gather | solution.py:36
  615.2 5464.7 %all-gather.293.cloned.1.call-start = ((), (), s32[]{:S(2)}) async-start(), calls=%async_computation.146 | async-start | bytes 2359296 | tf_op jit(solution)/shard_map/all_gather | solution.py:36
  626.5 5453.4 %all-gather.295.cloned.1.call-start = ((), (), s32[]{:S(2)}) async-start(), calls=%async_computation.147 | async-start | bytes 2359296 | tf_op jit(solution)/shard_map/all_gather | solution.py:36
  637.6 5619.6 %all-gather.297.cloned.1.call-start = ((), (), s32[]{:S(2)}) async-start(), calls=%async_computation.148 | async-start | bytes 2359296 | tf_op jit(solution)/shard_map/all_gather | solution.py:36
  649.1 5608.0 %all-gather.299.cloned.1.call-start = ((), (), s32[]{:S(2)}) async-start(), calls=%async_computation.149 | async-start | bytes 2359296 | tf_op jit(solution)/shard_map/all_gather | solution.py:36
  660.4 5774.1 %all-gather.301.cloned.1.call-start = ((), (), s32[]{:S(2)}) async-start(), calls=%async_computation.150 | async-start | bytes 2359296 | tf_op jit(solution)/shard_map/all_gather | solution.py:36
  671.7 5762.8 %all-gather.303.cloned.1.call-start = ((), (), s32[]{:S(2)}) async-start(), calls=%async_computation.151 | async-start | bytes 2359296 | tf_op jit(solution)/shard_map/all_gather | solution.py:36
  683.0 5928.7 %all-gather.305.cloned.1.call-start = ((), (), s32[]{:S(2)}) async-start(), calls=%async_computation.152 | async-start | bytes 2359296 | tf_op jit(solution)/shard_map/all_gather | solution.py:36
  694.3 5917.4 %all-gather.307.cloned.1.call-start = ((), (), s32[]{:S(2)}) async-start(), calls=%async_computation.153 | async-start | bytes 2359296 | tf_op jit(solution)/shard_map/all_gather | solution.py:36
  705.6 6083.7 %all-gather.309.cloned.1.call-start = ((), (), s32[]{:S(2)}) async-start(), calls=%async_computation.154 | async-start | bytes 2359296 | tf_op jit(solution)/shard_map/all_gather | solution.py:36
  716.6 6072.7 %all-gather.311.cloned.1.call-start = ((), (), s32[]{:S(2)}) async-start(), calls=%async_computation.155 | async-start | bytes 2359296 | tf_op jit(solution)/shard_map/all_gather | solution.py:36
  728.2 6238.3 %all-gather.313.cloned.1.call-start = ((), (), s32[]{:S(2)}) async-start(), calls=%async_computation.156 | async-start | bytes 2359296 | tf_op jit(solution)/shard_map/all_gather | solution.py:36
  739.6 6226.9 %all-gather.315.cloned.1.call-start = ((), (), s32[]{:S(2)}) async-start(), calls=%async_computation.157 | async-start | bytes 2359296 | tf_op jit(solution)/shard_map/all_gather | solution.py:36
  750.6 6393.2 %all-gather.317.cloned.1.call-start = ((), (), s32[]{:S(2)}) async-start(), calls=%async_computation.158 | async-start | bytes 2359296 | tf_op jit(solution)/shard_map/all_gather | solution.py:36
  762.1 6381.7 %all-gather.319.cloned.1.call-start = ((), (), s32[]{:S(2)}) async-start(), calls=%async_computation.159 | async-start | bytes 2359296 | tf_op jit(solution)/shard_map/all_gather | solution.py:36
  773.2 6591.0 %reduce-scatter.129.cloned.1.call-start = ((), (), s32[]{:S(2)}) async-start(), calls=%async_computation.64 | async-start | bytes 4718592 | tf_op jit(solution)/shard_map/reduce_scatter | solution.py:41
  (347 other events, 96891.1 us)
Sparse Core Ops, SparseCore 0:
  20.7 26.5 all-gather.192
  790.9 26.2 all-gather.252
  818.8 25.8 all-gather.254
  846.0 25.9 all-gather.256
  873.6 26.1 all-gather.258
  901.3 25.9 all-gather.260
  928.6 25.6 all-gather.262
  955.7 25.6 all-gather.264
  983.0 25.6 all-gather.266
  1010.1 25.6 all-gather.268
  1037.3 25.7 all-gather.270
  1064.6 25.8 all-gather.272
  1199.0 25.6 all-gather.282
  1226.1 25.6 all-gather.284
  1333.8 25.7 all-gather.292
  1522.7 25.8 all-gather.306
  7321.2 42.9 reduce-scatter.128
  7366.2 40.5 reduce-scatter.130
  7408.9 40.5 reduce-scatter.132
  7451.6 40.5 reduce-scatter.134
  7494.4 40.5 reduce-scatter.136
  7537.1 40.5 reduce-scatter.138
  7579.9 40.5 reduce-scatter.140
  7622.5 40.5 reduce-scatter.142
  7665.2 40.5 reduce-scatter.144
  7707.8 40.5 reduce-scatter.146
  7750.6 40.5 reduce-scatter.148
  7793.3 40.5 reduce-scatter.150
  7836.1 40.5 reduce-scatter.152
  7878.8 40.5 reduce-scatter.154
  7921.6 40.5 reduce-scatter.156
  7964.4 40.5 reduce-scatter.158
  8007.2 40.5 reduce-scatter.160
  8049.9 40.5 reduce-scatter.162
  8092.7 40.5 reduce-scatter.164
  8135.3 40.5 reduce-scatter.166
  8178.1 40.5 reduce-scatter.168
  8220.7 40.5 reduce-scatter.170
  8263.4 40.5 reduce-scatter.172
  8306.0 40.5 reduce-scatter.174
  8348.8 40.5 reduce-scatter.176
  8391.6 40.5 reduce-scatter.178
  8434.4 40.5 reduce-scatter.180
  8477.1 40.5 reduce-scatter.182
  8519.7 40.5 reduce-scatter.184
  8562.5 40.5 reduce-scatter.186
  8605.3 40.5 reduce-scatter.188
  8648.1 40.5 reduce-scatter.190
  (80 shorter events, 1889.8 us)
where the time goes:
time: 9560 us; the launch traced here: 9490 us
  matrix products  4410 us (46%)
  waiting for transfers between devices  2090 us (22%)
  blocking collectives  1610 us (17%)
  local copies, waits for them, and re-layouts  1090 us (11%)
  loops' own time  185 us (2%)
    reduce_scatter x32, waiting for transfers between devices, scatter_sum(): outer_part = lax.psum_scatter(grouped, 'cp_outer', scatter_dimension=0)  1330 us
    dot_general x256, matrix products, block_grads(): jnp.einsum('hgqk,qhgd->khd', ds_low, q_four, preferred_element_type=jnp.f...  1330 us
    dot_general x256, matrix products, block_grads(): jnp.einsum('hgqk,qhgd->khd', p_low, do_four, preferred_element_type=jnp.f...  1310 us
    all_gather x128, blocking collectives, gather_all(): inner_part = lax.all_gather(local_part, 'cp', axis=0)  1310 us
    dot_general x256, matrix products, block_grads(): jnp.einsum('qhgd,khd->hgqk', do_four, v_block, preferred_element_type=jnp...  909 us
    unnamed x160, waiting for transfers between devices  761 us
    dot_general x256, matrix products, block_grads(): jnp.einsum('qhgd,khd->hgqk', q_four, k_block, preferred_element_type=jnp....  685 us
    dynamic_slice x1280, local copies, waits for them, and re-layouts, local_grads(): lax.scan(source_step, (dk_acc, dv_acc), (q_all, do_all, lse_all, delta_al...  608 us

commit v1 on v0

v1 whole, which is shorter than its diff:
```python
import functools

import jax
import jax.numpy as jnp
from jax import lax
from jax.experimental import pallas as pl
from jax.experimental.pallas import tpu as pltpu
from jax.sharding import PartitionSpec as P

MESH = pl.DeviceIdType.MESH
SEQ_AXES = ("cp_outer", "cp")
BF16 = jnp.bfloat16
F32 = jnp.float32
LOG2E = 1.4426950408889634
TILE = 256
WIDE = 4
AHEAD = 6


def dot(a, b, ca, cb):
    return lax.dot_general(a, b, (((ca,), (cb,)), ((), ())), preferred_element_type=F32)


def attn_kernel(dims, q_h, do_h, k_h, v_h, st_h, dq_o, dk_o, dv_o,
                q_b, do_b, k_b, v_b, st_b, col_b, k_t, q_t, do_t, dq_a, dk_a, dv_a, dk_s, dv_s,
                in_send, out_send, st_recv, kv_recv, row_recv, out_recv):
    n_dev, inner, n_segs, group, q_rows, head_dim, k_rows, late = dims
    scale = head_dim ** -0.5
    me = lax.axis_index("cp_outer") * inner + lax.axis_index("cp")
    n_tiles = n_segs + 1
    n_wide = n_tiles // WIDE
    first_late = n_segs - late
    late_tile = first_late + 1
    seg_rows = group * TILE

    def peer(i):
        return lax.rem(me + i, n_dev)

    def device(p):
        return (0, lax.div(p, inner), lax.rem(p, inner))

    barrier = pltpu.get_barrier_semaphore()
    for i in range(1, n_dev):
        pl.semaphore_signal(barrier, inc=1, device_id=device(peer(i)), device_id_type=MESH)
    pl.semaphore_wait(barrier, n_dev - 1)

    def send(i, src, dst, send_sem, recv_sem):
        if i == 0:
            pltpu.make_async_copy(src, dst, recv_sem).start()
        else:
            pltpu.make_async_remote_copy(src_ref=src, dst_ref=dst, send_sem=send_sem, recv_sem=recv_sem,
                                         device_id=device(peer(i)), device_id_type=MESH).start()

    def arrived(ref, sem):
        pltpu.make_async_copy(ref, ref, sem).wait()

    def send_kv():
        for i in range(n_dev):
            p = peer(i)
            rows = pl.ds(pl.multiple_of(me * k_rows, 32), k_rows)
            send(i, k_h.at[p], k_b.at[rows], in_send.at[1], kv_recv.at[0, me])
            send(i, v_h.at[p], v_b.at[rows], in_send.at[2], kv_recv.at[1, me])

    def send_pair(r):
        segs = pl.ds(2 * r, 2)
        rows = pl.ds(pl.multiple_of(me * q_rows, q_rows), q_rows)
        for i in range(n_dev):
            p = peer(i)
            send(i, q_h.at[p, segs], q_b.at[segs, :, rows], in_send.at[3], row_recv.at[0, r])
            send(i, do_h.at[p, segs], do_b.at[segs, :, rows], in_send.at[4], row_recv.at[1, r])

        @pl.when((me > 0) & (r == lax.max(2 * me - 3, 0)))
        def _():
            send_kv()

    for i in range(n_dev):
        send(i, st_h.at[peer(i)], st_b.at[me], in_send.at[0], st_recv)

    @pl.when(me == 0)
    def _():
        send_kv()

    @pl.loop(0, AHEAD)
    def _(r):
        send_pair(r)

    @pl.loop(0, n_tiles)
    def _(i):
        dk_a[i] = jnp.zeros((head_dim, TILE), F32)
        dv_a[i] = jnp.zeros((head_dim, TILE), F32)

    arrived(st_b, st_recv)

    @pl.loop(0, n_segs // 4)
    def _(g):
        for b in range(n_dev):
            block = st_b[b, :, pl.ds(pl.multiple_of(g * 128, 128), 128)].T
            for s in range(4):
                col_b[4 * g + s, pl.ds(b * q_rows, q_rows), 0:8] = block[s * q_rows:(s + 1) * q_rows]

    def grads(j, slot, first, n, masked):
        keys = pl.ds(pl.multiple_of(first * TILE, TILE), n * TILE)
        k_blk = k_b[keys, :]
        v_blk = v_b[keys, :]
        if masked:
            visible = (lax.broadcasted_iota(jnp.int32, (TILE, TILE), 0)
                       >= lax.broadcasted_iota(jnp.int32, (TILE, TILE), 1))
        p_low = []
        ds_low = []
        for h in range(group):
            s = dot(q_b[j, h], k_blk, 1, 1)
            dp = dot(do_b[j, h], v_blk, 1, 1)
            p = jnp.exp2(s * (scale * LOG2E) - col_b[j, :, h:h + 1])
            if masked:
                p = jnp.where(visible, p, 0.0)
            ds = p * (dp - col_b[j, :, group + h:group + h + 1])
            p_low.append(p.astype(BF16))
            ds_low.append(ds.astype(BF16))
        p_all = jnp.concatenate(p_low, 0)
        ds_all = jnp.concatenate(ds_low, 0)
        for t in range(n):
            cols = slice(t * TILE, (t + 1) * TILE)
            dv_a[first + t] += dot(do_t[slot], p_all[:, cols], 1, 0)
            dk_a[first + t] += dot(q_t[slot], ds_all[:, cols], 1, 0)
        for h in range(group):
            acc = dq_a[slot, h]
            for t in range(n):
                acc = acc + dot(k_t[first + t], ds_low[h][:, t * TILE:(t + 1) * TILE], 1, 1)
            dq_a[slot, h] = acc

    def open_row(j, slot):
        @pl.when(lax.rem(j, 2) == 0)
        def _():
            segs = pl.ds(pl.multiple_of(j, 2), 2)
            pair = lax.div(j, 2)
            arrived(q_b.at[segs], row_recv.at[0, pair])
            arrived(do_b.at[segs], row_recv.at[1, pair])

            @pl.when(pair + AHEAD < n_segs // 2)
            def _():
                send_pair(pair + AHEAD)

        @pl.when((j == 0) | ((lax.rem(j, 4) == 3) & (j < n_segs - 1)))
        def _():
            owner = lax.div(j + 1, 4)
            rows = pl.ds(pl.multiple_of(owner * k_rows, 32), k_rows)
            arrived(k_b.at[rows], kv_recv.at[0, owner])
            arrived(v_b.at[rows], kv_recv.at[1, owner])

        def turn_keys(t):
            k_t[t] = k_b[pl.ds(pl.multiple_of(t * TILE, TILE), TILE), :].T

        @pl.when(j == 0)
        def _():
            turn_keys(0)

        turn_keys(j + 1)
        q_t[slot] = q_b[j].reshape(seg_rows, head_dim).T
        do_t[slot] = do_b[j].reshape(seg_rows, head_dim).T
        dq_a[slot] = jnp.zeros((group, head_dim, TILE), F32)

    def span(j, slot, lo, hi):
        n = hi - lo

        @pl.loop(0, lax.div(n, WIDE))
        def _(c):
            grads(j, slot, lo + c * WIDE, WIDE, False)

        @pl.loop(hi - lax.rem(n, WIDE), hi)
        def _(t):
            grads(j, slot, t, 1, False)

        grads(j, slot, hi, 1, True)

    def close_row(j, slot):
        for h in range(group):
            q_b[j, h] = (dq_a[slot, h].T * scale).astype(BF16)
        for i in range(n_dev):
            p = peer(i)
            rows = pl.ds(pl.multiple_of(p * q_rows, q_rows), q_rows)
            send(i, q_b.at[j, :, rows], dq_o.at[me, j], out_send.at[0], out_recv.at[0])

    def close_tile(t):
        keys = pl.ds(pl.multiple_of(t * TILE, TILE), TILE)
        dk_s[keys, :] = dk_a[t].T * scale
        dv_s[keys, :] = dv_a[t].T

    def send_piece(r):
        owner = lax.div(r * 32, k_rows)
        src = pl.ds(pl.multiple_of(r * 32, 32), 32)
        dst = pl.ds(pl.multiple_of(r * 32 - owner * k_rows, 32), 32)

        @pl.when(owner == me)
        def _():
            pltpu.make_async_copy(dk_s.at[src], dk_o.at[me, dst], out_recv.at[1]).start()
            pltpu.make_async_copy(dv_s.at[src], dv_o.at[me, dst], out_recv.at[2]).start()

        @pl.when(owner != me)
        def _():
            for s, d, n in ((dk_s, dk_o, 1), (dv_s, dv_o, 2)):
                pltpu.make_async_remote_copy(src_ref=s.at[src], dst_ref=d.at[me, dst], send_sem=out_send.at[n],
                                             recv_sem=out_recv.at[n], device_id=device(owner),
                                             device_id_type=MESH).start()

    @pl.loop(0, first_late)
    def _(j):
        open_row(j, 0)
        span(j, 0, 0, j + 1)
        close_row(j, 0)

    @pl.loop(first_late, n_segs)
    def _(j):
        open_row(j, j - first_late)
        span(j, j - first_late, late_tile, j + 1)

    @pl.loop(late_tile, n_tiles)
    def _(t):
        close_tile(t)

    @pl.loop(0, n_wide)
    def _(i):
        c = lax.rem(me + i, n_wide)

        @pl.when(c * WIDE < late_tile)
        def _():
            @pl.loop(first_late, n_segs)
            def _(j):
                grads(j, j - first_late, c * WIDE, WIDE, False)

            @pl.loop(c * WIDE, c * WIDE + WIDE)
            def _(t):
                close_tile(t)

        @pl.loop(0, WIDE * TILE // 32)
        def _(r):
            send_piece(c * (WIDE * TILE // 32) + r)

    @pl.loop(0, TILE // 32)
    def _(r):
        send_piece(n_wide * (WIDE * TILE // 32) + r)

    @pl.loop(first_late, n_segs)
    def _(j):
        close_row(j, j - first_late)

    rest = n_dev - 1
    for n, ref in enumerate((st_h, k_h, v_h, q_h, do_h)):
        arrived(ref.at[pl.ds(0, rest)], in_send.at[n])
    for n, ref in enumerate((dq_o, dk_o, dv_o)):
        arrived(ref.at[pl.ds(0, rest)], out_send.at[n])
        arrived(ref, out_recv.at[n])


def solution(mesh):
    outer, inner = mesh.shape["cp_outer"], mesh.shape["cp"]
    n_dev = outer * inner
    seq_spec = P(None, SEQ_AXES, "heads", None)
    stat_spec = P(None, SEQ_AXES, "heads")
    kv_spec = P(SEQ_AXES, "heads", None)

    def local_grads(q, k, v, o, do, lse):
        n_segs, q_rows, q_heads, head_dim = q.shape
        k_rows, kv_heads, _ = k.shape
        group = q_heads // kv_heads
        late = 9
        n_tiles = n_segs + 1
        keys = n_dev * k_rows

        def by_head(x):
            return x.reshape(n_segs, q_rows, kv_heads, group, head_dim).transpose(2, 0, 3, 1, 4)

        def stat(x):
            return x.reshape(n_segs, q_rows, kv_heads, group).transpose(2, 3, 0, 1).reshape(
                kv_heads, group, n_segs * q_rows)

        delta = jnp.sum(do.astype(F32) * o.astype(F32), axis=-1)
        stats = jnp.concatenate(
            [stat(lse * LOG2E), stat(delta), jnp.zeros((kv_heads, 8 - 2 * group, n_segs * q_rows), F32)], axis=1)
        dims = (n_dev, inner, n_segs, group, q_rows, head_dim, k_rows, late)
        hbm = pl.BlockSpec(memory_space=pl.ANY)
        row = pltpu.VMEM((n_segs, group, TILE, head_dim), BF16)
        key = pltpu.VMEM((keys, head_dim), BF16)
        turned = pltpu.VMEM((late, head_dim, group * TILE), BF16)
        key_sum = pltpu.VMEM((n_tiles, head_dim, TILE), F32)
        key_out = pltpu.VMEM((keys, head_dim), F32)
        dma = pltpu.SemaphoreType.DMA
        dq, dk, dv = pl.pallas_call(
            functools.partial(attn_kernel, dims),
            out_shape=(jax.ShapeDtypeStruct((kv_heads, n_segs, group, q_rows, head_dim), BF16),
                       jax.ShapeDtypeStruct((kv_heads, k_rows, head_dim), F32),
                       jax.ShapeDtypeStruct((kv_heads, k_rows, head_dim), F32)),
            in_specs=[hbm] * 5,
            out_specs=(hbm,) * 3,
            scratch_shapes=[
                row, row, key, key,
                pltpu.VMEM((n_dev, 8, n_segs * q_rows), F32),
                pltpu.VMEM((n_segs, TILE, 128), F32),
                pltpu.VMEM((n_tiles, head_dim, TILE), BF16),
                turned, turned,
                pltpu.VMEM((late, group, head_dim, TILE), F32),
                key_sum, key_sum, key_out, key_out,
                dma((5,)), dma((3,)), dma, dma((2, n_dev)), dma((2, n_segs // 2)), dma((3,))],
            compiler_params=pltpu.CompilerParams(
                collective_id=0, has_side_effects=True, vmem_limit_bytes=67043328),
            cost_estimate=pl.CostEstimate(flops=1680 * 5 * 2 * 256 * 256 * 128, bytes_accessed=64 << 20,
                                          transcendentals=1680 * 65536),
            name="attn_grads",
        )(by_head(q), by_head(do), k.transpose(1, 0, 2), v.transpose(1, 0, 2), stats)
        dq = dq.transpose(1, 3, 0, 2, 4).reshape(n_segs, q_rows, q_heads, head_dim)
        return dq, dk.transpose(1, 0, 2), dv.transpose(1, 0, 2)

    return jax.shard_map(local_grads, mesh=mesh,
                         in_specs=(seq_spec, kv_spec, kv_spec, seq_spec, seq_spec, stat_spec),
                         out_specs=(seq_spec, kv_spec, kv_spec), check_vma=False)
```

time: 9560 us -> 487 us (0.05)
  the two profiles are of different devices: /device:TPU:1 before, /device:TPU:7 now
where the time goes in v1:
time: 487 us
  Pallas kernels  434 us (89%)
  local copies, waits for them, and re-layouts  41.9 us (9%)
  other arithmetic  9.96 us (2%)
    pallas_call x1, Pallas kernels, local_grads(): pl.pallas_call(functools.partial(attn_kernel, dims), out_shape=(jax.Shape...  434 us
    unnamed x19, local copies, waits for them, and re-layouts  25.4 us

profile of v1, /device:TPU:7, one launch (start us, length us, event | category | flops | bytes accessed | tf_op | source)
XLA Modules:
  0.0 486.8 jit_solution(12522190435856924487)
XLA Ops:
  0.6 0.1 pad.2.clone
  0.7 1.1 copy_multiply_fusion
  1.8 0.2 reshape.34
  2.0 0.0 copy-start
  2.0 8.1 %multiply_reduce_fusion = f32[32,32,24]{2,1,0:T(8,128)S(1)} fusion(bf16[32,32,24,128]{3,2,1,0:T(8,128)(2,1)} %param.9, bf16[32,32,24,128]{3,2,1,0:T(8,128)(2,1)} %param.10), kind=kLoop, calls=%fused_computation | loop fusion | flops 12558336 | bytes 12681216 | tf_op jit(solution)/shard_map/reduce_sum | solution.py:276
  10.1 0.4 copy.51
  10.5 0.2 reshape.35
  10.7 0.8 maximum_maximum_fusion.st_h
  11.5 0.0 copy-done
  11.5 0.0 slice-start
  11.5 4.4 copy_bitcast_fusion.2
  15.9 0.0 slice-start.1
  15.9 4.4 copy.43
  20.3 0.0 slice-done
  20.3 0.0 slice-done.1
  20.3 1.5 copy.45
  21.8 6.4 %copy_bitcast_fusion = (bf16[8,32,3,32,128]{4,3,2,1,0:T(8,128)(2,1)}, bf16[8,32,3,32,128]{4,3,2,1,0:T(8,128)(2,1)}) fusion(bf16[32,32,8,3,128]{4,1,3,2,0:T(8,128)(2,1)S(1)} %bitcast.28, bf16[32,32,8,3,128]{4,1,3,2,0:T(8,128)(2,1)S(1)} %bitcast.27), kind=kLoop, calls=%fused_computation.1 | loop fusion | bytes 25165824 | tf_op jit(solution)/shard_map/transpose | solution.py:270
  28.2 434.2 %attn_grads.1 = (bf16[8,32,3,32,128]{4,3,2,1,0:T(8,128)(2,1)}, f32[8,1056,128]{2,1,0:T(8,128)}, f32[8,1056,128]{2,1,0:T(8,128)}) custom-call(bf16[8,32,3,32,128]{4,3,2,1,0:T(8,128)(2,1)} %get-tuple-element.22.q_h, bf16[8,32,3,32,128]{4,3,2,1,0:T(8,128)(2,1)} %get-tuple-element.21.do_h, bf16[8,1056,128]{2,1,0:T(8,128)(2,1)} %get-tuple-element.24.k_h, ...), custom_call_target="tpu_custom_call" | custom-call | flops 140928614400 | bytes 67108864 | tf_op jit(solution)/shard_map/attn_grads/pallas_call | solution.py:287
  462.4 0.0 slice-start.4
  462.4 4.8 copy.55
  467.2 0.0 slice-start.5
  467.2 5.6 %copy.56 = bf16[32,32,24,128]{3,2,1,0:T(8,128)(2,1)} copy(bf16[32,32,24,128]{3,1,2,0:T(8,128)(2,1)S(1)} %bitcast.26) | data formatting | bytes 12582912
  472.9 0.0 slice-start.2
  472.9 0.0 slice-done.4
  472.9 0.0 slice-done.5
  472.9 0.0 slice-start.3
  472.9 6.9 %copy.57 = f32[1056,8,128]{2,1,0:T(8,128)} copy(f32[1056,8,128]{2,0,1:T(8,128)S(1)} %bitcast.35) | data formatting | bytes 8650752
  479.8 0.0 slice-done.2
  479.8 0.0 slice-done.3
  479.8 6.9 %copy.58 = f32[1056,8,128]{2,1,0:T(8,128)} copy(f32[1056,8,128]{2,0,1:T(8,128)S(1)} %bitcast.32) | data formatting | bytes 8650752
  (4 shorter events, 0.0 us)
Async XLA Ops:
  2.0 9.5 %copy-start = (bf16[1056,8,128]{2,1,0:T(8,128)(2,1)S(1)}, bf16[1056,8,128]{2,1,0:T(8,128)(2,1)}, u32[]{:S(2)}) copy-start(bf16[1056,8,128]{2,1,0:T(8,128)(2,1)} %param.8) | copy-start | bytes 6488068
  11.5 8.8 %slice-start = ((s8[6291456]{0:T(1024)(128)(4,1)}), s8[4194304]{0:T(1024)(128)(4,1)S(1)}, s32[]{:S(2)}) async-start(s8[6291456]{0:T(1024)(128)(4,1)} %bitcast.24), calls=%async_computation | async-start | bytes 8388608
  15.9 4.4 slice-start.1
  462.4 10.5 %slice-start.4 = ((s8[4325376]{0:T(1024)(128)(4,1)}), s8[4194304]{0:T(1024)(128)(4,1)S(1)}, s32[]{:S(2)}) async-start(s8[4325376]{0:T(1024)(128)(4,1)} %bitcast.33), calls=%async_computation.4 | async-start | bytes 8388608
  467.2 5.6 %slice-start.5 = ((s8[4325376]{0:T(1024)(128)(4,1)}), s8[131072]{0:T(1024)(128)(4,1)S(1)}, s32[]{:S(2)}) async-start(s8[4325376]{0:T(1024)(128)(4,1)} %bitcast.33), calls=%async_computation.5 | async-start | bytes 262144
  472.9 7.0 %slice-start.2 = ((s8[4325376]{0:T(1024)(128)(4,1)}), s8[4194304]{0:T(1024)(128)(4,1)S(1)}, s32[]{:S(2)}) async-start(s8[4325376]{0:T(1024)(128)(4,1)} %bitcast.30), calls=%async_computation.2 | async-start | bytes 8388608
  472.9 7.0 %slice-start.3 = ((s8[4325376]{0:T(1024)(128)(4,1)}), s8[131072]{0:T(1024)(128)(4,1)S(1)}, s32[]{:S(2)}) async-start(s8[4325376]{0:T(1024)(128)(4,1)} %bitcast.30), calls=%async_computation.3 | async-start | bytes 262144

commit v2 on v0

v2 whole, which is shorter than its diff:
```python
import functools

import jax
import jax.numpy as jnp
from jax import lax
from jax.experimental import pallas as pl
from jax.experimental.pallas import tpu as pltpu
from jax.sharding import PartitionSpec as P

MESH = pl.DeviceIdType.MESH
SEQ_AXES = ("cp_outer", "cp")
BF16 = jnp.bfloat16
F32 = jnp.float32
LOG2E = 1.4426950408889634
TILE = 256
WIDE = 4
RING = 8
PIECE = 32
CHUNK = 96


def dot(a, b, ca, cb):
    return lax.dot_general(a, b, (((ca,), (cb,)), ((), ())), preferred_element_type=F32)


def attn_kernel(dims, q_n, do_n, o_n, k_n, v_n, ls_n, dq_o, dk_o, dv_o,
                nat, nat_k, ls_v, stg, o_s, kv_s, st_s, q_b, do_b, k_b, v_b, st_b,
                k_t, v_t, q_t, do_t, dq_a, dk_a, dv_a, col, p_c, d_c,
                nat_sem, natk_sem, ls_sem, row_send, kv_send, st_send, out_send,
                row_recv, kv_recv, st_recv, out_recv):
    n_dev, inner, n_segs, group, q_rows, head_dim, k_rows, late = dims
    scale = head_dim ** -0.5
    me = lax.axis_index("cp_outer") * inner + lax.axis_index("cp")
    n_pairs = n_segs // 2
    n_tiles = n_segs + 1
    first_late = n_segs - late
    late_tile = first_late
    n_cols = late_tile // WIDE
    pieces = k_rows // PIECE
    rest = n_dev - 1
    my_rows = pl.ds(pl.multiple_of(me * q_rows, q_rows), q_rows)

    def peer(i):
        return lax.rem(me + i, n_dev)

    def device(p):
        return (0, lax.div(p, inner), lax.rem(p, inner))

    def remote(src, dst, send_sem, recv_sem, p):
        pltpu.make_async_remote_copy(src_ref=src, dst_ref=dst, send_sem=send_sem, recv_sem=recv_sem,
                                     device_id=device(p), device_id_type=MESH).start()

    def arrived(ref, sem):
        pltpu.make_async_copy(ref, ref, sem).wait()

    def fetch(r):
        for a, src in enumerate((q_n, do_n, o_n)):
            pltpu.make_async_copy(src.at[pl.ds(r * 2 * q_rows, 2 * q_rows)], nat.at[lax.rem(r, 2), a],
                                  nat_sem.at[lax.rem(r, 2), a]).start()

    def fetch_keys(c):
        for a, src in enumerate((k_n, v_n)):
            pltpu.make_async_copy(src.at[pl.ds(c * CHUNK, CHUNK)], nat_k.at[lax.rem(c, 2), a],
                                  natk_sem.at[lax.rem(c, 2), a]).start()

    def send_keys():
        fetch_keys(0)

        @pl.loop(0, k_rows // CHUNK)
        def _(c):
            buf = lax.rem(c, 2)
            rows = pl.ds(pl.multiple_of(c * CHUNK, CHUNK), CHUNK)
            dst = pl.ds(pl.multiple_of(me * k_rows + c * CHUNK, 32), CHUNK)
            for a in range(2):
                arrived(nat_k.at[buf, a], natk_sem.at[buf, a])

            @pl.when(c + 1 < k_rows // CHUNK)
            def _():
                fetch_keys(c + 1)

            for a, land in enumerate((k_b, v_b)):
                kv_s[a, :, rows] = jnp.transpose(nat_k[buf, a], (1, 0, 2))
                land[dst, :] = kv_s[a, me, rows]
            for i in range(1, n_dev):
                p = peer(i)
                for a, land in enumerate((k_b, v_b)):
                    remote(kv_s.at[a, p, rows], land.at[dst], kv_send.at[a], kv_recv.at[a, me], p)

    def send_pair(r):
        buf, slot = lax.rem(r, 2), lax.rem(r, RING)
        segs = pl.ds(2 * r, 2)
        for a in range(3):
            arrived(nat.at[buf, a], nat_sem.at[buf, a])

        @pl.when(r + 1 < n_pairs)
        def _():
            fetch(r + 1)

        @pl.when(r >= RING)
        def _():
            for a in range(2):
                arrived(stg.at[slot, a, pl.ds(0, rest)], row_send.at[a, slot])

        for u in range(4):
            half = slice(16 * (u % 2), 16 * (u % 2) + 16)
            for a in range(3):
                block = jnp.transpose(nat[buf, a, 16 * u:16 * u + 16], (1, 0, 2)).reshape(n_dev, group, 16, head_dim)
                if a < 2:
                    stg[slot, a, :, u // 2, :, half] = block
                else:
                    o_s[:, u // 2, :, half] = block
        for s in range(2):
            q_b[2 * r + s, :, my_rows] = stg[slot, 0, me, s]
            do_b[2 * r + s, :, my_rows] = stg[slot, 1, me, s]
        for i in range(1, n_dev):
            p = peer(i)
            for a, land in enumerate((q_b, do_b)):
                remote(stg.at[slot, a, p], land.at[segs, :, my_rows], row_send.at[a, slot], row_recv.at[a, r], p)

        ones = jnp.ones((8, head_dim), BF16)
        blank = jnp.zeros((1, 128 - group * q_rows), F32)
        for p in range(n_dev):
            for s in range(2):
                rows = group * q_rows
                prod = (stg[slot, 1, p, s].reshape(rows, head_dim).astype(F32)
                        * o_s[p, s].reshape(rows, head_dim).astype(F32))
                hi = prod.astype(BF16)
                prod = prod - hi.astype(F32)
                mid = prod.astype(BF16)
                low = (prod - mid.astype(F32)).astype(BF16)
                delta = (dot(ones, hi, 1, 1) + dot(ones, mid, 1, 1)) + dot(ones, low, 1, 1)
                st_s[r, p, 0:1, 128 * s:128 * s + 128] = jnp.concatenate([delta[0:1], blank], 1)
            st_s[r, p, 1:2, :] = ls_v[r, p:p + 1, :]
        st_b[r, me] = st_s[r, me]
        for i in range(1, n_dev):
            p = peer(i)
            remote(st_s.at[r, p], st_b.at[r, me], st_send, st_recv.at[r], p)

        @pl.when(r == lax.max(2 * me - 3, 0))
        def _():
            send_keys()

    pltpu.make_async_copy(ls_n, ls_v, ls_sem).start()
    fetch(0)
    barrier = pltpu.get_barrier_semaphore()
    for i in range(1, n_dev):
        pl.semaphore_signal(barrier, inc=1, device_id=device(peer(i)), device_id_type=MESH)
    pl.semaphore_wait(barrier, rest)
    arrived(ls_v, ls_sem)

    @pl.loop(0, RING)
    def _(r):
        send_pair(r)

    @pl.loop(0, 2 * n_tiles)
    def _(i):
        dk_a[i] = jnp.zeros((head_dim, 128), F32)
        dv_a[i] = jnp.zeros((head_dim, 128), F32)

    q_t[1] = jnp.zeros(q_t.shape[1:], BF16)
    do_t[1] = jnp.zeros(do_t.shape[1:], BF16)
    dq_a[1] = jnp.zeros(dq_a.shape[1:], F32)
    p_c[...] = jnp.zeros(p_c.shape, BF16)
    d_c[...] = jnp.zeros(d_c.shape, BF16)

    def products(j, slot, tiles, old_slot, old_tile, masked=False):
        if masked:
            visible = (lax.broadcasted_iota(jnp.int32, (TILE, TILE), 0)
                       >= lax.broadcasted_iota(jnp.int32, (TILE, TILE), 1))
        old = [(p_c[h], d_c[h]) for h in range(group)]
        for t in tiles:
            new = []
            dv_sum = dk_sum = None
            for h in range(group):
                p_old, d_old = old[h]
                lanes = slice(h * TILE, (h + 1) * TILE)
                if t is not None:
                    s = dot(q_b[j, h], k_t[t], 1, 0)
                part = dot(do_t[old_slot, :, lanes], p_old, 1, 0)
                dv_sum = part if dv_sum is None else dv_sum + part
                if t is not None:
                    dp = dot(do_b[j, h], v_t[t], 1, 0)
                part = dot(q_t[old_slot, :, lanes], d_old, 1, 0)
                dk_sum = part if dk_sum is None else dk_sum + part
                dq_a[old_slot, h] += dot(k_t[old_tile], d_old, 1, 1)
                if t is not None:
                    p = jnp.exp2(s * (scale * LOG2E) - col[slot, :, 2 * h + 1:2 * h + 2])
                    if masked:
                        p = jnp.where(visible, p, 0.0)
                    ds = p * (dp - col[slot, :, 2 * h:2 * h + 1])
                    new.append((p.astype(BF16), ds.astype(BF16)))
            for acc, total in ((dv_a, dv_sum), (dk_a, dk_sum)):
                acc[2 * old_tile] += total[:, :128]
                acc[2 * old_tile + 1] += total[:, 128:]
            old, old_slot, old_tile = new, slot, t
        if old:
            for h in range(group):
                p_c[h], d_c[h] = old[h]

    def open_row(j, slot):
        pair, s = lax.div(j, 2), lax.rem(j, 2)

        @pl.when(s == 0)
        def _():
            segs = pl.ds(pl.multiple_of(j, 2), 2)
            for a, land in enumerate((q_b, do_b)):
                arrived(land.at[segs, :, pl.ds(0, rest * q_rows)], row_recv.at[a, pair])
            arrived(st_b.at[pair, pl.ds(0, rest)], st_recv.at[pair])

            @pl.when(pair + RING < n_pairs)
            def _():
                send_pair(pair + RING)

        owner = lax.div(j + 1, 4)

        @pl.when(((j == 0) | ((lax.rem(j, 4) == 3) & (j < n_segs - 1))) & (owner != me))
        def _():
            rows = pl.ds(pl.multiple_of(owner * k_rows, 32), k_rows)
            for a, land in enumerate((k_b, v_b)):
                arrived(land.at[rows], kv_recv.at[a, owner])

        def turn_keys(t):
            rows = pl.ds(pl.multiple_of(t * TILE, TILE), TILE)
            k_t[t] = k_b[rows, :].T
            v_t[t] = v_b[rows, :].T

        @pl.when(j == 0)
        def _():
            turn_keys(0)

        turn_keys(j + 1)
        q_t[slot] = q_b[j].reshape(group * TILE, head_dim).T
        do_t[slot] = do_b[j].reshape(group * TILE, head_dim).T
        dq_a[slot] = jnp.zeros((group, head_dim, TILE), F32)
        for b in range(n_dev):
            stats = st_b[pair, b, :, pl.ds(pl.multiple_of(s * 128, 128), 128)]
            turned = jnp.concatenate([stats, jnp.zeros((6, 128), F32)], 0).T
            for h in range(group):
                col[slot, b * q_rows:(b + 1) * q_rows, 2 * h:2 * h + 2] = turned[h * q_rows:(h + 1) * q_rows, 0:2]

    def close_row(j, slot):
        for h in range(group):
            q_b[j, h] = (dq_a[slot, h].T * scale).astype(BF16)
        pltpu.make_async_copy(q_b.at[j, :, my_rows], dq_o.at[j, me], out_recv.at[0]).start()
        for i in range(1, n_dev):
            p = peer(i)
            rows = pl.ds(pl.multiple_of(p * q_rows, q_rows), q_rows)
            remote(q_b.at[j, :, rows], dq_o.at[j, me], out_send.at[0], out_recv.at[0], p)

    def close_tile(t):
        for b in range(2):
            dk_a[2 * t + b] = dk_a[2 * t + b].T * scale
            dv_a[2 * t + b] = dv_a[2 * t + b].T

    def send_piece(r):
        owner = lax.div(r, pieces)
        block = lax.div(r, 4)
        rows = pl.ds(pl.multiple_of(lax.rem(r, 4) * PIECE, PIECE), PIECE)
        for n, src, dst in ((1, dk_a, dk_o), (2, dv_a, dv_o)):
            @pl.when(owner == me)
            def _():
                pltpu.make_async_copy(src.at[block, rows], dst.at[r - owner * pieces, me], out_recv.at[n]).start()

            @pl.when(owner != me)
            def _():
                remote(src.at[block, rows], dst.at[r - owner * pieces, me], out_send.at[n], out_recv.at[n], owner)

    def row(j, slot, old_slot, lo, close):
        n = j + 1 - lo

        @pl.loop(0, lax.div(n, WIDE))
        def _(c):
            t = lo + c * WIDE
            products(j, slot, [t + w for w in range(WIDE)],
                     jnp.where(c == 0, old_slot, slot), jnp.where(c == 0, j, t - 1))

        @pl.loop(j + 1 - lax.rem(n, WIDE), j + 1)
        def _(t):
            products(j, slot, [t], jnp.where(t == lo, old_slot, slot), jnp.where(t == lo, j, t - 1))

        close()
        products(j, slot, [j + 1], slot, j, masked=True)

    @pl.loop(0, first_late)
    def _(j):
        slot = lax.rem(j, 2)
        open_row(j, slot)

        def close():
            @pl.when(j > 0)
            def _():
                close_row(j - 1, 1 - slot)

        row(j, slot, 1 - slot, 0, close)

    @pl.loop(first_late, n_segs)
    def _(j):
        slot = j - first_late + 2
        open_row(j, slot)

        def close():
            @pl.when(j == first_late)
            def _():
                close_row(j - 1, 1)

        row(j, slot, slot - 1, late_tile, close)

    late_pieces = (n_tiles - late_tile) * (TILE // PIECE)
    share = late_pieces // n_cols
    wide_pieces = WIDE * TILE // PIECE

    def close_wide(c):
        @pl.loop(c * WIDE, c * WIDE + WIDE)
        def _(t):
            close_tile(t)

        @pl.loop(c * wide_pieces, (c + 1) * wide_pieces)
        def _(r):
            send_piece(r)

    @pl.loop(0, n_cols)
    def _(i):
        c = lax.rem(me + i, n_cols)
        done = lax.rem(me + i + n_cols - 1, n_cols)

        @pl.loop(first_late, n_segs)
        def _(j):
            slot = j - first_late + 2
            first = j == first_late
            products(j, slot, [c * WIDE + w for w in range(WIDE)],
                     jnp.where(first, late + 1, slot - 1),
                     jnp.where(first, jnp.where(i == 0, n_segs, done * WIDE + WIDE - 1), c * WIDE + WIDE - 1))

            @pl.when(first & (i == 0))
            def _():
                @pl.loop(late_tile, n_tiles)
                def _(t):
                    close_tile(t)

            @pl.when(first & (i > 0))
            def _():
                close_wide(done)

            @pl.when(first)
            def _():
                @pl.loop(0, share)
                def _(r):
                    send_piece(late_tile * (TILE // PIECE) + lax.rem(i * share + r + me * (late_pieces // n_dev),
                                                                      late_pieces))

            @pl.when((i == n_cols - 1) & jnp.logical_not(first))
            def _():
                close_row(j - 1, slot - 1)

    last = lax.rem(me + n_cols - 1, n_cols)
    products(0, 0, [None], late + 1, last * WIDE + WIDE - 1)
    close_row(n_segs - 1, late + 1)
    close_wide(last)

    @pl.loop(0, RING)
    def _(slot):
        for a in range(2):
            arrived(stg.at[slot, a, pl.ds(0, rest)], row_send.at[a, slot])

    for a in range(2):
        arrived(kv_s.at[a, pl.ds(0, rest)], kv_send.at[a])
    arrived(st_s.at[:, pl.ds(0, rest)], st_send)
    for n, ref in enumerate((dq_o, dk_o, dv_o)):
        arrived(ref.at[:, pl.ds(0, rest)], out_send.at[n])
        arrived(ref, out_recv.at[n])


def ungroup_kernel(dq_i, dk_i, dv_i, dq_o, dk_o, dv_o):
    @pl.when(pl.program_id(0) < pl.num_programs(0) - 1)
    def _():
        dq_o[...] = jnp.transpose(dq_i[0], (1, 0, 2))

    dk_o[...] = jnp.transpose(dk_i[0], (1, 0, 2))
    dv_o[...] = jnp.transpose(dv_i[0], (1, 0, 2))


def solution(mesh):
    outer, inner = mesh.shape["cp_outer"], mesh.shape["cp"]
    n_dev = outer * inner
    seq_spec = P(None, SEQ_AXES, "heads", None)
    stat_spec = P(None, SEQ_AXES, "heads")
    kv_spec = P(SEQ_AXES, "heads", None)

    def local_grads(q, k, v, o, do, lse):
        n_segs, q_rows, q_heads, head_dim = q.shape
        k_rows, kv_heads, _ = k.shape
        group = q_heads // kv_heads
        late = 8
        n_tiles = n_segs + 1
        n_pairs = n_segs // 2
        pieces = k_rows // PIECE
        keys = n_dev * k_rows

        def flat(x):
            return x.reshape(n_segs * q_rows, q_heads, head_dim)

        stats = (lse * LOG2E).reshape(n_pairs, 2, q_rows, kv_heads, group).transpose(0, 3, 1, 4, 2)
        stats = jnp.pad(stats.reshape(n_pairs, kv_heads, 2, group * q_rows),
                        ((0, 0), (0, 0), (0, 0), (0, 128 - group * q_rows)))
        stats = stats.reshape(n_pairs, kv_heads, 256)
        dims = (n_dev, inner, n_segs, group, q_rows, head_dim, k_rows, late)
        hbm = pl.BlockSpec(memory_space=pl.ANY)
        vmem = pltpu.VMEM
        row = vmem((n_segs, group, TILE, head_dim), BF16)
        key = vmem((keys, head_dim), BF16)
        key_t = vmem((n_tiles, head_dim, TILE), BF16)
        row_t = vmem((late + 2, head_dim, group * TILE), BF16)
        key_sum = vmem((2 * n_tiles, head_dim, 128), F32)
        stat = vmem((n_pairs, n_dev, 2, 256), F32)
        carried = vmem((group, TILE, TILE), BF16)
        dma = pltpu.SemaphoreType.DMA
        kv_out = jax.ShapeDtypeStruct((pieces, kv_heads, PIECE, head_dim), F32)
        dq, dk, dv = pl.pallas_call(
            functools.partial(attn_kernel, dims),
            out_shape=(jax.ShapeDtypeStruct((n_segs, kv_heads, group, q_rows, head_dim), BF16), kv_out, kv_out),
            in_specs=[hbm] * 6,
            out_specs=(hbm,) * 3,
            scratch_shapes=[
                vmem((2, 3, 2 * q_rows, q_heads, head_dim), BF16),
                vmem((2, 2, CHUNK, kv_heads, head_dim), BF16),
                vmem((n_pairs, kv_heads, 256), F32),
                vmem((RING, 2, kv_heads, 2, group, q_rows, head_dim), BF16),
                vmem((kv_heads, 2, group, q_rows, head_dim), BF16),
                vmem((2, kv_heads, k_rows, head_dim), BF16),
                stat, row, row, key, key, stat,
                key_t, key_t, row_t, row_t,
                vmem((late + 2, group, head_dim, TILE), F32),
                key_sum, key_sum,
                vmem((late + 2, TILE, 8), F32),
                carried, carried,
                dma((2, 3)), dma((2, 2)), dma, dma((2, RING)), dma((2,)), dma, dma((3,)),
                dma((2, n_pairs)), dma((2, n_dev)), dma((n_pairs,)), dma((3,))],
            compiler_params=pltpu.CompilerParams(
                collective_id=0, has_side_effects=True, vmem_limit_bytes=67043328),
            cost_estimate=pl.CostEstimate(flops=1680 * 5 * 2 * 256 * 256 * 128, bytes_accessed=64 << 20,
                                          transcendentals=1680 * 65536),
            name="attn_grads",
        )(flat(q), flat(do), flat(o), k, v, stats)

        last = n_segs - 1
        kv_in = pl.BlockSpec((1, kv_heads, PIECE, head_dim), lambda i: (i, 0, 0, 0))
        kv_back = pl.BlockSpec((PIECE, kv_heads, head_dim), lambda i: (i, 0, 0))
        dq, dk, dv = pl.pallas_call(
            ungroup_kernel,
            grid=(pieces,),
            out_shape=(jax.ShapeDtypeStruct((n_segs * q_rows, q_heads, head_dim), BF16),
                       jax.ShapeDtypeStruct((k_rows, kv_heads, head_dim), F32),
                       jax.ShapeDtypeStruct((k_rows, kv_heads, head_dim), F32)),
            in_specs=[pl.BlockSpec((1, q_heads, q_rows, head_dim), lambda i: (jnp.minimum(i, last), 0, 0, 0)),
                      kv_in, kv_in],
            out_specs=(pl.BlockSpec((q_rows, q_heads, head_dim), lambda i: (jnp.minimum(i, last), 0, 0)),
                       kv_back, kv_back),
            name="ungroup",
        )(dq.reshape(n_segs, q_heads, q_rows, head_dim), dk, dv)
        return dq.reshape(n_segs, q_rows, q_heads, head_dim), dk, dv

    return jax.shard_map(local_grads, mesh=mesh,
                         in_specs=(seq_spec, kv_spec, kv_spec, seq_spec, seq_spec, stat_spec),
                         out_specs=(seq_spec, kv_spec, kv_spec), check_vma=False)
```

time: 9560 us -> 443 us (0.05)
  matrix products: 4410 us -> 0 us
  waiting for transfers between devices: 2090 us -> 0 us
  blocking collectives: 1610 us -> 0 us
  local copies, waits for them, and re-layouts: 1090 us -> 1.16 us
  Pallas kernels: 0 us -> 432 us
  loops' own time: 185 us -> 0 us
    dot_general x1280 -> x0, matrix products: 4410 us -> none  [the longest x256 1330 us: block_grads(): jnp.einsum('hgqk,qhgd->khd', ds_low, q_four, preferred_element_type=jnp.f...]
    all_gather x192 -> x0, blocking collectives: 1610 us -> none  [the longest x128 1310 us: gather_all(): inner_part = lax.all_gather(local_part, 'cp', axis=0)]
    reduce_scatter x32 -> x0, waiting for transfers between devices: 1330 us -> none  [scatter_sum(): outer_part = lax.psum_scatter(grouped, 'cp_outer', scatter_dimension=0)]
    unnamed x160 -> x0, waiting for transfers between devices: 761 us -> none
    dynamic_slice x1280 -> x0, local copies, waits for them, and re-layouts: 608 us -> none  [local_grads(): lax.scan(source_step, (dk_acc, dv_acc), (q_all, do_all, lse_all, delta_al...]
    pallas_call x0 -> x2, Pallas kernels: none -> 432 us  [the longest x1 409 us: local_grads(): pl.pallas_call(functools.partial(attn_kernel, dims), out_shape=(jax.Shape...]
    dynamic_update_slice x256 -> x0, local copies, waits for them, and re-layouts: 255 us -> none  [local_grads(): lax.scan(source_step, (dk_acc, dv_acc), (q_all, do_all, lse_all, delta_al...]
    another operation x32 -> x0, loops' own time: 185 us -> none  [local_grads(): lax.scan(source_step, (dk_acc, dv_acc), (q_all, do_all, lse_all, delta_al...]
where the time goes in v2:
time: 443 us; the launch traced here: 435 us
  Pallas kernels  432 us (98%)
    pallas_call x1, Pallas kernels, local_grads(): pl.pallas_call(functools.partial(attn_kernel, dims), out_shape=(jax.Shape...  409 us
    pallas_call x1, Pallas kernels, local_grads(): pl.pallas_call(ungroup_kernel, grid=(pieces,), out_shape=(jax.ShapeDtypeS...  22.9 us

profile of v2, /device:TPU:1, one launch (start us, length us, event | category | flops | bytes accessed | tf_op | source)
XLA Modules:
  0.0 434.6 jit_solution(14165594579890596452)
XLA Ops:
  0.6 1.1 copy_multiply_fusion
  1.7 0.3 copy.10
  2.0 0.2 reshape.34
  2.2 0.7 pad_bitcast_fusion.ls_n
  2.9 408.8 %attn_grads.1 = (bf16[32,8,3,32,128]{4,3,2,1,0:T(8,128)(2,1)}, f32[33,8,32,128]{3,2,1,0:T(8,128)}, f32[33,8,32,128]{3,2,1,0:T(8,128)}) custom-call(bf16[1024,24,128]{2,1,0:T(8,128)(2,1)} %bitcast.14, bf16[1024,24,128]{2,1,0:T(8,128)(2,1)} %bitcast.15, bf16[1024,24,128]{2,1,0:T(8,128)(2,1)} %bitcast.16, bf16[1056,8,128]{2,1,0:T(8,128)(2,1)} %k_n.1, ...), custom_call_target="tpu_custom_call" | custom-call | flops 140928614400 | bytes 67108864 | tf_op jit(solution)/shard_map/attn_grads/pallas_call | solution.py:418
  411.7 22.9 %ungroup.1 = (bf16[1024,24,128]{2,1,0:T(8,128)(2,1)}, f32[1056,8,128]{2,1,0:T(8,128)}, f32[1056,8,128]{2,1,0:T(8,128)}) custom-call(bf16[32,24,32,128]{3,2,1,0:T(8,128)(2,1)} %bitcast.12, f32[33,8,32,128]{3,2,1,0:T(8,128)} %get-tuple-element.10.dk_i, f32[33,8,32,128]{3,2,1,0:T(8,128)} %get-tuple-element.11.dv_i), custom_call_target="tpu_custom_call" | custom-call | tf_op jit(solution)/shard_map/ungroup/pallas_call | solution.py:448

commit v3 on v2

v3 whole, which is shorter than its diff:
```python
import functools

import jax
import jax.numpy as jnp
from jax import lax
from jax.experimental import pallas as pl
from jax.experimental.pallas import tpu as pltpu
from jax.sharding import PartitionSpec as P

MESH = pl.DeviceIdType.MESH
SEQ_AXES = ("cp_outer", "cp")
BF16 = jnp.bfloat16
F32 = jnp.float32
LOG2E = 1.4426950408889634
TILE = 256
WIDE = 4
PIECE = 32
CHUNK = 96


def dot(a, b, ca, cb):
    return lax.dot_general(a, b, (((ca,), (cb,)), ((), ())), preferred_element_type=F32)


def attn_kernel(dims, q_n, do_n, o_n, k_n, v_n, ls_n, dq_o, dk_o, dv_o, box, mir_kv, mir_q, mir_k, mir_v,
                nat, nat_k, ls_v, stg, o_s, kv_s, st_s, qd_b, k_b, v_b, st_b,
                k_t, v_t, q_t, do_t, dq_a, dk_a, dv_a, col, p_c, d_c,
                nat_sem, natk_sem, ls_sem, box_own, box_send, box_recv, pair_send, pair_d2d,
                kv_send, kv_d2d, kv_mir, kv_mir_recv, st_send, dq_send, dq_d2d, dq_mir, dq_mir_recv,
                dkv_send, dkv_d2d, dkv_mir, dkv_mir_recv, row_recv, kv_recv, st_recv, out_recv):
    n_dev, inner, n_segs, group, q_rows, head_dim, k_rows, late = dims
    scale = head_dim ** -0.5
    outer_at, inner_at = lax.axis_index("cp_outer"), lax.axis_index("cp")
    me = outer_at * inner + inner_at
    core = lax.rem(inner_at, 2)
    mate = me + 1 - 2 * core
    n_pairs = n_segs // 2
    n_tiles = n_segs + 1
    first_late = n_segs - late
    late_tile = first_late
    n_cols = late_tile // WIDE
    pieces = k_rows // PIECE
    rest = n_dev - 1
    early_pairs = first_late // 2

    def chip_cores(flip_outer, flip_inner):
        y = 1 - outer_at if flip_outer else outer_at
        x = (inner - 2) - (inner_at - core) if flip_inner else inner_at - core
        return [y * inner + x + c for c in range(2)]

    along = chip_cores(False, True) + chip_cores(True, False)
    across = chip_cores(True, True)

    def sent_by_me(send_all):
        @pl.when(core == 0)
        def _():
            send_all(along)

        @pl.when(core == 1)
        def _():
            send_all(across)

    def rows_of(p):
        return pl.ds(pl.multiple_of(p * q_rows, q_rows), q_rows)

    def device(p):
        return (0, lax.div(p, inner), lax.rem(p, inner))

    def remote(src, dst, send_sem, recv_sem, p):
        pltpu.make_async_remote_copy(src_ref=src, dst_ref=dst, send_sem=send_sem, recv_sem=recv_sem,
                                     device_id=device(p), device_id_type=MESH).start()

    def arrived(ref, sem):
        pltpu.make_async_copy(ref, ref, sem).wait()

    def wait_sent(whole, half, sem):
        @pl.when(core == 0)
        def _():
            arrived(whole, sem)

        @pl.when(core == 1)
        def _():
            arrived(half, sem)

    def pair_at(k):
        return jnp.where(k < early_pairs, early_pairs - 1 - k, k)

    def fetch(k):
        r = pair_at(k)
        for a, src in enumerate((q_n, do_n, o_n)):
            pltpu.make_async_copy(src.at[pl.ds(r * 2 * q_rows, 2 * q_rows)], nat.at[lax.rem(k, 2), a],
                                  nat_sem.at[lax.rem(k, 2), a]).start()

    def fetch_keys(c):
        for a, src in enumerate((k_n, v_n)):
            pltpu.make_async_copy(src.at[pl.ds(c * CHUNK, CHUNK)], nat_k.at[lax.rem(c, 2), a],
                                  natk_sem.at[lax.rem(c, 2), a]).start()

    def send_keys(src, owner):
        dst = pl.ds(pl.multiple_of(owner * k_rows, 32), k_rows)

        def send_all(to):
            for p in to:
                for a, land in enumerate((k_b, v_b)):
                    remote(src.at[a, p], land.at[dst], kv_send.at[a], kv_recv.at[a], p)

        sent_by_me(send_all)

    def stage_keys():
        @pl.loop(0, k_rows // CHUNK)
        def _(c):
            buf = lax.rem(c, 2)
            rows = pl.ds(pl.multiple_of(c * CHUNK, CHUNK), CHUNK)
            dst = pl.ds(pl.multiple_of(me * k_rows + c * CHUNK, 32), CHUNK)
            for a in range(2):
                arrived(nat_k.at[buf, a], natk_sem.at[buf, a])

            @pl.when(c + 1 < k_rows // CHUNK)
            def _():
                fetch_keys(c + 1)

            for a, land in enumerate((k_b, v_b)):
                kv_s[a, :, rows] = jnp.transpose(nat_k[buf, a], (1, 0, 2))
                land[dst, :] = kv_s[a, me, rows]

        send_keys(kv_s, me)
        dst = pl.ds(pl.multiple_of(me * k_rows, 32), k_rows)
        for a, land in enumerate((k_b, v_b)):
            remote(kv_s.at[a, mate], land.at[dst], kv_d2d.at[a], kv_recv.at[a], mate)
            remote(kv_s.at[a], mir_kv.at[a], kv_mir.at[a], kv_mir_recv.at[a], mate)

    def forward_keys():
        for a in range(2):
            arrived(mir_kv.at[a], kv_mir_recv.at[a])
        send_keys(mir_kv, mate)

    def stage_pair(k):
        buf = lax.rem(k, 2)
        r = pair_at(k)
        for a in range(3):
            arrived(nat.at[buf, a], nat_sem.at[buf, a])

        @pl.when(k + 1 < n_pairs)
        def _():
            fetch(k + 1)

        for u in range(4):
            half = slice(16 * (u % 2), 16 * (u % 2) + 16)
            for a in range(3):
                block = jnp.transpose(nat[buf, a, 16 * u:16 * u + 16], (1, 0, 2)).reshape(n_dev, group, 16, head_dim)
                if a < 2:
                    stg[buf, :, u // 2, a, :, half] = block
                else:
                    o_s[:, u // 2, :, half] = block
        segs = pl.ds(2 * r, 2)
        for s in range(2):
            qd_b[2 * r + s, :, :, rows_of(me)] = stg[buf, me, s]
        pltpu.make_async_copy(stg.at[buf], box.at[core, k], box_own.at[buf]).start()
        remote(stg.at[buf], box.at[core, k], box_send.at[buf], box_recv.at[k], mate)
        remote(stg.at[buf, mate], qd_b.at[segs, :, :, rows_of(me)], pair_d2d.at[buf], row_recv.at[r], mate)

        ones = jnp.ones((8, head_dim), BF16)
        rows = group * q_rows
        blank = jnp.zeros((1, 128 - rows), F32)
        for p in range(n_dev):
            for s in range(2):
                prod = (stg[buf, p, s, 1].reshape(rows, head_dim).astype(F32)
                        * o_s[p, s].reshape(rows, head_dim).astype(F32))
                hi = prod.astype(BF16)
                prod = prod - hi.astype(F32)
                mid = prod.astype(BF16)
                low = (prod - mid.astype(F32)).astype(BF16)
                delta = (dot(ones, hi, 1, 1) + dot(ones, mid, 1, 1)) + dot(ones, low, 1, 1)
                st_s[r, p, 0:1, 128 * s:128 * s + 128] = jnp.concatenate([delta[0:1], blank], 1)
            st_s[r, p, 1:2, :] = ls_v[r, p:p + 1, :]
        st_b[r, me] = st_s[r, me]
        for p in along + across + [mate]:
            remote(st_s.at[r, p], st_b.at[r, me], st_send, st_recv.at[r], p)

    def ship_pair(k):
        buf = lax.rem(k, 2)
        r = pair_at(k)
        segs = pl.ds(2 * r, 2)
        arrived(stg.at[buf], box_own.at[buf])
        arrived(stg.at[buf], box_send.at[buf])
        arrived(stg.at[buf, 0], pair_d2d.at[buf])
        arrived(box.at[0, k], box_recv.at[k])

        def send_all(to):
            for src in range(2):
                for p in to:
                    remote(box.at[src, k, p], qd_b.at[segs, :, :, rows_of(me - core + src)], pair_send, row_recv.at[r], p)

        sent_by_me(send_all)

    pltpu.make_async_copy(ls_n, ls_v, ls_sem).start()
    fetch_keys(0)
    fetch(0)
    barrier = pltpu.get_barrier_semaphore()
    for p in along + across + [mate]:
        pl.semaphore_signal(barrier, inc=1, device_id=device(p), device_id_type=MESH)
    pl.semaphore_wait(barrier, rest)
    arrived(ls_v, ls_sem)
    stage_keys()

    @pl.loop(0, n_pairs)
    def _(k):
        stage_pair(k)

        @pl.when(k == 1)
        def _():
            forward_keys()

        @pl.when(k > 0)
        def _():
            ship_pair(k - 1)

    ship_pair(n_pairs - 1)

    @pl.loop(0, 2 * n_tiles)
    def _(i):
        dk_a[i] = jnp.zeros((head_dim, 128), F32)
        dv_a[i] = jnp.zeros((head_dim, 128), F32)

    q_t[0] = jnp.zeros(q_t.shape[1:], BF16)
    do_t[0] = jnp.zeros(do_t.shape[1:], BF16)
    dq_a[0] = jnp.zeros(dq_a.shape[1:], F32)
    p_c[...] = jnp.zeros(p_c.shape, BF16)
    d_c[...] = jnp.zeros(d_c.shape, BF16)

    for a, land in enumerate((k_b, v_b)):
        arrived(land.at[pl.ds(0, rest * k_rows)], kv_recv.at[a])

    @pl.loop(0, n_tiles)
    def _(t):
        rows = pl.ds(pl.multiple_of(t * TILE, TILE), TILE)
        k_t[t] = k_b[rows, :].T
        v_t[t] = v_b[rows, :].T

    def products(j, slot, tiles, old_slot, old_tile, masked=False):
        if masked:
            visible = (lax.broadcasted_iota(jnp.int32, (TILE, TILE), 0)
                       >= lax.broadcasted_iota(jnp.int32, (TILE, TILE), 1))
        old = [(p_c[h], d_c[h]) for h in range(group)]
        for t in tiles:
            new = []
            dv_sum = dk_sum = None
            for h in range(group):
                p_old, d_old = old[h]
                lanes = slice(h * TILE, (h + 1) * TILE)
                if t is not None:
                    s = dot(qd_b[j, 0, h], k_t[t], 1, 0)
                part = dot(do_t[old_slot, :, lanes], p_old, 1, 0)
                dv_sum = part if dv_sum is None else dv_sum + part
                if t is not None:
                    dp = dot(qd_b[j, 1, h], v_t[t], 1, 0)
                part = dot(q_t[old_slot, :, lanes], d_old, 1, 0)
                dk_sum = part if dk_sum is None else dk_sum + part
                dq_a[old_slot, h] += dot(k_t[old_tile], d_old, 1, 1)
                if t is not None:
                    p = jnp.exp2(s * (scale * LOG2E) - col[slot, :, 2 * h + 1:2 * h + 2])
                    if masked:
                        p = jnp.where(visible, p, 0.0)
                    ds = p * (dp - col[slot, :, 2 * h:2 * h + 1])
                    new.append((p.astype(BF16), ds.astype(BF16)))
            for acc, total in ((dv_a, dv_sum), (dk_a, dk_sum)):
                acc[2 * old_tile] += total[:, :128]
                acc[2 * old_tile + 1] += total[:, 128:]
            old, old_slot, old_tile = new, slot, t
        if old:
            for h in range(group):
                p_c[h], d_c[h] = old[h]

    def open_row(j, slot, first):
        pair, s = lax.div(j, 2), lax.rem(j, 2)

        @pl.when(s == first)
        def _():
            arrived(qd_b.at[pl.ds(2 * pair, 2), :, :, pl.ds(0, rest * q_rows)], row_recv.at[pair])
            arrived(st_b.at[pair, pl.ds(0, rest)], st_recv.at[pair])

        q_t[slot] = qd_b[j, 0].reshape(group * TILE, head_dim).T
        do_t[slot] = qd_b[j, 1].reshape(group * TILE, head_dim).T
        dq_a[slot] = jnp.zeros((group, head_dim, TILE), F32)
        for b in range(n_dev):
            stats = st_b[pair, b, :, pl.ds(pl.multiple_of(s * 128, 128), 128)]
            turned = jnp.concatenate([stats, jnp.zeros((6, 128), F32)], 0).T
            for h in range(group):
                col[slot, b * q_rows:(b + 1) * q_rows, 2 * h:2 * h + 2] = turned[h * q_rows:(h + 1) * q_rows, 0:2]

    def forward_row(j):
        arrived(mir_q.at[j], dq_mir_recv.at[j])

        def send_all(to):
            for p in to:
                remote(mir_q.at[j, :, rows_of(p)], dq_o.at[j, mate], dq_send, out_recv.at[0], p)

        sent_by_me(send_all)

    def close_row(j, slot, before):
        for h in range(group):
            qd_b[j, 0, h] = (dq_a[slot, h].T * scale).astype(BF16)
        remote(qd_b.at[j, 0], mir_q.at[j], dq_mir, dq_mir_recv.at[j], mate)
        remote(qd_b.at[j, 0, :, rows_of(mate)], dq_o.at[j, me], dq_d2d, out_recv.at[0], mate)
        pltpu.make_async_copy(qd_b.at[j, 0, :, rows_of(me)], dq_o.at[j, me], out_recv.at[0]).start()

        def send_all(to):
            for p in to:
                remote(qd_b.at[j, 0, :, rows_of(p)], dq_o.at[j, me], dq_send, out_recv.at[0], p)

        sent_by_me(send_all)

        @pl.when(before >= 0)
        def _():
            forward_row(before)

    flat_sums = [ref.reshape(2 * n_tiles * 128 // PIECE, PIECE, head_dim) for ref in (dk_a, dv_a)]
    flat_mirs = [ref.reshape(2 * n_tiles * 128 // PIECE, PIECE, head_dim) for ref in (mir_k, mir_v)]
    per_tile = TILE // PIECE

    def ship_tile(t, src_dev, mine):
        def part(p, n):
            owner = lax.div(p, pieces)
            src, dst = pl.ds(p, n), pl.ds(p - owner * pieces, n)
            on_chip = lax.div(owner, 2) == lax.div(me, 2)
            both = (lax.div(owner, inner) != outer_at) & (lax.div(lax.rem(owner, inner), 2) != lax.div(inner_at, 2))
            mine_to_send = jnp.where(both, 1, 0) == core
            for n_out, out in enumerate((dk_o, dv_o)):
                ref = (flat_sums if mine else flat_mirs)[n_out]
                if mine:
                    @pl.when(owner == me)
                    def _():
                        pltpu.make_async_copy(ref.at[src], out.at[dst, src_dev], out_recv.at[1 + n_out]).start()

                    @pl.when(owner == mate)
                    def _():
                        remote(ref.at[src], out.at[dst, src_dev], dkv_d2d.at[n_out], out_recv.at[1 + n_out], mate)

                @pl.when(jnp.logical_not(on_chip) & mine_to_send)
                def _():
                    remote(ref.at[src], out.at[dst, src_dev], dkv_send.at[n_out], out_recv.at[1 + n_out], owner)

        first = t * per_tile
        whole = lax.div(first, pieces) == lax.div(first + per_tile - 1, pieces)

        @pl.when(whole)
        def _():
            part(first, per_tile)

        @pl.when(jnp.logical_not(whole))
        def _():
            @pl.loop(0, per_tile)
            def _(i):
                part(first + i, 1)

    def close_tiles(lo, n, step, mir):
        @pl.loop(0, n)
        def _(w):
            t = lo + w * step
            for b in range(2):
                dk_a[2 * t + b] = dk_a[2 * t + b].T * scale
                dv_a[2 * t + b] = dv_a[2 * t + b].T
            for a, (src, dst) in enumerate(((dk_a, mir_k), (dv_a, mir_v))):
                remote(src.at[pl.ds(2 * t, 2)], dst.at[pl.ds(2 * t, 2)], dkv_mir.at[a], dkv_mir_recv.at[a, mir], mate)

    def row(j, slot, old_slot, old_tile, lo, close):
        n = j + 1 - lo

        @pl.loop(0, lax.div(n, WIDE))
        def _(c):
            t = lo + c * WIDE
            products(j, slot, [t + w for w in range(WIDE)],
                     jnp.where(c == 0, old_slot, slot), jnp.where(c == 0, old_tile, t - 1))

        @pl.loop(j + 1 - lax.rem(n, WIDE), j + 1)
        def _(t):
            products(j, slot, [t], jnp.where(t == lo, old_slot, slot), jnp.where(t == lo, old_tile, t - 1))

        close()
        products(j, slot, [j + 1], slot, j, masked=True)

    @pl.loop(0, first_late)
    def _(i):
        j = first_late - 1 - i
        slot = lax.rem(j, 2)
        open_row(j, slot, 1)

        def close():
            @pl.when(i > 0)
            def _():
                close_row(j + 1, 1 - slot, jnp.where(i > 1, j + 2, -1))

        row(j, slot, 1 - slot, j + 2, 0, close)

    @pl.loop(first_late, n_segs)
    def _(j):
        slot = j - first_late + 2
        first = j == first_late
        open_row(j, slot, 0)

        def close():
            @pl.when(first)
            def _():
                close_row(0, 0, 1)

        row(j, slot, jnp.where(first, 0, slot - 1), jnp.where(first, 1, j), late_tile, close)

    n_late = n_tiles - late_tile

    def column(dev, i):
        return lax.rem(dev + i, n_cols)

    def ship_column(dev, i, mine):
        @pl.loop(0, WIDE)
        def _(w):
            ship_tile(column(dev, i) + w * n_cols, dev, mine)

    def ship_late(dev, i, mine):
        @pl.loop(lax.div(i * n_late, n_cols), lax.div((i + 1) * n_late, n_cols))
        def _(n):
            ship_tile(late_tile + lax.rem(n + dev, n_late), dev, mine)

    def forward_column(i):
        for a, ref in enumerate((mir_k, mir_v)):
            arrived(ref.at[pl.ds(0, 2 * WIDE)], dkv_mir_recv.at[a, i])
        ship_column(mate, i, False)

    @pl.loop(0, n_cols)
    def _(i):
        c = column(me, i)

        @pl.loop(first_late, n_segs)
        def _(j):
            slot = j - first_late + 2
            first = j == first_late
            middle = j == first_late + late // 2
            last_tile = c + (WIDE - 1) * n_cols
            products(j, slot, [c + w * n_cols for w in range(WIDE)],
                     jnp.where(first, late + 1, slot - 1),
                     jnp.where(first, jnp.where(i == 0, n_segs, column(me, i + n_cols - 1) + (WIDE - 1) * n_cols),
                               last_tile))

            @pl.when(first & (i == 0))
            def _():
                close_tiles(late_tile, n_late, 1, n_cols)

            @pl.when(first & (i > 0))
            def _():
                close_tiles(column(me, i - 1), WIDE, n_cols, i - 1)
                ship_column(me, i - 1, True)

            @pl.when(first)
            def _():
                ship_late(me, i, True)

            @pl.when(middle & (i == 0))
            def _():
                for a, ref in enumerate((mir_k, mir_v)):
                    arrived(ref.at[pl.ds(0, 2 * n_late)], dkv_mir_recv.at[a, n_cols])

            @pl.when(middle & (i > 0))
            def _():
                forward_column(i - 1)

            @pl.when(middle)
            def _():
                ship_late(mate, i, False)

            @pl.when((i == n_cols - 1) & jnp.logical_not(first))
            def _():
                close_row(j - 1, slot - 1, jnp.where(j - 1 == first_late, 0, j - 2))

    products(0, 0, [None], late + 1, column(me, n_cols - 1) + (WIDE - 1) * n_cols)
    close_tiles(column(me, n_cols - 1), WIDE, n_cols, n_cols - 1)
    close_row(n_segs - 1, late + 1, n_segs - 2)
    ship_column(me, n_cols - 1, True)
    forward_row(n_segs - 1)
    forward_column(n_cols - 1)

    half = pl.ds(0, n_dev // 2)
    one = pl.ds(0, 1)
    wait_sent(box.at[0], box.at[0, :, half], pair_send)
    for a in range(2):
        wait_sent(kv_s.at[a], kv_s.at[a, half], kv_send.at[a])
        arrived(kv_s.at[a, one], kv_d2d.at[a])
        arrived(kv_s.at[a], kv_mir.at[a])
    arrived(st_s.at[:, pl.ds(0, rest)], st_send)
    wait_sent(dq_o, dq_o.at[:, half], dq_send)
    arrived(dq_o.at[:, one], dq_d2d)
    arrived(mir_q, dq_mir)
    for a, (out, ref) in enumerate(((dk_o, dk_a), (dv_o, dv_a))):
        wait_sent(out, out.at[:, half], dkv_send.at[a])
        arrived(out.at[:, one], dkv_d2d.at[a])
        arrived(ref, dkv_mir.at[a])
    for n, ref in enumerate((dq_o, dk_o, dv_o)):
        arrived(ref, out_recv.at[n])


def ungroup_kernel(n_q, dq_i, dk_i, dv_i, dq_o, dk_o, dv_o):
    @pl.when(pl.program_id(0) < n_q)
    def _():
        rows = dq_i.shape[2]
        for i in range(dq_i.shape[0]):
            dq_o[i * rows:(i + 1) * rows] = jnp.transpose(dq_i[i], (1, 0, 2))

    rows = dk_i.shape[2]
    for i in range(dk_i.shape[0]):
        dk_o[i * rows:(i + 1) * rows] = jnp.transpose(dk_i[i], (1, 0, 2))
        dv_o[i * rows:(i + 1) * rows] = jnp.transpose(dv_i[i], (1, 0, 2))


def solution(mesh):
    outer, inner = mesh.shape["cp_outer"], mesh.shape["cp"]
    n_dev = outer * inner
    seq_spec = P(None, SEQ_AXES, "heads", None)
    stat_spec = P(None, SEQ_AXES, "heads")
    kv_spec = P(SEQ_AXES, "heads", None)

    def local_grads(q, k, v, o, do, lse):
        n_segs, q_rows, q_heads, head_dim = q.shape
        k_rows, kv_heads, _ = k.shape
        group = q_heads // kv_heads
        late = 8
        n_tiles = n_segs + 1
        n_pairs = n_segs // 2
        pieces = k_rows // PIECE
        keys = n_dev * k_rows

        def flat(x):
            return x.reshape(n_segs * q_rows, q_heads, head_dim)

        stats = (lse * LOG2E).reshape(n_pairs, 2, q_rows, kv_heads, group).transpose(0, 3, 1, 4, 2)
        stats = jnp.pad(stats.reshape(n_pairs, kv_heads, 2, group * q_rows),
                        ((0, 0), (0, 0), (0, 0), (0, 128 - group * q_rows)))
        stats = stats.reshape(n_pairs, kv_heads, 256)
        dims = (n_dev, inner, n_segs, group, q_rows, head_dim, k_rows, late)
        hbm = pl.BlockSpec(memory_space=pl.ANY)
        vmem = pltpu.VMEM
        key = vmem((keys, head_dim), BF16)
        key_t = vmem((n_tiles, head_dim, TILE), BF16)
        row_t = vmem((late + 2, head_dim, group * TILE), BF16)
        key_sum = vmem((2 * n_tiles, head_dim, 128), F32)
        stat = vmem((n_pairs, n_dev, 2, 256), F32)
        carried = vmem((group, TILE, TILE), BF16)
        dma = pltpu.SemaphoreType.DMA
        n_cols = (n_segs - late) // WIDE
        kv_out = jax.ShapeDtypeStruct((pieces, kv_heads, PIECE, head_dim), F32)
        sums = jax.ShapeDtypeStruct((2 * n_tiles, 128, head_dim), F32)
        pair = (kv_heads, 2, 2, group, q_rows, head_dim)
        dq, dk, dv = pl.pallas_call(
            functools.partial(attn_kernel, dims),
            out_shape=(jax.ShapeDtypeStruct((n_segs, kv_heads, group, q_rows, head_dim), BF16), kv_out, kv_out,
                       jax.ShapeDtypeStruct((2, n_pairs) + pair, BF16),
                       jax.ShapeDtypeStruct((2, kv_heads, k_rows, head_dim), BF16),
                       jax.ShapeDtypeStruct((n_segs, group, TILE, head_dim), BF16), sums, sums),
            in_specs=[hbm] * 6,
            out_specs=(hbm,) * 8,
            scratch_shapes=[
                vmem((2, 3, 2 * q_rows, q_heads, head_dim), BF16),
                vmem((2, 2, CHUNK, kv_heads, head_dim), BF16),
                vmem((n_pairs, kv_heads, 256), F32),
                vmem((2,) + pair, BF16),
                vmem((kv_heads, 2, group, q_rows, head_dim), BF16),
                vmem((2, kv_heads, k_rows, head_dim), BF16),
                stat, vmem((n_segs, 2, group, TILE, head_dim), BF16), key, key, stat,
                key_t, key_t, row_t, row_t,
                vmem((late + 2, group, head_dim, TILE), F32),
                key_sum, key_sum,
                vmem((late + 2, TILE, 8), F32),
                carried, carried,
                dma((2, 3)), dma((2, 2)), dma, dma((2,)), dma((2,)), dma((n_pairs,)), dma, dma((2,)),
                dma((2,)), dma((2,)), dma((2,)), dma((2,)), dma, dma, dma, dma, dma((n_segs,)),
                dma((2,)), dma((2,)), dma((2,)), dma((2, n_cols + 1)), dma((n_pairs,)), dma((2,)), dma((n_pairs,)),
                dma((3,))],
            compiler_params=pltpu.CompilerParams(
                collective_id=0, has_side_effects=True, vmem_limit_bytes=67043328),
            cost_estimate=pl.CostEstimate(flops=1680 * 5 * 2 * 256 * 256 * 128, bytes_accessed=64 << 20,
                                          transcendentals=1680 * 65536),
            name="attn_grads",
        )(flat(q), flat(do), flat(o), k, v, stats)[:3]

        q_step, k_step = 4, 3
        n_q = n_segs // q_step
        kv_in = pl.BlockSpec((k_step, kv_heads, PIECE, head_dim), lambda i: (i, 0, 0, 0))
        kv_back = pl.BlockSpec((k_step * PIECE, kv_heads, head_dim), lambda i: (i, 0, 0))
        dq, dk, dv = pl.pallas_call(
            functools.partial(ungroup_kernel, n_q),
            grid=(pieces // k_step,),
            out_shape=(jax.ShapeDtypeStruct((n_segs * q_rows, q_heads, head_dim), BF16),
                       jax.ShapeDtypeStruct((k_rows, kv_heads, head_dim), F32),
                       jax.ShapeDtypeStruct((k_rows, kv_heads, head_dim), F32)),
            in_specs=[pl.BlockSpec((q_step, q_heads, q_rows, head_dim), lambda i: (jnp.minimum(i, n_q - 1), 0, 0, 0)),
                      kv_in, kv_in],
            out_specs=(pl.BlockSpec((q_step * q_rows, q_heads, head_dim), lambda i: (jnp.minimum(i, n_q - 1), 0, 0)),
                       kv_back, kv_back),
            name="ungroup",
        )(dq.reshape(n_segs, q_heads, q_rows, head_dim), dk, dv)
        return dq.reshape(n_segs, q_rows, q_heads, head_dim), dk, dv

    return jax.shard_map(local_grads, mesh=mesh,
                         in_specs=(seq_spec, kv_spec, kv_spec, seq_spec, seq_spec, stat_spec),
                         out_specs=(seq_spec, kv_spec, kv_spec), check_vma=False)
```

time: 443 us -> 414 us (0.935); the launches traced: 435 us -> 412 us
  Pallas kernels: 432 us -> 409 us
    pallas_call x1, Pallas kernels: 409 us -> 395 us  [local_grads(): pl.pallas_call(functools.partial(attn_kernel, dims), out_shape=(jax.Shape...]
    pallas_call x1, Pallas kernels: 22.9 us -> 14.6 us  [local_grads(): pl.pallas_call(functools.partial(ungroup_kernel, n_q), grid=(pieces // k_...]
where the time goes in v3:
time: 414 us; the launch traced here: 412 us
  Pallas kernels  409 us (99%)
    pallas_call x1, Pallas kernels, local_grads(): pl.pallas_call(functools.partial(attn_kernel, dims), out_shape=(jax.Shape...  395 us
    pallas_call x1, Pallas kernels, local_grads(): pl.pallas_call(functools.partial(ungroup_kernel, n_q), grid=(pieces // k_...  14.6 us

profile of v3, /device:TPU:1, one launch (start us, length us, event | category | flops | bytes accessed | tf_op | source)
XLA Modules:
  0.0 412.2 jit_solution(17125005195568103428)
XLA Ops:
  0.6 1.1 copy_multiply_fusion
  1.7 0.3 copy.10
  2.0 0.2 reshape.34
  2.2 0.7 pad_bitcast_fusion.ls_n
  2.9 394.6 %attn_grads.1 = (bf16[32,8,3,32,128]{4,3,2,1,0:T(8,128)(2,1)}, f32[33,8,32,128]{3,2,1,0:T(8,128)}, f32[33,8,32,128]{3,2,1,0:T(8,128)}, bf16[2,16,8,2,2,3,32,128]...) custom-call(bf16[1024,24,128]{2,1,0:T(8,128)(2,1)} %bitcast.14, ...), custom_call_target="tpu_custom_call" | custom-call | flops 140928614400 | bytes 67108864 | tf_op jit(solution)/shard_map/attn_grads/pallas_call | solution.py:550
  397.5 14.6 %ungroup.1 = (bf16[1024,24,128]{2,1,0:T(8,128)(2,1)}, f32[1056,8,128]{2,1,0:T(8,128)}, f32[1056,8,128]{2,1,0:T(8,128)}) custom-call(bf16[32,24,32,128]{3,2,1,0:T(8,128)(2,1)} %bitcast.12, f32[33,8,32,128]{3,2,1,0:T(8,128)} %get-tuple-element.10.dk_i, f32[33,8,32,128]{3,2,1,0:T(8,128)} %get-tuple-element.11.dv_i), custom_call_target="tpu_custom_call" | custom-call | tf_op jit(solution)/shard_map/ungroup/pallas_call | solution.py:586

commit v4 on v3

--- a/solution.py
+++ b/solution.py
@@ -13,7 +13,9 @@
 F32 = jnp.float32
 LOG2E = 1.4426950408889634
 TILE = 256
-WIDE = 4
+WIDE = 8
+HALF = 4
+ORDER = "SVPKSQPVSKPQVKQ"
 PIECE = 32
 CHUNK = 96
 
@@ -24,7 +26,7 @@
 
 def attn_kernel(dims, q_n, do_n, o_n, k_n, v_n, ls_n, dq_o, dk_o, dv_o, box, mir_kv, mir_q, mir_k, mir_v,
                 nat, nat_k, ls_v, stg, o_s, kv_s, st_s, qd_b, k_b, v_b, st_b,
-                k_t, v_t, q_t, do_t, dq_a, dk_a, dv_a, col, p_c, d_c,
+                k_t, v_t, q_t, do_t, dq_a, dk_a, dv_a, aug, aug_k, p_c, d_c, turn,
                 nat_sem, natk_sem, ls_sem, box_own, box_send, box_recv, pair_send, pair_d2d,
                 kv_send, kv_d2d, kv_mir, kv_mir_recv, st_send, dq_send, dq_d2d, dq_mir, dq_mir_recv,
                 dkv_send, dkv_d2d, dkv_mir, dkv_mir_recv, row_recv, kv_recv, st_recv, out_recv):
@@ -38,7 +40,7 @@
     n_tiles = n_segs + 1
     first_late = n_segs - late
     late_tile = first_late
-    n_cols = late_tile // WIDE
+    n_cols = late_tile // HALF
     pieces = k_rows // PIECE
     rest = n_dev - 1
     early_pairs = first_late // 2
@@ -96,18 +98,19 @@
             pltpu.make_async_copy(src.at[pl.ds(c * CHUNK, CHUNK)], nat_k.at[lax.rem(c, 2), a],
                                   natk_sem.at[lax.rem(c, 2), a]).start()
 
-    def send_keys(src, owner):
-        dst = pl.ds(pl.multiple_of(owner * k_rows, 32), k_rows)
+    def send_keys(src, owner, lo, n):
+        rows = pl.ds(lo, n)
+        dst = pl.ds(pl.multiple_of(owner * k_rows + lo, 32), n)
 
         def send_all(to):
             for p in to:
                 for a, land in enumerate((k_b, v_b)):
-                    remote(src.at[a, p], land.at[dst], kv_send.at[a], kv_recv.at[a], p)
+                    remote(src.at[a, p, rows], land.at[dst], kv_send.at[a], kv_recv.at[a], p)
 
         sent_by_me(send_all)
 
-    def stage_keys():
-        @pl.loop(0, k_rows // CHUNK)
+    def stage_keys(first, n):
+        @pl.loop(first, first + n)
         def _(c):
             buf = lax.rem(c, 2)
             rows = pl.ds(pl.multiple_of(c * CHUNK, CHUNK), CHUNK)
@@ -123,16 +126,18 @@
                 kv_s[a, :, rows] = jnp.transpose(nat_k[buf, a], (1, 0, 2))
                 land[dst, :] = kv_s[a, me, rows]
 
-        send_keys(kv_s, me)
-        dst = pl.ds(pl.multiple_of(me * k_rows, 32), k_rows)
+        lo, rows = first * CHUNK, n * CHUNK
+        send_keys(kv_s, me, lo, rows)
+        src = pl.ds(lo, rows)
+        dst = pl.ds(pl.multiple_of(me * k_rows + lo, 32), rows)
         for a, land in enumerate((k_b, v_b)):
-            remote(kv_s.at[a, mate], land.at[dst], kv_d2d.at[a], kv_recv.at[a], mate)
-            remote(kv_s.at[a], mir_kv.at[a], kv_mir.at[a], kv_mir_recv.at[a], mate)
+            remote(kv_s.at[a, mate, src], land.at[dst], kv_d2d.at[a], kv_recv.at[a], mate)
+            remote(kv_s.at[a, :, src], mir_kv.at[a, :, src], kv_mir.at[a], kv_mir_recv.at[a], mate)
 
     def forward_keys():
         for a in range(2):
             arrived(mir_kv.at[a], kv_mir_recv.at[a])
-        send_keys(mir_kv, mate)
+        send_keys(mir_kv, mate, 0, k_rows)
 
     def stage_pair(k):
         buf = lax.rem(k, 2)
@@ -171,8 +176,9 @@
                 mid = prod.astype(BF16)
                 low = (prod - mid.astype(F32)).astype(BF16)
                 delta = (dot(ones, hi, 1, 1) + dot(ones, mid, 1, 1)) + dot(ones, low, 1, 1)
+                lse = [ls_v[2 * r + s, p * group + h:p * group + h + 1, :] for h in range(group)]
                 st_s[r, p, 0:1, 128 * s:128 * s + 128] = jnp.concatenate([delta[0:1], blank], 1)
-            st_s[r, p, 1:2, :] = ls_v[r, p:p + 1, :]
+                st_s[r, p, 1:2, 128 * s:128 * s + 128] = jnp.concatenate(lse + [blank], 1) * (1 / scale)
         st_b[r, me] = st_s[r, me]
         for p in along + across + [mate]:
             remote(st_s.at[r, p], st_b.at[r, me], st_send, st_recv.at[r], p)
@@ -201,7 +207,9 @@
         pl.semaphore_signal(barrier, inc=1, device_id=device(p), device_id_type=MESH)
     pl.semaphore_wait(barrier, rest)
     arrived(ls_v, ls_sem)
-    stage_keys()
+    chunks = k_rows // CHUNK
+    stage_keys(0, chunks // 2)
+    stage_keys(chunks // 2, chunks - chunks // 2)
 
     @pl.loop(0, n_pairs)
     def _(k):
@@ -227,6 +235,11 @@
     dq_a[0] = jnp.zeros(dq_a.shape[1:], F32)
     p_c[...] = jnp.zeros(p_c.shape, BF16)
     d_c[...] = jnp.zeros(d_c.shape, BF16)
+    turn[1] = jnp.zeros(turn.shape[1:], BF16)
+    aug[...] = jnp.zeros(aug.shape, BF16)
+    place = lax.broadcasted_iota(jnp.int32, (head_dim, TILE), 0)
+    for a in range(2):
+        aug_k[a] = jnp.where((place < 6) & (lax.rem(place, 2) == 1 - a), -1.0, 0.0).astype(BF16)
 
     for a, land in enumerate((k_b, v_b)):
         arrived(land.at[pl.ds(0, rest * k_rows)], kv_recv.at[a])
@@ -237,44 +250,58 @@
         k_t[t] = k_b[rows, :].T
         v_t[t] = v_b[rows, :].T
 
-    def products(j, slot, tiles, old_slot, old_tile, masked=False):
-        if masked:
-            visible = (lax.broadcasted_iota(jnp.int32, (TILE, TILE), 0)
-                       >= lax.broadcasted_iota(jnp.int32, (TILE, TILE), 1))
+    def products(items, old_slot, old_tile, masked=False):
+        n = len(items)
         old = [(p_c[h], d_c[h]) for h in range(group)]
-        for t in tiles:
-            new = []
-            dv_sum = dk_sum = None
-            for h in range(group):
-                p_old, d_old = old[h]
-                lanes = slice(h * TILE, (h + 1) * TILE)
-                if t is not None:
-                    s = dot(qd_b[j, 0, h], k_t[t], 1, 0)
-                part = dot(do_t[old_slot, :, lanes], p_old, 1, 0)
-                dv_sum = part if dv_sum is None else dv_sum + part
-                if t is not None:
-                    dp = dot(qd_b[j, 1, h], v_t[t], 1, 0)
-                part = dot(q_t[old_slot, :, lanes], d_old, 1, 0)
-                dk_sum = part if dk_sum is None else dk_sum + part
-                dq_a[old_slot, h] += dot(k_t[old_tile], d_old, 1, 1)
-                if t is not None:
-                    p = jnp.exp2(s * (scale * LOG2E) - col[slot, :, 2 * h + 1:2 * h + 2])
-                    if masked:
-                        p = jnp.where(visible, p, 0.0)
-                    ds = p * (dp - col[slot, :, 2 * h:2 * h + 1])
-                    new.append((p.astype(BF16), ds.astype(BF16)))
-            for acc, total in ((dv_a, dv_sum), (dk_a, dk_sum)):
+        old_turn = 1
+        for w, item in enumerate(items):
+            new = [None] * group
+            new_turn = 1 if w == n - 1 else 0 if (n - 1 - w) % 2 else 2
+            sums = {"V": None, "K": None}
+            raw = {"S": [None] * group, "P": [None] * group}
+            count = dict.fromkeys("SPVKQ", 0)
+            kept = [turn[old_turn, h] for h in range(group)] if new_turn == old_turn else None
+            for step in ORDER:
+                h = count[step]
+                count[step] += 1
+                if step in "SP":
+                    if item is None:
+                        continue
+                    j, slot, t = item
+                    a = "SP".index(step)
+                    rows = jnp.concatenate([qd_b[j, a, h], aug[slot, h]], 1)
+                    cols = jnp.concatenate([(k_t, v_t)[a][t], aug_k[a]], 0)
+                    raw[step][h] = dot(rows, cols, 1, 0)
+                    if raw["S"][h] is not None and raw["P"][h] is not None:
+                        p = jnp.exp2(raw["S"][h] * (scale * LOG2E))
+                        if masked and w == n - 1:
+                            visible = (lax.broadcasted_iota(jnp.int32, (TILE, TILE), 0)
+                                       >= lax.broadcasted_iota(jnp.int32, (TILE, TILE), 1))
+                            p = jnp.where(visible, p, 0.0)
+                        ds = (p * raw["P"][h]).astype(BF16)
+                        new[h] = (p.astype(BF16), ds)
+                        turn[new_turn, h] = ds.T
+                elif step == "Q":
+                    right = turn[old_turn, h] if kept is None else kept[h]
+                    dq_a[old_slot, h] += dot(k_t[old_tile], right, 1, 0)
+                else:
+                    lanes = slice(h * TILE, (h + 1) * TILE)
+                    left = (do_t if step == "V" else q_t)[old_slot, :, lanes]
+                    part = dot(left, old[h]["VK".index(step)], 1, 0)
+                    sums[step] = part if sums[step] is None else sums[step] + part
+            for acc, total in ((dv_a, sums["V"]), (dk_a, sums["K"])):
                 acc[2 * old_tile] += total[:, :128]
                 acc[2 * old_tile + 1] += total[:, 128:]
-            old, old_slot, old_tile = new, slot, t
-        if old:
-            for h in range(group):
-                p_c[h], d_c[h] = old[h]
-
-    def open_row(j, slot, first):
+            if item is None:
+                return
+            old, old_turn, old_slot, old_tile = new, new_turn, slot, t
+        for h in range(group):
+            p_c[h], d_c[h] = old[h]
+
+    def open_row(j, slot, opens_pair):
         pair, s = lax.div(j, 2), lax.rem(j, 2)
 
-        @pl.when(s == first)
+        @pl.when(opens_pair)
         def _():
             arrived(qd_b.at[pl.ds(2 * pair, 2), :, :, pl.ds(0, rest * q_rows)], row_recv.at[pair])
             arrived(st_b.at[pair, pl.ds(0, rest)], st_recv.at[pair])
@@ -284,9 +311,11 @@
         dq_a[slot] = jnp.zeros((group, head_dim, TILE), F32)
         for b in range(n_dev):
             stats = st_b[pair, b, :, pl.ds(pl.multiple_of(s * 128, 128), 128)]
-            turned = jnp.concatenate([stats, jnp.zeros((6, 128), F32)], 0).T
+            hi = stats.astype(BF16).astype(F32)
+            mid = (stats - hi).astype(BF16).astype(F32)
+            parts = jnp.concatenate([hi, mid, (stats - hi) - mid, jnp.zeros((2, 128), F32)], 0).T.astype(BF16)
             for h in range(group):
-                col[slot, b * q_rows:(b + 1) * q_rows, 2 * h:2 * h + 2] = turned[h * q_rows:(h + 1) * q_rows, 0:2]
+                aug[slot, h, b * q_rows:(b + 1) * q_rows, 0:8] = parts[h * q_rows:(h + 1) * q_rows]
 
     def forward_row(j):
         arrived(mir_q.at[j], dq_mir_recv.at[j])
@@ -363,47 +392,43 @@
             for a, (src, dst) in enumerate(((dk_a, mir_k), (dv_a, mir_v))):
                 remote(src.at[pl.ds(2 * t, 2)], dst.at[pl.ds(2 * t, 2)], dkv_mir.at[a], dkv_mir_recv.at[a, mir], mate)
 
-    def row(j, slot, old_slot, old_tile, lo, close):
+    @pl.loop(0, n_segs)
+    def _(i):
+        early = i < first_late
+        j = jnp.where(early, first_late - 1 - i, i)
+        slot = jnp.where(early, lax.rem(j, 2), i - first_late + 2)
+        lo = jnp.where(early, 0, late_tile)
+        before = jnp.where(early, j + 1, jnp.where(i == first_late, 0, j - 1))
+        old_slot = jnp.where(early, 1 - slot, jnp.where(i == first_late, 0, slot - 1))
+        open_row(j, slot, lax.rem(i, 2) == 0)
         n = j + 1 - lo
+
+        def tiles(t, n):
+            return [(j, slot, t + w) for w in range(n)]
+
+        def after(t):
+            return jnp.where(t == lo, old_slot, slot), jnp.where(t == lo, before + 1, t - 1)
+
+        wide_end = lo + lax.div(n, WIDE) * WIDE
+        half_end = lo + lax.div(n, HALF) * HALF
 
         @pl.loop(0, lax.div(n, WIDE))
         def _(c):
             t = lo + c * WIDE
-            products(j, slot, [t + w for w in range(WIDE)],
-                     jnp.where(c == 0, old_slot, slot), jnp.where(c == 0, old_tile, t - 1))
-
-        @pl.loop(j + 1 - lax.rem(n, WIDE), j + 1)
-        def _(t):
-            products(j, slot, [t], jnp.where(t == lo, old_slot, slot), jnp.where(t == lo, old_tile, t - 1))
-
-        close()
-        products(j, slot, [j + 1], slot, j, masked=True)
-
-    @pl.loop(0, first_late)
-    def _(i):
-        j = first_late - 1 - i
-        slot = lax.rem(j, 2)
-        open_row(j, slot, 1)
-
-        def close():
-            @pl.when(i > 0)
-            def _():
-                close_row(j + 1, 1 - slot, jnp.where(i > 1, j + 2, -1))
-
-        row(j, slot, 1 - slot, j + 2, 0, close)
-
-    @pl.loop(first_late, n_segs)
-    def _(j):
-        slot = j - first_late + 2
-        first = j == first_late
-        open_row(j, slot, 0)
-
-        def close():
-            @pl.when(first)
-            def _():
-                close_row(0, 0, 1)
-
-        row(j, slot, jnp.where(first, 0, slot - 1), jnp.where(first, 1, j), late_tile, close)
+            products(tiles(t, WIDE), *after(t))
+
+        @pl.when(half_end > wide_end)
+        def _():
+            products(tiles(wide_end, HALF), *after(wide_end))
+
+        for r in range(HALF):
+            @pl.when(lax.rem(n, HALF) == r)
+            def _():
+                products(tiles(half_end, r + 1), *after(half_end), masked=True)
+
+        @pl.when((i > 0) & (i <= first_late))
+        def _():
+            close_row(before, old_slot, jnp.where(i > 1, before + 1, -1))
 
     n_late = n_tiles - late_tile
 
@@ -411,7 +436,7 @@
         return lax.rem(dev + i, n_cols)
 
     def ship_column(dev, i, mine):
-        @pl.loop(0, WIDE)
+        @pl.loop(0, HALF)
         def _(w):
             ship_tile(column(dev, i) + w * n_cols, dev, mine)
 
@@ -422,22 +447,23 @@
 
     def forward_column(i):
         for a, ref in enumerate((mir_k, mir_v)):
-            arrived(ref.at[pl.ds(0, 2 * WIDE)], dkv_mir_recv.at[a, i])
+            arrived(ref.at[pl.ds(0, 2 * HALF)], dkv_mir_recv.at[a, i])
         ship_column(mate, i, False)
 
     @pl.loop(0, n_cols)
     def _(i):
         c = column(me, i)
 
-        @pl.loop(first_late, n_segs)
-        def _(j):
-            slot = j - first_late + 2
-            first = j == first_late
-            middle = j == first_late + late // 2
-            last_tile = c + (WIDE - 1) * n_cols
-            products(j, slot, [c + w * n_cols for w in range(WIDE)],
+        @pl.loop(0, late // 2)
+        def _(pair):
+            j = first_late + 2 * pair
+            slot = 2 * pair + 2
+            first = pair == 0
+            middle = pair == late // 4
+            last_tile = c + (HALF - 1) * n_cols
+            products([(j + u, slot + u, c + w * n_cols) for u in range(2) for w in range(HALF)],
                      jnp.where(first, late + 1, slot - 1),
-                     jnp.where(first, jnp.where(i == 0, n_segs, column(me, i + n_cols - 1) + (WIDE - 1) * n_cols),
+                     jnp.where(first, jnp.where(i == 0, n_segs, column(me, i + n_cols - 1) + (HALF - 1) * n_cols),
                                last_tile))
 
             @pl.when(first & (i == 0))
@@ -446,7 +472,7 @@
 
             @pl.when(first & (i > 0))
             def _():
-                close_tiles(column(me, i - 1), WIDE, n_cols, i - 1)
+                close_tiles(column(me, i - 1), HALF, n_cols, i - 1)
                 ship_column(me, i - 1, True)
 
             @pl.when(first)
@@ -466,12 +492,16 @@
             def _():
                 ship_late(mate, i, False)
 
-            @pl.when((i == n_cols - 1) & jnp.logical_not(first))
-            def _():
-                close_row(j - 1, slot - 1, jnp.where(j - 1 == first_late, 0, j - 2))
-
-    products(0, 0, [None], late + 1, column(me, n_cols - 1) + (WIDE - 1) * n_cols)
-    close_tiles(column(me, n_cols - 1), WIDE, n_cols, n_cols - 1)
+            @pl.when(i == n_cols - 1)
+            def _():
+                @pl.when(jnp.logical_not(first))
+                def _():
+                    close_row(j - 1, slot - 1, j - 2)
+
+                close_row(j, slot, jnp.where(first, 0, j - 1))
+
+    products([None], late + 1, column(me, n_cols - 1) + (HALF - 1) * n_cols)
+    close_tiles(column(me, n_cols - 1), HALF, n_cols, n_cols - 1)
     close_row(n_segs - 1, late + 1, n_segs - 2)
     ship_column(me, n_cols - 1, True)
     forward_row(n_segs - 1)
@@ -496,17 +526,38 @@
         arrived(ref, out_recv.at[n])
 
 
-def ungroup_kernel(n_q, dq_i, dk_i, dv_i, dq_o, dk_o, dv_o):
-    @pl.when(pl.program_id(0) < n_q)
-    def _():
-        rows = dq_i.shape[2]
-        for i in range(dq_i.shape[0]):
-            dq_o[i * rows:(i + 1) * rows] = jnp.transpose(dq_i[i], (1, 0, 2))
-
-    rows = dk_i.shape[2]
-    for i in range(dk_i.shape[0]):
-        dk_o[i * rows:(i + 1) * rows] = jnp.transpose(dk_i[i], (1, 0, 2))
-        dv_o[i * rows:(i + 1) * rows] = jnp.transpose(dv_i[i], (1, 0, 2))
+def ungroup_kernel(q_step, k_step, dq_i, dk_i, dv_i, dq_o, dk_o, dv_o, q_in, k_in, v_in, q_out, k_out, v_out,
+                   q_sem, k_sem, v_sem, q_done, k_done, v_done):
+    groups = ((dq_i, q_in, q_out, dq_o, q_step, q_sem, q_done), (dk_i, k_in, k_out, dk_o, k_step, k_sem, k_done),
+              (dv_i, v_in, v_out, dv_o, k_step, v_sem, v_done))
+
+    def part(n, i, step):
+        return pl.ds(i * step * n, step * n)
+
+    for src, held, _, _, step, sem, _ in groups:
+        @pl.loop(0, src.shape[0] // step)
+        def _(i):
+            pltpu.make_async_copy(src.at[part(1, i, step)], held.at[part(1, i, step)], sem.at[i]).start()
+
+    for src, held, turned, dst, step, sem, done in groups:
+        rows = src.shape[2]
+
+        @pl.loop(0, src.shape[0] // step)
+        def _(i):
+            block = held.at[part(1, i, step)]
+            pltpu.make_async_copy(block, block, sem.at[i]).wait()
+            for u in range(step):
+                at = pl.ds(pl.multiple_of((i * step + u) * rows, rows), rows)
+                turned[at] = jnp.transpose(held[i * step + u], (1, 0, 2))
+            pltpu.make_async_copy(turned.at[part(rows, i, step)], dst.at[part(rows, i, step)], done.at[i]).start()
+
+    for src, _, turned, _, step, _, done in groups:
+        rows = src.shape[2]
+
+        @pl.loop(0, src.shape[0] // step)
+        def _(i):
+            block = turned.at[part(rows, i, step)]
+            pltpu.make_async_copy(block, block, done.at[i]).wait()
 
 
 def solution(mesh):
@@ -529,10 +580,6 @@
         def flat(x):
             return x.reshape(n_segs * q_rows, q_heads, head_dim)
 
-        stats = (lse * LOG2E).reshape(n_pairs, 2, q_rows, kv_heads, group).transpose(0, 3, 1, 4, 2)
-        stats = jnp.pad(stats.reshape(n_pairs, kv_heads, 2, group * q_rows),
-                        ((0, 0), (0, 0), (0, 0), (0, 128 - group * q_rows)))
-        stats = stats.reshape(n_pairs, kv_heads, 256)
         dims = (n_dev, inner, n_segs, group, q_rows, head_dim, k_rows, late)
         hbm = pl.BlockSpec(memory_space=pl.ANY)
         vmem = pltpu.VMEM
@@ -543,7 +590,7 @@
         stat = vmem((n_pairs, n_dev, 2, 256), F32)
         carried = vmem((group, TILE, TILE), BF16)
         dma = pltpu.SemaphoreType.DMA
-        n_cols = (n_segs - late) // WIDE
+        n_cols = (n_segs - late) // HALF
         kv_out = jax.ShapeDtypeStruct((pieces, kv_heads, PIECE, head_dim), F32)
         sums = jax.ShapeDtypeStruct((2 * n_tiles, 128, head_dim), F32)
         pair = (kv_heads, 2, 2, group, q_rows, head_dim)
@@ -558,7 +605,7 @@
             scratch_shapes=[
                 vmem((2, 3, 2 * q_rows, q_heads, head_dim), BF16),
                 vmem((2, 2, CHUNK, kv_heads, head_dim), BF16),
-                vmem((n_pairs, kv_heads, 256), F32),
+                vmem((n_segs, q_heads, q_rows), F32),
                 vmem((2,) + pair, BF16),
                 vmem((kv_heads, 2, group, q_rows, head_dim), BF16),
                 vmem((2, kv_heads, k_rows, head_dim), BF16),
@@ -566,8 +613,8 @@
                 key_t, key_t, row_t, row_t,
                 vmem((late + 2, group, head_dim, TILE), F32),
                 key_sum, key_sum,
-                vmem((late + 2, TILE, 8), F32),
-                carried, carried,
+                vmem((late + 2, group, TILE, head_dim), BF16), vmem((2, head_dim, TILE), BF16),
+                carried, carried, vmem((3, group, TILE, TILE), BF16),
                 dma((2, 3)), dma((2, 2)), dma, dma((2,)), dma((2,)), dma((n_pairs,)), dma, dma((2,)),
                 dma((2,)), dma((2,)), dma((2,)), dma((2,)), dma, dma, dma, dma, dma((n_segs,)),
                 dma((2,)), dma((2,)), dma((2,)), dma((2, n_cols + 1)), dma((n_pairs,)), dma((2,)), dma((n_pairs,)),
@@ -577,22 +624,22 @@
             cost_estimate=pl.CostEstimate(flops=1680 * 5 * 2 * 256 * 256 * 128, bytes_accessed=64 << 20,
                                           transcendentals=1680 * 65536),
             name="attn_grads",
-        )(flat(q), flat(do), flat(o), k, v, stats)[:3]
+        )(flat(q), flat(do), flat(o), k, v, lse.transpose(0, 2, 1))[:3]
 
         q_step, k_step = 4, 3
-        n_q = n_segs // q_step
-        kv_in = pl.BlockSpec((k_step, kv_heads, PIECE, head_dim), lambda i: (i, 0, 0, 0))
-        kv_back = pl.BlockSpec((k_step * PIECE, kv_heads, head_dim), lambda i: (i, 0, 0))
+        q_rows_out = jax.ShapeDtypeStruct((n_segs * q_rows, q_heads, head_dim), BF16)
+        k_rows_out = jax.ShapeDtypeStruct((k_rows, kv_heads, head_dim), F32)
+        q_sems, k_sems = dma((n_segs // q_step,)), dma((pieces // k_step,))
+        q_blocks, k_blocks = vmem((n_segs, q_heads, q_rows, head_dim), BF16), vmem(kv_out.shape, F32)
+        q_turned, k_turned = vmem(q_rows_out.shape, BF16), vmem(k_rows_out.shape, F32)
         dq, dk, dv = pl.pallas_call(
-            functools.partial(ungroup_kernel, n_q),
-            grid=(pieces // k_step,),
-            out_shape=(jax.ShapeDtypeStruct((n_segs * q_rows, q_heads, head_dim), BF16),
-                       jax.ShapeDtypeStruct((k_rows, kv_heads, head_dim), F32),
-                       jax.ShapeDtypeStruct((k_rows, kv_heads, head_dim), F32)),
-            in_specs=[pl.BlockSpec((q_step, q_heads, q_rows, head_dim), lambda i: (jnp.minimum(i, n_q - 1), 0, 0, 0)),
-                      kv_in, kv_in],
-            out_specs=(pl.BlockSpec((q_step * q_rows, q_heads, head_dim), lambda i: (jnp.minimum(i, n_q - 1), 0, 0)),
-                       kv_back, kv_back),
+            functools.partial(ungroup_kernel, q_step, k_step),
+            out_shape=(q_rows_out, k_rows_out, k_rows_out),
+            in_specs=[hbm] * 3,
+            out_specs=(hbm,) * 3,
+            scratch_shapes=[q_blocks, k_blocks, k_blocks, q_turned, k_turned, k_turned,
+                            q_sems, k_sems, k_sems, q_sems, k_sems, k_sems],
+            compiler_params=pltpu.CompilerParams(vmem_limit_bytes=67043328),
             name="ungroup",
         )(dq.reshape(n_segs, q_heads, q_rows, head_dim), dk, dv)
         return dq.reshape(n_segs, q_rows, q_heads, head_dim), dk, dv

time: 414 us -> 376 us (0.908)
  Pallas kernels: 409 us -> 375 us
    pallas_call x1, Pallas kernels: 395 us -> 364 us  [local_grads(): pl.pallas_call(functools.partial(attn_kernel, dims), out_shape=(jax.Shape...]
where the time goes in v4:
time: 376 us; the launch traced here: 375 us
  Pallas kernels  375 us (100%)
    pallas_call x1, Pallas kernels, local_grads(): pl.pallas_call(functools.partial(attn_kernel, dims), out_shape=(jax.Shape...  364 us
    pallas_call x1, Pallas kernels, local_grads(): pl.pallas_call(functools.partial(ungroup_kernel, q_step, k_step), out_sha...  10.9 us

profile of v4, /device:TPU:1, one launch (start us, length us, event | category | flops | bytes accessed | tf_op | source)
XLA Modules:
  0.0 375.3 jit_solution(16191277880132159173)
XLA Ops:
  0.6 363.6 %attn_grads.1 = (bf16[32,8,3,32,128]{4,3,2,1,0:T(8,128)(2,1)}, f32[33,8,32,128]{3,2,1,0:T(8,128)}, f32[33,8,32,128]{3,2,1,0:T(8,128)}, bf16[2,16,8,2,2,3,32,128]...) custom-call(bf16[1024,24,128]{2,1,0:T(8,128)(2,1)} %bitcast.7, ...), custom_call_target="tpu_custom_call" | custom-call | flops 140928614400 | bytes 67108864 | tf_op jit(solution)/shard_map/attn_grads/pallas_call | solution.py:597
  364.2 10.9 %ungroup.1 = (bf16[1024,24,128]{2,1,0:T(8,128)(2,1)}, f32[1056,8,128]{2,1,0:T(8,128)}, f32[1056,8,128]{2,1,0:T(8,128)}) custom-call(bf16[32,24,32,128]{3,2,1,0:T(8,128)(2,1)} %bitcast.6, f32[33,8,32,128]{3,2,1,0:T(8,128)} %get-tuple-element.10.dk_i, f32[33,8,32,128]{3,2,1,0:T(8,128)} %get-tuple-element.11.dv_i), custom_call_target="tpu_custom_call" | custom-call | tf_op jit(solution)/shard_map/ungroup/pallas_call | solution.py:635

commit v5 on v4

--- a/solution.py
+++ b/solution.py
@@ -43,7 +43,7 @@
     n_cols = late_tile // HALF
     pieces = k_rows // PIECE
     rest = n_dev - 1
-    early_pairs = first_late // 2
+    middle_row = first_late // 2
 
     def chip_cores(flip_outer, flip_inner):
         y = 1 - outer_at if flip_outer else outer_at
@@ -84,8 +84,12 @@
         def _():
             arrived(half, sem)
 
+    def row_at(i):
+        return jnp.where(i < middle_row, first_late - 1 - i,
+                         jnp.where(i < middle_row + late, first_late - middle_row + i, n_segs - 1 - i))
+
     def pair_at(k):
-        return jnp.where(k < early_pairs, early_pairs - 1 - k, k)
+        return lax.div(row_at(2 * k), 2)
 
     def fetch(k):
         r = pair_at(k)
@@ -126,6 +130,7 @@
                 kv_s[a, :, rows] = jnp.transpose(nat_k[buf, a], (1, 0, 2))
                 land[dst, :] = kv_s[a, me, rows]
 
+    def ship_keys(first, n):
         lo, rows = first * CHUNK, n * CHUNK
         send_keys(kv_s, me, lo, rows)
         src = pl.ds(lo, rows)
@@ -205,11 +210,13 @@
     barrier = pltpu.get_barrier_semaphore()
     for p in along + across + [mate]:
         pl.semaphore_signal(barrier, inc=1, device_id=device(p), device_id_type=MESH)
+    chunks = k_rows // CHUNK
+    stage_keys(0, 2)
     pl.semaphore_wait(barrier, rest)
+    ship_keys(0, 2)
+    stage_keys(2, chunks - 2)
+    ship_keys(2, chunks - 2)
     arrived(ls_v, ls_sem)
-    chunks = k_rows // CHUNK
-    stage_keys(0, chunks // 2)
-    stage_keys(chunks // 2, chunks - chunks // 2)
 
     @pl.loop(0, n_pairs)
     def _(k):
@@ -392,14 +399,35 @@
             for a, (src, dst) in enumerate(((dk_a, mir_k), (dv_a, mir_v))):
                 remote(src.at[pl.ds(2 * t, 2)], dst.at[pl.ds(2 * t, 2)], dkv_mir.at[a], dkv_mir_recv.at[a, mir], mate)
 
+    n_late = n_tiles - late_tile
+
+    def column(dev, i):
+        return lax.rem(dev + i, n_cols)
+
+    def ship_column(dev, i, mine):
+        @pl.loop(0, HALF)
+        def _(w):
+            ship_tile(column(dev, i) + w * n_cols, dev, mine)
+
+    def ship_late(dev, n, mine):
+        ship_tile(late_tile + lax.rem(n + dev, n_late), dev, mine)
+
+    def forward_column(i):
+        for a, ref in enumerate((mir_k, mir_v)):
+            arrived(ref.at[pl.ds(0, 2 * HALF)], dkv_mir_recv.at[a, i])
+        ship_column(mate, i, False)
+
+    late_end = middle_row + late
+
     @pl.loop(0, n_segs)
     def _(i):
-        early = i < first_late
-        j = jnp.where(early, first_late - 1 - i, i)
-        slot = jnp.where(early, lax.rem(j, 2), i - first_late + 2)
+        j = row_at(i)
+        before = jnp.where(i == 0, first_late, row_at(jnp.maximum(i - 1, 0)))
+        early = j < first_late
+        early_before = (before < first_late) | (i == 0)
+        slot = jnp.where(early, lax.rem(j, 2), j - first_late + 2)
+        old_slot = jnp.where(early_before, lax.rem(before, 2), before - first_late + 2)
         lo = jnp.where(early, 0, late_tile)
-        before = jnp.where(early, j + 1, jnp.where(i == first_late, 0, j - 1))
-        old_slot = jnp.where(early, 1 - slot, jnp.where(i == first_late, 0, slot - 1))
         open_row(j, slot, lax.rem(i, 2) == 0)
         n = j + 1 - lo
 
@@ -426,29 +454,30 @@
             def _():
                 products(tiles(half_end, r + 1), *after(half_end), masked=True)
 
-        @pl.when((i > 0) & (i <= first_late))
+        @pl.when((i > 0) & early_before)
         def _():
             close_row(before, old_slot, jnp.where(i > 1, before + 1, -1))
 
-    n_late = n_tiles - late_tile
-
-    def column(dev, i):
-        return lax.rem(dev + i, n_cols)
-
-    def ship_column(dev, i, mine):
-        @pl.loop(0, HALF)
-        def _(w):
-            ship_tile(column(dev, i) + w * n_cols, dev, mine)
-
-    def ship_late(dev, i, mine):
-        @pl.loop(lax.div(i * n_late, n_cols), lax.div((i + 1) * n_late, n_cols))
-        def _(n):
-            ship_tile(late_tile + lax.rem(n + dev, n_late), dev, mine)
-
-    def forward_column(i):
-        for a, ref in enumerate((mir_k, mir_v)):
-            arrived(ref.at[pl.ds(0, 2 * HALF)], dkv_mir_recv.at[a, i])
-        ship_column(mate, i, False)
+        @pl.when(i == late_end)
+        def _():
+            close_tiles(late_tile, n_late, 1, n_cols)
+
+        @pl.when(i == late_end + 1)
+        def _():
+            for a, ref in enumerate((mir_k, mir_v)):
+                arrived(ref.at[pl.ds(0, 2 * n_late)], dkv_mir_recv.at[a, n_cols])
+
+        @pl.when(i >= late_end)
+        def _():
+            turn_of = lax.div(i - late_end, 2)
+
+            @pl.when(lax.rem(i, 2) == 0)
+            def _():
+                ship_late(me, turn_of, True)
+
+            @pl.when(lax.rem(i, 2) == 1)
+            def _():
+                ship_late(mate, turn_of, False)
 
     @pl.loop(0, n_cols)
     def _(i):
@@ -462,35 +491,32 @@
             middle = pair == late // 4
             last_tile = c + (HALF - 1) * n_cols
             products([(j + u, slot + u, c + w * n_cols) for u in range(2) for w in range(HALF)],
-                     jnp.where(first, late + 1, slot - 1),
-                     jnp.where(first, jnp.where(i == 0, n_segs, column(me, i + n_cols - 1) + (HALF - 1) * n_cols),
+                     jnp.where(first, jnp.where(i == 0, 0, late + 1), slot - 1),
+                     jnp.where(first, jnp.where(i == 0, 1, column(me, i + n_cols - 1) + (HALF - 1) * n_cols),
                                last_tile))
 
             @pl.when(first & (i == 0))
             def _():
-                close_tiles(late_tile, n_late, 1, n_cols)
+                close_row(0, 0, 1)
 
             @pl.when(first & (i > 0))
             def _():
                 close_tiles(column(me, i - 1), HALF, n_cols, i - 1)
                 ship_column(me, i - 1, True)
 
-            @pl.when(first)
-            def _():
-                ship_late(me, i, True)
-
-            @pl.when(middle & (i == 0))
-            def _():
-                for a, ref in enumerate((mir_k, mir_v)):
-                    arrived(ref.at[pl.ds(0, 2 * n_late)], dkv_mir_recv.at[a, n_cols])
+            shipped = (n_segs - late_end) // 2
+
+            @pl.when(first & (i < n_late - shipped))
+            def _():
+                ship_late(me, shipped + i, True)
 
             @pl.when(middle & (i > 0))
             def _():
                 forward_column(i - 1)
 
-            @pl.when(middle)
-            def _():
-                ship_late(mate, i, False)
+            @pl.when(middle & (i < n_late - shipped))
+            def _():
+                ship_late(mate, shipped + i, False)
 
             @pl.when(i == n_cols - 1)
             def _():

time: 376 us -> 377 us (level)
  no operation moved by 1% of the time
where the time goes in v5:
time: 377 us; the launch traced here: 375 us
  Pallas kernels  374 us (99%)
    pallas_call x1, Pallas kernels, local_grads(): pl.pallas_call(functools.partial(attn_kernel, dims), out_shape=(jax.Shape...  363 us
    pallas_call x1, Pallas kernels, local_grads(): pl.pallas_call(functools.partial(ungroup_kernel, q_step, k_step), out_sha...  10.9 us

profile of v5, /device:TPU:1, one launch (start us, length us, event | category | flops | bytes accessed | tf_op | source)
XLA Modules:
  0.0 374.8 jit_solution(4737284508940000880)
XLA Ops:
  0.6 363.0 %attn_grads.1 = (bf16[32,8,3,32,128]{4,3,2,1,0:T(8,128)(2,1)}, f32[33,8,32,128]{3,2,1,0:T(8,128)}, f32[33,8,32,128]{3,2,1,0:T(8,128)}, bf16[2,16,8,2,2,3,32,128]...) custom-call(bf16[1024,24,128]{2,1,0:T(8,128)(2,1)} %bitcast.7, ...), custom_call_target="tpu_custom_call" | custom-call | flops 140928614400 | bytes 67108864 | tf_op jit(solution)/shard_map/attn_grads/pallas_call | solution.py:623
  363.7 10.9 %ungroup.1 = (bf16[1024,24,128]{2,1,0:T(8,128)(2,1)}, f32[1056,8,128]{2,1,0:T(8,128)}, f32[1056,8,128]{2,1,0:T(8,128)}) custom-call(bf16[32,24,32,128]{3,2,1,0:T(8,128)(2,1)} %bitcast.6, f32[33,8,32,128]{3,2,1,0:T(8,128)} %get-tuple-element.10.dk_i, f32[33,8,32,128]{3,2,1,0:T(8,128)} %get-tuple-element.11.dv_i), custom_call_target="tpu_custom_call" | custom-call | tf_op jit(solution)/shard_map/ungroup/pallas_call | solution.py:661

commit v6 on v5

--- a/solution.py
+++ b/solution.py
@@ -18,6 +18,7 @@
 ORDER = "SVPKSQPVSKPQVKQ"
 PIECE = 32
 CHUNK = 96
+MAIN_VMEM = 48 << 20
 
 
 def dot(a, b, ca, cb):
@@ -25,10 +26,10 @@
 
 
 def attn_kernel(dims, q_n, do_n, o_n, k_n, v_n, ls_n, dq_o, dk_o, dv_o, box, mir_kv, mir_q, mir_k, mir_v,
-                nat, nat_k, ls_v, stg, o_s, kv_s, st_s, qd_b, k_b, v_b, st_b,
+                nat, nat_k, ls_v, stg, o_s, st_s, qd_b, k_b, v_b, st_b,
                 k_t, v_t, q_t, do_t, dq_a, dk_a, dv_a, aug, aug_k, p_c, d_c, turn,
                 nat_sem, natk_sem, ls_sem, box_own, box_send, box_recv, pair_send, pair_d2d,
-                kv_send, kv_d2d, kv_mir, kv_mir_recv, st_send, dq_send, dq_d2d, dq_mir, dq_mir_recv,
+                kv_send, kv_fwd, kv_d2d, kv_mir, kv_mir_recv, st_send, dq_send, dq_d2d, dq_mir, dq_mir_recv,
                 dkv_send, dkv_d2d, dkv_mir, dkv_mir_recv, row_recv, kv_recv, st_recv, out_recv):
     n_dev, inner, n_segs, group, q_rows, head_dim, k_rows, late = dims
     scale = head_dim ** -0.5
@@ -45,6 +46,8 @@
     rest = n_dev - 1
     middle_row = first_late // 2
 
+    kv_s = [ref.reshape(n_dev, k_rows, head_dim) for ref in (k_t, v_t)]
+
     def chip_cores(flip_outer, flip_inner):
         y = 1 - outer_at if flip_outer else outer_at
         x = (inner - 2) - (inner_at - core) if flip_inner else inner_at - core
@@ -102,14 +105,14 @@
             pltpu.make_async_copy(src.at[pl.ds(c * CHUNK, CHUNK)], nat_k.at[lax.rem(c, 2), a],
                                   natk_sem.at[lax.rem(c, 2), a]).start()
 
-    def send_keys(src, owner, lo, n):
+    def send_keys(src, owner, lo, n, sem):
         rows = pl.ds(lo, n)
         dst = pl.ds(pl.multiple_of(owner * k_rows + lo, 32), n)
 
         def send_all(to):
             for p in to:
                 for a, land in enumerate((k_b, v_b)):
-                    remote(src.at[a, p, rows], land.at[dst], kv_send.at[a], kv_recv.at[a], p)
+                    remote(src[a].at[p, rows], land.at[dst], sem.at[a], kv_recv.at[a], p)
 
         sent_by_me(send_all)
 
@@ -127,22 +130,23 @@
                 fetch_keys(c + 1)
 
             for a, land in enumerate((k_b, v_b)):
-                kv_s[a, :, rows] = jnp.transpose(nat_k[buf, a], (1, 0, 2))
-                land[dst, :] = kv_s[a, me, rows]
+                block = jnp.transpose(nat_k[buf, a], (1, 0, 2))
+                kv_s[a][:, rows] = block
+                land[dst, :] = kv_s[a][me, rows]
 
     def ship_keys(first, n):
         lo, rows = first * CHUNK, n * CHUNK
-        send_keys(kv_s, me, lo, rows)
+        send_keys(kv_s, me, lo, rows, kv_send)
         src = pl.ds(lo, rows)
         dst = pl.ds(pl.multiple_of(me * k_rows + lo, 32), rows)
         for a, land in enumerate((k_b, v_b)):
-            remote(kv_s.at[a, mate, src], land.at[dst], kv_d2d.at[a], kv_recv.at[a], mate)
-            remote(kv_s.at[a, :, src], mir_kv.at[a, :, src], kv_mir.at[a], kv_mir_recv.at[a], mate)
+            remote(kv_s[a].at[mate, src], land.at[dst], kv_d2d.at[a], kv_recv.at[a], mate)
+            remote(kv_s[a].at[:, src], mir_kv.at[a, :, src], kv_mir.at[a], kv_mir_recv.at[a], mate)
 
     def forward_keys():
         for a in range(2):
             arrived(mir_kv.at[a], kv_mir_recv.at[a])
-        send_keys(mir_kv, mate, 0, k_rows)
+        send_keys([mir_kv.at[a] for a in range(2)], mate, 0, k_rows, kv_fwd)
 
     def stage_pair(k):
         buf = lax.rem(k, 2)
@@ -251,11 +255,23 @@
     for a, land in enumerate((k_b, v_b)):
         arrived(land.at[pl.ds(0, rest * k_rows)], kv_recv.at[a])
 
+    half = pl.ds(0, n_dev // 2)
+    quarter = pl.ds(0, n_dev // 4)
+    one = pl.ds(0, 1)
+    for a in range(2):
+        wait_sent(kv_s[a].at[half], kv_s[a].at[quarter], kv_send.at[a])
+        arrived(kv_s[a].at[one], kv_d2d.at[a])
+        arrived(kv_s[a], kv_mir.at[a])
+
     @pl.loop(0, n_tiles)
     def _(t):
-        rows = pl.ds(pl.multiple_of(t * TILE, TILE), TILE)
-        k_t[t] = k_b[rows, :].T
-        v_t[t] = v_b[rows, :].T
+        for b in range(2):
+            rows = pl.ds(pl.multiple_of(t * TILE + b * 128, 128), 128)
+            k_t[2 * t + b] = k_b[rows, :].T
+            v_t[2 * t + b] = v_b[rows, :].T
+
+    def tile_of(ref, t):
+        return jnp.concatenate([ref[2 * t], ref[2 * t + 1]], 1)
 
     def products(items, old_slot, old_tile, masked=False):
         n = len(items)
@@ -277,7 +293,7 @@
                     j, slot, t = item
                     a = "SP".index(step)
                     rows = jnp.concatenate([qd_b[j, a, h], aug[slot, h]], 1)
-                    cols = jnp.concatenate([(k_t, v_t)[a][t], aug_k[a]], 0)
+                    cols = jnp.concatenate([tile_of((k_t, v_t)[a], t), aug_k[a]], 0)
                     raw[step][h] = dot(rows, cols, 1, 0)
                     if raw["S"][h] is not None and raw["P"][h] is not None:
                         p = jnp.exp2(raw["S"][h] * (scale * LOG2E))
@@ -290,7 +306,7 @@
                         turn[new_turn, h] = ds.T
                 elif step == "Q":
                     right = turn[old_turn, h] if kept is None else kept[h]
-                    dq_a[old_slot, h] += dot(k_t[old_tile], right, 1, 0)
+                    dq_a[old_slot, h] += dot(tile_of(k_t, old_tile), right, 1, 0)
                 else:
                     lanes = slice(h * TILE, (h + 1) * TILE)
                     left = (do_t if step == "V" else q_t)[old_slot, :, lanes]
@@ -338,7 +354,7 @@
             qd_b[j, 0, h] = (dq_a[slot, h].T * scale).astype(BF16)
         remote(qd_b.at[j, 0], mir_q.at[j], dq_mir, dq_mir_recv.at[j], mate)
         remote(qd_b.at[j, 0, :, rows_of(mate)], dq_o.at[j, me], dq_d2d, out_recv.at[0], mate)
-        pltpu.make_async_copy(qd_b.at[j, 0, :, rows_of(me)], dq_o.at[j, me], out_recv.at[0]).start()
+        dq_o[j, me] = qd_b[j, 0, :, rows_of(me)]
 
         def send_all(to):
             for p in to:
@@ -366,7 +382,7 @@
                 if mine:
                     @pl.when(owner == me)
                     def _():
-                        pltpu.make_async_copy(ref.at[src], out.at[dst, src_dev], out_recv.at[1 + n_out]).start()
+                        out[dst, src_dev] = ref[src]
 
                     @pl.when(owner == mate)
                     def _():
@@ -533,13 +549,9 @@
     forward_row(n_segs - 1)
     forward_column(n_cols - 1)
 
-    half = pl.ds(0, n_dev // 2)
-    one = pl.ds(0, 1)
     wait_sent(box.at[0], box.at[0, :, half], pair_send)
     for a in range(2):
-        wait_sent(kv_s.at[a], kv_s.at[a, half], kv_send.at[a])
-        arrived(kv_s.at[a, one], kv_d2d.at[a])
-        arrived(kv_s.at[a], kv_mir.at[a])
+        wait_sent(mir_kv.at[a, half], mir_kv.at[a, quarter], kv_fwd.at[a])
     arrived(st_s.at[:, pl.ds(0, rest)], st_send)
     wait_sent(dq_o, dq_o.at[:, half], dq_send)
     arrived(dq_o.at[:, one], dq_d2d)
@@ -549,41 +561,30 @@
         arrived(out.at[:, one], dkv_d2d.at[a])
         arrived(ref, dkv_mir.at[a])
     for n, ref in enumerate((dq_o, dk_o, dv_o)):
-        arrived(ref, out_recv.at[n])
-
-
-def ungroup_kernel(q_step, k_step, dq_i, dk_i, dv_i, dq_o, dk_o, dv_o, q_in, k_in, v_in, q_out, k_out, v_out,
-                   q_sem, k_sem, v_sem, q_done, k_done, v_done):
-    groups = ((dq_i, q_in, q_out, dq_o, q_step, q_sem, q_done), (dk_i, k_in, k_out, dk_o, k_step, k_sem, k_done),
-              (dv_i, v_in, v_out, dv_o, k_step, v_sem, v_done))
-
-    def part(n, i, step):
-        return pl.ds(i * step * n, step * n)
-
-    for src, held, _, _, step, sem, _ in groups:
+        arrived(ref.at[:, pl.ds(0, rest)], out_recv.at[n])
+
+
+def ungroup_kernel(q_step, k_step, dq_i, dk_i, dv_i, dq_o, dk_o, dv_o, q_out, k_out, v_out, q_done, k_done, v_done):
+    groups = ((dq_i, q_out, dq_o, q_step, q_done), (dk_i, k_out, dk_o, k_step, k_done), (dv_i, v_out, dv_o, k_step, v_done))
+
+    for src, turned, dst, step, done in groups:
+        rows, width = src.shape[-2], src.shape[-1]
+
         @pl.loop(0, src.shape[0] // step)
         def _(i):
-            pltpu.make_async_copy(src.at[part(1, i, step)], held.at[part(1, i, step)], sem.at[i]).start()
-
-    for src, held, turned, dst, step, sem, done in groups:
-        rows = src.shape[2]
+            for u in range(step):
+                at = pl.ds(pl.multiple_of((i * step + u) * rows, rows), rows)
+                turned[at] = jnp.transpose(src[i * step + u].reshape(-1, rows, width), (1, 0, 2))
+            part = pl.ds(i * step * rows, step * rows)
+            pltpu.make_async_copy(turned.at[part], dst.at[part], done.at[i]).start()
+
+    for src, turned, _, step, done in groups:
+        rows = src.shape[-2]
 
         @pl.loop(0, src.shape[0] // step)
         def _(i):
-            block = held.at[part(1, i, step)]
-            pltpu.make_async_copy(block, block, sem.at[i]).wait()
-            for u in range(step):
-                at = pl.ds(pl.multiple_of((i * step + u) * rows, rows), rows)
-                turned[at] = jnp.transpose(held[i * step + u], (1, 0, 2))
-            pltpu.make_async_copy(turned.at[part(rows, i, step)], dst.at[part(rows, i, step)], done.at[i]).start()
-
-    for src, _, turned, _, step, _, done in groups:
-        rows = src.shape[2]
-
-        @pl.loop(0, src.shape[0] // step)
-        def _(i):
-            block = turned.at[part(rows, i, step)]
-            pltpu.make_async_copy(block, block, done.at[i]).wait()
+            part = turned.at[pl.ds(i * step * rows, step * rows)]
+            pltpu.make_async_copy(part, part, done.at[i]).wait()
 
 
 def solution(mesh):
@@ -610,31 +611,32 @@
         hbm = pl.BlockSpec(memory_space=pl.ANY)
         vmem = pltpu.VMEM
         key = vmem((keys, head_dim), BF16)
-        key_t = vmem((n_tiles, head_dim, TILE), BF16)
+        key_t = vmem((2 * n_tiles, head_dim, 128), BF16)
         row_t = vmem((late + 2, head_dim, group * TILE), BF16)
         key_sum = vmem((2 * n_tiles, head_dim, 128), F32)
         stat = vmem((n_pairs, n_dev, 2, 256), F32)
         carried = vmem((group, TILE, TILE), BF16)
         dma = pltpu.SemaphoreType.DMA
         n_cols = (n_segs - late) // HALF
-        kv_out = jax.ShapeDtypeStruct((pieces, kv_heads, PIECE, head_dim), F32)
+        q_out = vmem((n_segs, kv_heads, group, q_rows, head_dim), BF16)
+        kv_out = vmem((pieces, kv_heads, PIECE, head_dim), F32)
+        on_chip = pl.BlockSpec(memory_space=pltpu.VMEM)
         sums = jax.ShapeDtypeStruct((2 * n_tiles, 128, head_dim), F32)
         pair = (kv_heads, 2, 2, group, q_rows, head_dim)
         dq, dk, dv = pl.pallas_call(
             functools.partial(attn_kernel, dims),
-            out_shape=(jax.ShapeDtypeStruct((n_segs, kv_heads, group, q_rows, head_dim), BF16), kv_out, kv_out,
+            out_shape=(q_out, kv_out, kv_out,
                        jax.ShapeDtypeStruct((2, n_pairs) + pair, BF16),
                        jax.ShapeDtypeStruct((2, kv_heads, k_rows, head_dim), BF16),
                        jax.ShapeDtypeStruct((n_segs, group, TILE, head_dim), BF16), sums, sums),
             in_specs=[hbm] * 6,
-            out_specs=(hbm,) * 8,
+            out_specs=(on_chip,) * 3 + (hbm,) * 5,
             scratch_shapes=[
                 vmem((2, 3, 2 * q_rows, q_heads, head_dim), BF16),
                 vmem((2, 2, CHUNK, kv_heads, head_dim), BF16),
                 vmem((n_segs, q_heads, q_rows), F32),
                 vmem((2,) + pair, BF16),
                 vmem((kv_heads, 2, group, q_rows, head_dim), BF16),
-                vmem((2, kv_heads, k_rows, head_dim), BF16),
                 stat, vmem((n_segs, 2, group, TILE, head_dim), BF16), key, key, stat,
                 key_t, key_t, row_t, row_t,
                 vmem((late + 2, group, head_dim, TILE), F32),
@@ -642,11 +644,11 @@
                 vmem((late + 2, group, TILE, head_dim), BF16), vmem((2, head_dim, TILE), BF16),
                 carried, carried, vmem((3, group, TILE, TILE), BF16),
                 dma((2, 3)), dma((2, 2)), dma, dma((2,)), dma((2,)), dma((n_pairs,)), dma, dma((2,)),
-                dma((2,)), dma((2,)), dma((2,)), dma((2,)), dma, dma, dma, dma, dma((n_segs,)),
+                dma((2,)), dma((2,)), dma((2,)), dma((2,)), dma((2,)), dma, dma, dma, dma, dma((n_segs,)),
                 dma((2,)), dma((2,)), dma((2,)), dma((2, n_cols + 1)), dma((n_pairs,)), dma((2,)), dma((n_pairs,)),
                 dma((3,))],
             compiler_params=pltpu.CompilerParams(
-                collective_id=0, has_side_effects=True, vmem_limit_bytes=67043328),
+                collective_id=0, has_side_effects=True, vmem_limit_bytes=MAIN_VMEM),
             cost_estimate=pl.CostEstimate(flops=1680 * 5 * 2 * 256 * 256 * 128, bytes_accessed=64 << 20,
                                           transcendentals=1680 * 65536),
             name="attn_grads",
@@ -656,18 +658,16 @@
         q_rows_out = jax.ShapeDtypeStruct((n_segs * q_rows, q_heads, head_dim), BF16)
         k_rows_out = jax.ShapeDtypeStruct((k_rows, kv_heads, head_dim), F32)
         q_sems, k_sems = dma((n_segs // q_step,)), dma((pieces // k_step,))
-        q_blocks, k_blocks = vmem((n_segs, q_heads, q_rows, head_dim), BF16), vmem(kv_out.shape, F32)
         q_turned, k_turned = vmem(q_rows_out.shape, BF16), vmem(k_rows_out.shape, F32)
         dq, dk, dv = pl.pallas_call(
             functools.partial(ungroup_kernel, q_step, k_step),
             out_shape=(q_rows_out, k_rows_out, k_rows_out),
-            in_specs=[hbm] * 3,
+            in_specs=[on_chip] * 3,
             out_specs=(hbm,) * 3,
-            scratch_shapes=[q_blocks, k_blocks, k_blocks, q_turned, k_turned, k_turned,
-                            q_sems, k_sems, k_sems, q_sems, k_sems, k_sems],
-            compiler_params=pltpu.CompilerParams(vmem_limit_bytes=67043328),
+            scratch_shapes=[q_turned, k_turned, k_turned, q_sems, k_sems, k_sems],
+            compiler_params=pltpu.CompilerParams(vmem_limit_bytes=24 << 20),
             name="ungroup",
-        )(dq.reshape(n_segs, q_heads, q_rows, head_dim), dk, dv)
+        )(dq, dk, dv)
         return dq.reshape(n_segs, q_rows, q_heads, head_dim), dk, dv
 
     return jax.shard_map(local_grads, mesh=mesh,

time: 377 us -> 371 us (0.984)
  Pallas kernels: 374 us -> 368 us
    pallas_call x1, Pallas kernels: 10.9 us -> 5.75 us  [local_grads(): pl.pallas_call(functools.partial(ungroup_kernel, q_step, k_step), out_sha...]
where the time goes in v6:
time: 371 us; the launch traced here: 369 us
  Pallas kernels  368 us (99%)
    pallas_call x1, Pallas kernels, local_grads(): pl.pallas_call(functools.partial(attn_kernel, dims), out_shape=(q_out, kv...  362 us

profile of v6, /device:TPU:1, one launch (start us, length us, event | category | flops | bytes accessed | tf_op | source)
XLA Modules:
  0.0 368.7 jit_solution(13020442658379718587)
XLA Ops:
  0.6 362.1 %attn_grads.1 = (bf16[32,8,3,32,128]{4,3,2,1,0:T(8,128)(2,1)S(1)}, f32[33,8,32,128]{3,2,1,0:T(8,128)S(1)}, f32[33,8,32,128]{3,2,1,0:T(8,128)S(1)}, bf16[2,16,8,2...) custom-call(bf16[1024,24,128]{2,1,0:T(8,128)(2,1)} %bitcast.5, ...), custom_call_target="tpu_custom_call" | custom-call | flops 140928614400 | bytes 67108864 | tf_op jit(solution)/shard_map/attn_grads/pallas_call | solution.py:626
  362.8 5.8 %ungroup.1 = (bf16[1024,24,128]{2,1,0:T(8,128)(2,1)}, f32[1056,8,128]{2,1,0:T(8,128)}, f32[1056,8,128]{2,1,0:T(8,128)}) custom-call(bf16[32,8,3,32,128]{4,3,2,1,0:T(8,128)(2,1)S(1)} %get-tuple-element.9.dq_i, f32[33,8,32,128]{3,2,1,0:T(8,128)S(1)} %get-tuple-element.10.dk_i, f32[33,8,32,128]{3,2,1,0:T(8,128)S(1)} %get-tuple-element.11.dv_i), custom_call_target="tpu_custom_call" | custom-call | tf_op jit(solution)/shard_map/ungroup/pallas_call | solution.py:662

commit v7 on v6

--- a/solution.py
+++ b/solution.py
@@ -15,10 +15,11 @@
 TILE = 256
 WIDE = 8
 HALF = 4
+EARLY_SLOTS = 3
 ORDER = "SVPKSQPVSKPQVKQ"
 PIECE = 32
 CHUNK = 96
-MAIN_VMEM = 48 << 20
+MAIN_VMEM = 49 << 20
 
 
 def dot(a, b, ca, cb):
@@ -241,9 +242,10 @@
         dk_a[i] = jnp.zeros((head_dim, 128), F32)
         dv_a[i] = jnp.zeros((head_dim, 128), F32)
 
-    q_t[0] = jnp.zeros(q_t.shape[1:], BF16)
-    do_t[0] = jnp.zeros(do_t.shape[1:], BF16)
-    dq_a[0] = jnp.zeros(dq_a.shape[1:], F32)
+    unused = EARLY_SLOTS - 1
+    q_t[unused] = jnp.zeros(q_t.shape[1:], BF16)
+    do_t[unused] = jnp.zeros(do_t.shape[1:], BF16)
+    dq_a[unused] = jnp.zeros(dq_a.shape[1:], F32)
     p_c[...] = jnp.zeros(p_c.shape, BF16)
     d_c[...] = jnp.zeros(d_c.shape, BF16)
     turn[1] = jnp.zeros(turn.shape[1:], BF16)
@@ -273,7 +275,7 @@
     def tile_of(ref, t):
         return jnp.concatenate([ref[2 * t], ref[2 * t + 1]], 1)
 
-    def products(items, old_slot, old_tile, masked=False):
+    def products(items, old_slot, old_tile, masked=False, last=None):
         n = len(items)
         old = [(p_c[h], d_c[h]) for h in range(group)]
         old_turn = 1
@@ -320,15 +322,18 @@
             old, old_turn, old_slot, old_tile = new, new_turn, slot, t
         for h in range(group):
             p_c[h], d_c[h] = old[h]
-
-    def open_row(j, slot, opens_pair):
-        pair, s = lax.div(j, 2), lax.rem(j, 2)
-
-        @pl.when(opens_pair)
-        def _():
+        if last is not None:
+            last()
+
+    def await_pair(i):
+        @pl.when((lax.rem(i, 2) == 0) & (i < n_segs))
+        def _():
+            pair = pair_at(lax.div(i, 2))
             arrived(qd_b.at[pl.ds(2 * pair, 2), :, :, pl.ds(0, rest * q_rows)], row_recv.at[pair])
             arrived(st_b.at[pair, pl.ds(0, rest)], st_recv.at[pair])
 
+    def open_row(j, slot):
+        pair, s = lax.div(j, 2), lax.rem(j, 2)
         q_t[slot] = qd_b[j, 0].reshape(group * TILE, head_dim).T
         do_t[slot] = qd_b[j, 1].reshape(group * TILE, head_dim).T
         dq_a[slot] = jnp.zeros((group, head_dim, TILE), F32)
@@ -349,9 +354,11 @@
 
         sent_by_me(send_all)
 
-    def close_row(j, slot, before):
+    def round_row(j, slot):
         for h in range(group):
             qd_b[j, 0, h] = (dq_a[slot, h].T * scale).astype(BF16)
+
+    def close_row(j, before):
         remote(qd_b.at[j, 0], mir_q.at[j], dq_mir, dq_mir_recv.at[j], mate)
         remote(qd_b.at[j, 0, :, rows_of(mate)], dq_o.at[j, me], dq_d2d, out_recv.at[0], mate)
         dq_o[j, me] = qd_b[j, 0, :, rows_of(me)]
@@ -434,17 +441,24 @@
         ship_column(mate, i, False)
 
     late_end = middle_row + late
+    late_slot = EARLY_SLOTS + late - 1
+
+    def slot_at(i):
+        early_index = jnp.where(i < middle_row, i, i - late)
+        return jnp.where((i >= middle_row) & (i < late_end), i - middle_row + EARLY_SLOTS,
+                         lax.rem(early_index + EARLY_SLOTS, EARLY_SLOTS))
+
+    await_pair(0)
+    open_row(first_late - 1, 0)
 
     @pl.loop(0, n_segs)
     def _(i):
-        j = row_at(i)
+        j, slot = row_at(i), slot_at(i)
         before = jnp.where(i == 0, first_late, row_at(jnp.maximum(i - 1, 0)))
-        early = j < first_late
         early_before = (before < first_late) | (i == 0)
-        slot = jnp.where(early, lax.rem(j, 2), j - first_late + 2)
-        old_slot = jnp.where(early_before, lax.rem(before, 2), before - first_late + 2)
-        lo = jnp.where(early, 0, late_tile)
-        open_row(j, slot, lax.rem(i, 2) == 0)
+        old_slot = jnp.where(i == 0, unused, slot_at(i - 1))
+        lo = jnp.where(j < first_late, 0, late_tile)
+        closes = (i > 0) & early_before
         n = j + 1 - lo
 
         def tiles(t, n):
@@ -452,27 +466,25 @@
 
         def after(t):
             return jnp.where(t == lo, old_slot, slot), jnp.where(t == lo, before + 1, t - 1)
-
-        wide_end = lo + lax.div(n, WIDE) * WIDE
-        half_end = lo + lax.div(n, HALF) * HALF
 
         @pl.loop(0, lax.div(n, WIDE))
         def _(c):
             t = lo + c * WIDE
             products(tiles(t, WIDE), *after(t))
 
-        @pl.when(half_end > wide_end)
-        def _():
-            products(tiles(wide_end, HALF), *after(wide_end))
-
-        for r in range(HALF):
-            @pl.when(lax.rem(n, HALF) == r)
-            def _():
-                products(tiles(half_end, r + 1), *after(half_end), masked=True)
-
-        @pl.when((i > 0) & early_before)
-        def _():
-            close_row(before, old_slot, jnp.where(i > 1, before + 1, -1))
+        await_pair(i + 1)
+        coming = jnp.minimum(i + 1, n_segs - 1)
+        wide_end = lo + lax.div(n, WIDE) * WIDE
+        for r in range(WIDE):
+            @pl.when(lax.rem(n, WIDE) == r)
+            def _():
+                products(tiles(wide_end, r + 1), *after(wide_end), masked=True,
+                         last=lambda: open_row(row_at(coming), slot_at(i + 1)))
+
+        @pl.when(closes)
+        def _():
+            round_row(before, old_slot)
+            close_row(before, jnp.where(i > 1, before + 1, -1))
 
         @pl.when(i == late_end)
         def _():
@@ -502,18 +514,19 @@
         @pl.loop(0, late // 2)
         def _(pair):
             j = first_late + 2 * pair
-            slot = 2 * pair + 2
+            slot = 2 * pair + EARLY_SLOTS
             first = pair == 0
             middle = pair == late // 4
             last_tile = c + (HALF - 1) * n_cols
             products([(j + u, slot + u, c + w * n_cols) for u in range(2) for w in range(HALF)],
-                     jnp.where(first, jnp.where(i == 0, 0, late + 1), slot - 1),
+                     jnp.where(first, jnp.where(i == 0, slot_at(n_segs - 1), late_slot), slot - 1),
                      jnp.where(first, jnp.where(i == 0, 1, column(me, i + n_cols - 1) + (HALF - 1) * n_cols),
                                last_tile))
 
             @pl.when(first & (i == 0))
             def _():
-                close_row(0, 0, 1)
+                round_row(0, slot_at(n_segs - 1))
+                close_row(0, 1)
 
             @pl.when(first & (i > 0))
             def _():
@@ -538,13 +551,16 @@
             def _():
                 @pl.when(jnp.logical_not(first))
                 def _():
-                    close_row(j - 1, slot - 1, j - 2)
-
-                close_row(j, slot, jnp.where(first, 0, j - 1))
-
-    products([None], late + 1, column(me, n_cols - 1) + (HALF - 1) * n_cols)
+                    round_row(j - 1, slot - 1)
+                    close_row(j - 1, j - 2)
+
+                round_row(j, slot)
+                close_row(j, jnp.where(first, 0, j - 1))
+
+    products([None], late_slot, column(me, n_cols - 1) + (HALF - 1) * n_cols)
     close_tiles(column(me, n_cols - 1), HALF, n_cols, n_cols - 1)
-    close_row(n_segs - 1, late + 1, n_segs - 2)
+    round_row(n_segs - 1, late_slot)
+    close_row(n_segs - 1, n_segs - 2)
     ship_column(me, n_cols - 1, True)
     forward_row(n_segs - 1)
     forward_column(n_cols - 1)
@@ -612,7 +628,7 @@
         vmem = pltpu.VMEM
         key = vmem((keys, head_dim), BF16)
         key_t = vmem((2 * n_tiles, head_dim, 128), BF16)
-        row_t = vmem((late + 2, head_dim, group * TILE), BF16)
+        row_t = vmem((late + EARLY_SLOTS, head_dim, group * TILE), BF16)
         key_sum = vmem((2 * n_tiles, head_dim, 128), F32)
         stat = vmem((n_pairs, n_dev, 2, 256), F32)
         carried = vmem((group, TILE, TILE), BF16)
@@ -639,9 +655,9 @@
                 vmem((kv_heads, 2, group, q_rows, head_dim), BF16),
                 stat, vmem((n_segs, 2, group, TILE, head_dim), BF16), key, key, stat,
                 key_t, key_t, row_t, row_t,
-                vmem((late + 2, group, head_dim, TILE), F32),
+                vmem((late + EARLY_SLOTS, group, head_dim, TILE), F32),
                 key_sum, key_sum,
-                vmem((late + 2, group, TILE, head_dim), BF16), vmem((2, head_dim, TILE), BF16),
+                vmem((late + EARLY_SLOTS, group, TILE, head_dim), BF16), vmem((2, head_dim, TILE), BF16),
                 carried, carried, vmem((3, group, TILE, TILE), BF16),
                 dma((2, 3)), dma((2, 2)), dma, dma((2,)), dma((2,)), dma((n_pairs,)), dma, dma((2,)),
                 dma((2,)), dma((2,)), dma((2,)), dma((2,)), dma((2,)), dma, dma, dma, dma, dma((n_segs,)),

time: 371 us -> 365 us (0.984)
  Pallas kernels: 368 us -> 364 us
    pallas_call x1, Pallas kernels: 362 us -> 358 us  [local_grads(): pl.pallas_call(functools.partial(attn_kernel, dims), out_shape=(q_out, kv...]
where the time goes in v7:
time: 365 us
  Pallas kernels  364 us (100%)
    pallas_call x1, Pallas kernels, local_grads(): pl.pallas_call(functools.partial(attn_kernel, dims), out_shape=(q_out, kv...  358 us

profile of v7, /device:TPU:1, one launch (start us, length us, event | category | flops | bytes accessed | tf_op | source)
XLA Modules:
  0.0 364.7 jit_solution(16953561471960167297)
XLA Ops:
  0.6 358.1 %attn_grads.1 = (bf16[32,8,3,32,128]{4,3,2,1,0:T(8,128)(2,1)S(1)}, f32[33,8,32,128]{3,2,1,0:T(8,128)S(1)}, f32[33,8,32,128]{3,2,1,0:T(8,128)S(1)}, bf16[2,16,8,2...) custom-call(bf16[1024,24,128]{2,1,0:T(8,128)(2,1)} %bitcast.5, ...), custom_call_target="tpu_custom_call" | custom-call | flops 140928614400 | bytes 67108864 | tf_op jit(solution)/shard_map/attn_grads/pallas_call | solution.py:642
  358.7 5.8 %ungroup.1 = (bf16[1024,24,128]{2,1,0:T(8,128)(2,1)}, f32[1056,8,128]{2,1,0:T(8,128)}, f32[1056,8,128]{2,1,0:T(8,128)}) custom-call(bf16[32,8,3,32,128]{4,3,2,1,0:T(8,128)(2,1)S(1)} %get-tuple-element.9.dq_i, f32[33,8,32,128]{3,2,1,0:T(8,128)S(1)} %get-tuple-element.10.dk_i, f32[33,8,32,128]{3,2,1,0:T(8,128)S(1)} %get-tuple-element.11.dv_i), custom_call_target="tpu_custom_call" | custom-call | tf_op jit(solution)/shard_map/ungroup/pallas_call | solution.py:678

commit v8 on v7

--- a/solution.py
+++ b/solution.py
@@ -167,12 +167,13 @@
                     stg[buf, :, u // 2, a, :, half] = block
                 else:
                     o_s[:, u // 2, :, half] = block
-        segs = pl.ds(2 * r, 2)
         for s in range(2):
             qd_b[2 * r + s, :, :, rows_of(me)] = stg[buf, me, s]
         pltpu.make_async_copy(stg.at[buf], box.at[core, k], box_own.at[buf]).start()
         remote(stg.at[buf], box.at[core, k], box_send.at[buf], box_recv.at[k], mate)
-        remote(stg.at[buf, mate], qd_b.at[segs, :, :, rows_of(me)], pair_d2d.at[buf], row_recv.at[r], mate)
+        for u in range(2):
+            j = row_at(2 * k + u)
+            remote(stg.at[buf, mate, lax.rem(j, 2)], qd_b.at[j, :, :, rows_of(me)], pair_d2d.at[buf], row_recv.at[j], mate)
 
         ones = jnp.ones((8, head_dim), BF16)
         rows = group * q_rows
@@ -195,17 +196,18 @@
 
     def ship_pair(k):
         buf = lax.rem(k, 2)
-        r = pair_at(k)
-        segs = pl.ds(2 * r, 2)
         arrived(stg.at[buf], box_own.at[buf])
         arrived(stg.at[buf], box_send.at[buf])
         arrived(stg.at[buf, 0], pair_d2d.at[buf])
         arrived(box.at[0, k], box_recv.at[k])
 
         def send_all(to):
-            for src in range(2):
-                for p in to:
-                    remote(box.at[src, k, p], qd_b.at[segs, :, :, rows_of(me - core + src)], pair_send, row_recv.at[r], p)
+            for u in range(2):
+                j = row_at(2 * k + u)
+                for src in range(2):
+                    for p in to:
+                        remote(box.at[src, k, p, lax.rem(j, 2)], qd_b.at[j, :, :, rows_of(me - core + src)],
+                               pair_send, row_recv.at[j], p)
 
         sent_by_me(send_all)
 
@@ -325,11 +327,16 @@
         if last is not None:
             last()
 
-    def await_pair(i):
+    def await_row(i):
+        j = row_at(jnp.minimum(i, n_segs - 1))
+
+        @pl.when(i < n_segs)
+        def _():
+            arrived(qd_b.at[j, :, :, pl.ds(0, rest * q_rows)], row_recv.at[j])
+
         @pl.when((lax.rem(i, 2) == 0) & (i < n_segs))
         def _():
-            pair = pair_at(lax.div(i, 2))
-            arrived(qd_b.at[pl.ds(2 * pair, 2), :, :, pl.ds(0, rest * q_rows)], row_recv.at[pair])
+            pair = lax.div(j, 2)
             arrived(st_b.at[pair, pl.ds(0, rest)], st_recv.at[pair])
 
     def open_row(j, slot):
@@ -356,7 +363,7 @@
 
     def round_row(j, slot):
         for h in range(group):
-            qd_b[j, 0, h] = (dq_a[slot, h].T * scale).astype(BF16)
+            qd_b[j, 0, h] = (dq_a[slot, h] * scale).astype(BF16).T
 
     def close_row(j, before):
         remote(qd_b.at[j, 0], mir_q.at[j], dq_mir, dq_mir_recv.at[j], mate)
@@ -448,7 +455,7 @@
         return jnp.where((i >= middle_row) & (i < late_end), i - middle_row + EARLY_SLOTS,
                          lax.rem(early_index + EARLY_SLOTS, EARLY_SLOTS))
 
-    await_pair(0)
+    await_row(0)
     open_row(first_late - 1, 0)
 
     @pl.loop(0, n_segs)
@@ -472,7 +479,7 @@
             t = lo + c * WIDE
             products(tiles(t, WIDE), *after(t))
 
-        await_pair(i + 1)
+        await_row(i + 1)
         coming = jnp.minimum(i + 1, n_segs - 1)
         wide_end = lo + lax.div(n, WIDE) * WIDE
         for r in range(WIDE):
@@ -661,7 +668,7 @@
                 carried, carried, vmem((3, group, TILE, TILE), BF16),
                 dma((2, 3)), dma((2, 2)), dma, dma((2,)), dma((2,)), dma((n_pairs,)), dma, dma((2,)),
                 dma((2,)), dma((2,)), dma((2,)), dma((2,)), dma((2,)), dma, dma, dma, dma, dma((n_segs,)),
-                dma((2,)), dma((2,)), dma((2,)), dma((2, n_cols + 1)), dma((n_pairs,)), dma((2,)), dma((n_pairs,)),
+                dma((2,)), dma((2,)), dma((2,)), dma((2, n_cols + 1)), dma((n_segs,)), dma((2,)), dma((n_pairs,)),
                 dma((3,))],
             compiler_params=pltpu.CompilerParams(
                 collective_id=0, has_side_effects=True, vmem_limit_bytes=MAIN_VMEM),

time: 365 us -> 364 us (level)
  no operation moved by 1% of the time
where the time goes in v8:
time: 364 us; the launch traced here: 363 us
  Pallas kernels  363 us (100%)
    pallas_call x1, Pallas kernels, local_grads(): pl.pallas_call(functools.partial(attn_kernel, dims), out_shape=(q_out, kv...  357 us

profile of v8, /device:TPU:1, one launch (start us, length us, event | category | flops | bytes accessed | tf_op | source)
XLA Modules:
  0.0 363.4 jit_solution(2201583634479261903)
XLA Ops:
  0.6 356.8 %attn_grads.1 = (bf16[32,8,3,32,128]{4,3,2,1,0:T(8,128)(2,1)S(1)}, f32[33,8,32,128]{3,2,1,0:T(8,128)S(1)}, f32[33,8,32,128]{3,2,1,0:T(8,128)S(1)}, bf16[2,16,8,2...) custom-call(bf16[1024,24,128]{2,1,0:T(8,128)(2,1)} %bitcast.5, ...), custom_call_target="tpu_custom_call" | custom-call | flops 140928614400 | bytes 67108864 | tf_op jit(solution)/shard_map/attn_grads/pallas_call | solution.py:649
  357.5 5.8 %ungroup.1 = (bf16[1024,24,128]{2,1,0:T(8,128)(2,1)}, f32[1056,8,128]{2,1,0:T(8,128)}, f32[1056,8,128]{2,1,0:T(8,128)}) custom-call(bf16[32,8,3,32,128]{4,3,2,1,0:T(8,128)(2,1)S(1)} %get-tuple-element.9.dq_i, f32[33,8,32,128]{3,2,1,0:T(8,128)S(1)} %get-tuple-element.10.dk_i, f32[33,8,32,128]{3,2,1,0:T(8,128)S(1)} %get-tuple-element.11.dv_i), custom_call_target="tpu_custom_call" | custom-call | tf_op jit(solution)/shard_map/ungroup/pallas_call | solution.py:685

commit v9 on v8

--- a/solution.py
+++ b/solution.py
@@ -57,6 +57,19 @@
     along = chip_cores(False, True) + chip_cores(True, False)
     across = chip_cores(True, True)
 
+    along_chips, across_chips = [along[0], along[2]], [across[0]]
+
+    def each_chip(for_mate, act):
+        @pl.when(core == (1 if for_mate else 0))
+        def _():
+            for p in along_chips:
+                act(p)
+
+        @pl.when(core == (0 if for_mate else 1))
+        def _():
+            for p in across_chips:
+                act(p)
+
     def sent_by_me(send_all):
         @pl.when(core == 0)
         def _():
@@ -79,12 +92,12 @@
     def arrived(ref, sem):
         pltpu.make_async_copy(ref, ref, sem).wait()
 
-    def wait_sent(whole, half, sem):
-        @pl.when(core == 0)
+    def wait_sent(whole, half, sem, whole_on=0):
+        @pl.when(core == whole_on)
         def _():
             arrived(whole, sem)
 
-        @pl.when(core == 1)
+        @pl.when(core == 1 - whole_on)
         def _():
             arrived(half, sem)
 
@@ -142,11 +155,12 @@
         dst = pl.ds(pl.multiple_of(me * k_rows + lo, 32), rows)
         for a, land in enumerate((k_b, v_b)):
             remote(kv_s[a].at[mate, src], land.at[dst], kv_d2d.at[a], kv_recv.at[a], mate)
-            remote(kv_s[a].at[:, src], mir_kv.at[a, :, src], kv_mir.at[a], kv_mir_recv.at[a], mate)
+            each_chip(True, lambda p: remote(kv_s[a].at[pl.ds(p, 2), src], mir_kv.at[a, pl.ds(p, 2), src],
+                                             kv_mir.at[a], kv_mir_recv.at[a], mate))
 
     def forward_keys():
         for a in range(2):
-            arrived(mir_kv.at[a], kv_mir_recv.at[a])
+            wait_sent(mir_kv.at[a, pl.ds(0, n_dev // 2)], mir_kv.at[a, pl.ds(0, n_dev // 4)], kv_mir_recv.at[a])
         send_keys([mir_kv.at[a] for a in range(2)], mate, 0, k_rows, kv_fwd)
 
     def stage_pair(k):
@@ -169,8 +183,10 @@
                     o_s[:, u // 2, :, half] = block
         for s in range(2):
             qd_b[2 * r + s, :, :, rows_of(me)] = stg[buf, me, s]
-        pltpu.make_async_copy(stg.at[buf], box.at[core, k], box_own.at[buf]).start()
-        remote(stg.at[buf], box.at[core, k], box_send.at[buf], box_recv.at[k], mate)
+        each_chip(True, lambda p: remote(stg.at[buf, pl.ds(p, 2)], box.at[core, k, pl.ds(p, 2)],
+                                         box_send.at[buf], box_recv.at[k], mate))
+        each_chip(False, lambda p: pltpu.make_async_copy(stg.at[buf, pl.ds(p, 2)], box.at[core, k, pl.ds(p, 2)],
+                                                         box_own.at[buf]).start())
         for u in range(2):
             j = row_at(2 * k + u)
             remote(stg.at[buf, mate, lax.rem(j, 2)], qd_b.at[j, :, :, rows_of(me)], pair_d2d.at[buf], row_recv.at[j], mate)
@@ -196,10 +212,11 @@
 
     def ship_pair(k):
         buf = lax.rem(k, 2)
-        arrived(stg.at[buf], box_own.at[buf])
-        arrived(stg.at[buf], box_send.at[buf])
+        four, two = pl.ds(0, n_dev // 2), pl.ds(0, n_dev // 4)
+        wait_sent(stg.at[buf, four], stg.at[buf, two], box_own.at[buf])
+        wait_sent(stg.at[buf, four], stg.at[buf, two], box_send.at[buf], 1)
         arrived(stg.at[buf, 0], pair_d2d.at[buf])
-        arrived(box.at[0, k], box_recv.at[k])
+        wait_sent(box.at[0, k, four], box.at[0, k, two], box_recv.at[k])
 
         def send_all(to):
             for u in range(2):
@@ -265,7 +282,7 @@
     for a in range(2):
         wait_sent(kv_s[a].at[half], kv_s[a].at[quarter], kv_send.at[a])
         arrived(kv_s[a].at[one], kv_d2d.at[a])
-        arrived(kv_s[a], kv_mir.at[a])
+        wait_sent(kv_s[a].at[half], kv_s[a].at[quarter], kv_mir.at[a], 1)
 
     @pl.loop(0, n_tiles)
     def _(t):
@@ -353,7 +370,7 @@
                 aug[slot, h, b * q_rows:(b + 1) * q_rows, 0:8] = parts[h * q_rows:(h + 1) * q_rows]
 
     def forward_row(j):
-        arrived(mir_q.at[j], dq_mir_recv.at[j])
+        wait_sent(mir_q.at[j, :, pl.ds(0, 4 * q_rows)], mir_q.at[j, :, pl.ds(0, 2 * q_rows)], dq_mir_recv.at[j])
 
         def send_all(to):
             for p in to:
@@ -366,7 +383,11 @@
             qd_b[j, 0, h] = (dq_a[slot, h] * scale).astype(BF16).T
 
     def close_row(j, before):
-        remote(qd_b.at[j, 0], mir_q.at[j], dq_mir, dq_mir_recv.at[j], mate)
+        def hand_over(p):
+            rows = pl.ds(pl.multiple_of(p * q_rows, 2 * q_rows), 2 * q_rows)
+            remote(qd_b.at[j, 0, :, rows], mir_q.at[j, :, rows], dq_mir, dq_mir_recv.at[j], mate)
+
+        each_chip(True, hand_over)
         remote(qd_b.at[j, 0, :, rows_of(mate)], dq_o.at[j, me], dq_d2d, out_recv.at[0], mate)
         dq_o[j, me] = qd_b[j, 0, :, rows_of(me)]
 
@@ -578,7 +599,7 @@
     arrived(st_s.at[:, pl.ds(0, rest)], st_send)
     wait_sent(dq_o, dq_o.at[:, half], dq_send)
     arrived(dq_o.at[:, one], dq_d2d)
-    arrived(mir_q, dq_mir)
+    wait_sent(mir_q.at[:, :, pl.ds(0, 4 * q_rows)], mir_q.at[:, :, pl.ds(0, 2 * q_rows)], dq_mir, 1)
     for a, (out, ref) in enumerate(((dk_o, dk_a), (dv_o, dv_a))):
         wait_sent(out, out.at[:, half], dkv_send.at[a])
         arrived(out.at[:, one], dkv_d2d.at[a])

time: 364 us -> 364 us (level)
  no operation moved by 1% of the time
where the time goes in v9:
time: 364 us; the launch traced here: 363 us
  Pallas kernels  363 us (100%)
    pallas_call x1, Pallas kernels, local_grads(): pl.pallas_call(functools.partial(attn_kernel, dims), out_shape=(q_out, kv...  357 us

profile of v9, /device:TPU:1, one launch (start us, length us, event | category | flops | bytes accessed | tf_op | source)
XLA Modules:
  0.0 363.4 jit_solution(8124890235572084811)
XLA Ops:
  0.6 356.8 %attn_grads.1 = (bf16[32,8,3,32,128]{4,3,2,1,0:T(8,128)(2,1)S(1)}, f32[33,8,32,128]{3,2,1,0:T(8,128)S(1)}, f32[33,8,32,128]{3,2,1,0:T(8,128)S(1)}, bf16[2,16,8,2...) custom-call(bf16[1024,24,128]{2,1,0:T(8,128)(2,1)} %bitcast.5, ...), custom_call_target="tpu_custom_call" | custom-call | flops 140928614400 | bytes 67108864 | tf_op jit(solution)/shard_map/attn_grads/pallas_call | solution.py:670
  357.5 5.8 %ungroup.1 = (bf16[1024,24,128]{2,1,0:T(8,128)(2,1)}, f32[1056,8,128]{2,1,0:T(8,128)}, f32[1056,8,128]{2,1,0:T(8,128)}) custom-call(bf16[32,8,3,32,128]{4,3,2,1,0:T(8,128)(2,1)S(1)} %get-tuple-element.9.dq_i, f32[33,8,32,128]{3,2,1,0:T(8,128)S(1)} %get-tuple-element.10.dk_i, f32[33,8,32,128]{3,2,1,0:T(8,128)S(1)} %get-tuple-element.11.dv_i), custom_call_target="tpu_custom_call" | custom-call | tf_op jit(solution)/shard_map/ungroup/pallas_call | solution.py:706

commit v10 on v9

--- a/solution.py
+++ b/solution.py
@@ -49,6 +49,8 @@
 
     kv_s = [ref.reshape(n_dev, k_rows, head_dim) for ref in (k_t, v_t)]
 
+    role = 1 - core
+
     def chip_cores(flip_outer, flip_inner):
         y = 1 - outer_at if flip_outer else outer_at
         x = (inner - 2) - (inner_at - core) if flip_inner else inner_at - core
@@ -60,22 +62,22 @@
     along_chips, across_chips = [along[0], along[2]], [across[0]]
 
     def each_chip(for_mate, act):
-        @pl.when(core == (1 if for_mate else 0))
+        @pl.when(role == (1 if for_mate else 0))
         def _():
             for p in along_chips:
                 act(p)
 
-        @pl.when(core == (0 if for_mate else 1))
+        @pl.when(role == (0 if for_mate else 1))
         def _():
             for p in across_chips:
                 act(p)
 
     def sent_by_me(send_all):
-        @pl.when(core == 0)
+        @pl.when(role == 0)
         def _():
             send_all(along)
 
-        @pl.when(core == 1)
+        @pl.when(role == 1)
         def _():
             send_all(across)
 
@@ -93,11 +95,11 @@
         pltpu.make_async_copy(ref, ref, sem).wait()
 
     def wait_sent(whole, half, sem, whole_on=0):
-        @pl.when(core == whole_on)
+        @pl.when(role == whole_on)
         def _():
             arrived(whole, sem)
 
-        @pl.when(core == 1 - whole_on)
+        @pl.when(role == 1 - whole_on)
         def _():
             arrived(half, sem)
 
@@ -235,11 +237,11 @@
     for p in along + across + [mate]:
         pl.semaphore_signal(barrier, inc=1, device_id=device(p), device_id_type=MESH)
     chunks = k_rows // CHUNK
-    stage_keys(0, 2)
+    stage_keys(0, 1)
     pl.semaphore_wait(barrier, rest)
-    ship_keys(0, 2)
-    stage_keys(2, chunks - 2)
-    ship_keys(2, chunks - 2)
+    ship_keys(0, 1)
+    stage_keys(1, chunks - 1)
+    ship_keys(1, chunks - 1)
     arrived(ls_v, ls_sem)
 
     @pl.loop(0, n_pairs)
@@ -411,7 +413,7 @@
             src, dst = pl.ds(p, n), pl.ds(p - owner * pieces, n)
             on_chip = lax.div(owner, 2) == lax.div(me, 2)
             both = (lax.div(owner, inner) != outer_at) & (lax.div(lax.rem(owner, inner), 2) != lax.div(inner_at, 2))
-            mine_to_send = jnp.where(both, 1, 0) == core
+            mine_to_send = jnp.where(both, 1, 0) == role
             for n_out, out in enumerate((dk_o, dv_o)):
                 ref = (flat_sums if mine else flat_mirs)[n_out]
                 if mine:

time: 364 us -> 366 us (level)
  no operation moved by 1% of the time
where the time goes in v10:
time: 366 us
  Pallas kernels  365 us (100%)
    pallas_call x1, Pallas kernels, local_grads(): pl.pallas_call(functools.partial(attn_kernel, dims), out_shape=(q_out, kv...  359 us

profile of v10, /device:TPU:1, one launch (start us, length us, event | category | flops | bytes accessed | tf_op | source)
XLA Modules:
  0.0 365.6 jit_solution(9460201410785262059)
XLA Ops:
  0.6 359.0 %attn_grads.1 = (bf16[32,8,3,32,128]{4,3,2,1,0:T(8,128)(2,1)S(1)}, f32[33,8,32,128]{3,2,1,0:T(8,128)S(1)}, f32[33,8,32,128]{3,2,1,0:T(8,128)S(1)}, bf16[2,16,8,2...) custom-call(bf16[1024,24,128]{2,1,0:T(8,128)(2,1)} %bitcast.5, ...), custom_call_target="tpu_custom_call" | custom-call | flops 140928614400 | bytes 67108864 | tf_op jit(solution)/shard_map/attn_grads/pallas_call | solution.py:672
  359.7 5.8 %ungroup.1 = (bf16[1024,24,128]{2,1,0:T(8,128)(2,1)}, f32[1056,8,128]{2,1,0:T(8,128)}, f32[1056,8,128]{2,1,0:T(8,128)}) custom-call(bf16[32,8,3,32,128]{4,3,2,1,0:T(8,128)(2,1)S(1)} %get-tuple-element.9.dq_i, f32[33,8,32,128]{3,2,1,0:T(8,128)S(1)} %get-tuple-element.10.dk_i, f32[33,8,32,128]{3,2,1,0:T(8,128)S(1)} %get-tuple-element.11.dv_i), custom_call_target="tpu_custom_call" | custom-call | tf_op jit(solution)/shard_map/ungroup/pallas_call | solution.py:708
